TPU v7x, 32 devices: a whole 2x2x4 slice. The times are simulated.
32 devices in a mesh: dp: 8 (over y, x, core), seq: 4 (over z).
Axes of the slice: x: 2, y: 2, z: 4, core: 2. Of those that a mesh axis runs over, the one named last changes fastest.
Arguments:
- images: bfloat16 [16, 1152, 1024], P('dp', 'seq'), may hold values from -6 to 6
- qkv_weight: bfloat16 [1024, 3072], P('dp'), may hold values from -4 to 4, as said below
- qv_bias: bfloat16 [2048], P('dp'), may hold values from -3 to 3
- proj_weight: bfloat16 [1024, 1024], P('dp'), may hold values from -3.5 to 3.5
- proj_bias: bfloat16 [1024], P('dp'), may hold values from -3 to 3
- ln1_gain: bfloat16 [1024], P('dp'), may hold values from 0.25 to 1.75
- ln1_bias: bfloat16 [1024], P('dp'), may hold values from -3 to 3
- ln2_gain: bfloat16 [1024], P('dp'), may hold values from 0.25 to 1.75
- ln2_bias: bfloat16 [1024], P('dp'), may hold values from -3 to 3
- fc1_weight: bfloat16 [1024, 4096], P('dp'), may hold values from -0.1875 to 0.1875
- fc1_bias: bfloat16 [4096], P('dp'), may hold values from -3 to 3
- fc2_weight: bfloat16 [4096, 1024], P('dp'), may hold values from -0.09375 to 0.09375
- fc2_bias: bfloat16 [1024], P('dp'), may hold values from -3 to 3
- cotangent: bfloat16 [16, 1152, 1024], P('dp', 'seq'), may hold values from -6 to 6
Outputs:
- output: float32 [16, 1152, 1024], P('dp', 'seq')
- image_grad: float32 [16, 1152, 1024], P('dp', 'seq')
- qkv_weight_grad: float32 [1024, 3072], P('dp')
- qv_bias_grad: float32 [2048], P('dp')
- proj_weight_grad: float32 [1024, 1024], P('dp')
- proj_bias_grad: float32 [1024], P('dp')
- ln1_gain_grad: float32 [1024], P('dp')
- ln1_bias_grad: float32 [1024], P('dp')
- ln2_gain_grad: float32 [1024], P('dp')
- ln2_bias_grad: float32 [1024], P('dp')
- fc1_weight_grad: float32 [1024, 4096], P('dp')
- fc1_bias_grad: float32 [4096], P('dp')
- fc2_weight_grad: float32 [4096, 1024], P('dp')
- fc2_bias_grad: float32 [1024], P('dp')
Inputs may be any that keep to these rules, and one draw needn't show every extreme that they name: `qkv_weight`: most entries are of order 1024^-1/2; others may be larger, within the stated range.
All inputs are finite; a program needn't handle non-finite values.
Results may differ from a plain program's by a relative error of at most 0.02.
The roundings to bfloat16 on the way count: a program that leaves them out, or rounds other values in their place, can miss the bound.
Values may be sent and summed in bfloat16 or wider, within the bound.
A program may use at most 256 MiB of HBM per device.

v0:
```python
import jax
import jax.numpy as jnp
from jax import lax
from jax.sharding import PartitionSpec as P

HEAD_DIM = 64


epsilon = 1e-06


def norm_forward(matrix, gain, shift):
    mean_val = jnp.mean(matrix, axis=-1, keepdims=True)
    centred = matrix - mean_val
    inv_std = lax.rsqrt(jnp.mean(centred * centred, axis=-1, keepdims=True) + epsilon)
    normed = centred * inv_std
    return (normed, inv_std, normed * gain + shift)


def norm_backward(grad_in, normed, inv_std, gain):
    scaled = grad_in * gain
    return inv_std * (
        scaled
        - jnp.mean(scaled, axis=-1, keepdims=True)
        - normed * jnp.mean(scaled * normed, axis=-1, keepdims=True)
    )


def gelu_cdf(pre_act):
    return 0.5 * (1.0 + lax.erf(pre_act * 0.7071067811865476))


def gelu_slope(pre_act):
    return gelu_cdf(pre_act) + pre_act * jnp.exp(-0.5 * pre_act * pre_act) * 0.3989422804014327


def block_count(length):
    block_total = max(1, length // 512)
    while length % block_total:
        block_total -= 1
    return block_total


def split_parts(heads_in, which):
    item_count, length, head_cols = (heads_in.shape[0], heads_in.shape[1], heads_in.shape[4])
    return heads_in[:, :, which, 0, :].reshape(item_count, length, head_cols // HEAD_DIM, HEAD_DIM)


def to_blocks(array, block_total):
    item_count, length, groups = (array.shape[0], array.shape[1], array.shape[2])
    return jnp.moveaxis(
        array.reshape(item_count, block_total, length // block_total, groups, HEAD_DIM), 1, 0
    )


def attend(heads_in):
    item_count, length, head_cols = (heads_in.shape[0], heads_in.shape[1], heads_in.shape[4])
    groups = head_cols // HEAD_DIM
    score_scale = HEAD_DIM ** (-0.5)
    key_heads = split_parts(heads_in, 1)
    value_heads = split_parts(heads_in, 2)
    block_total = block_count(length)

    def one_block(query_block):
        scores = (
            jnp.einsum(
                "nqgd,nkgd->ngqk", query_block, key_heads, preferred_element_type=jnp.float32
            )
            * score_scale
        )
        row_peak = jnp.max(scores, axis=-1, keepdims=True)
        lifted = jnp.exp(scores - row_peak)
        row_total = jnp.sum(lifted, axis=-1, keepdims=True)
        probs_low = (lifted / row_total).astype(jnp.bfloat16)
        attended = jnp.einsum(
            "ngqk,nkgd->nqgd", probs_low, value_heads, preferred_element_type=jnp.float32
        ).astype(jnp.bfloat16)
        return (attended, (row_peak + jnp.log(row_total))[..., 0])

    attended, log_total = lax.map(one_block, to_blocks(split_parts(heads_in, 0), block_total))
    attended = jnp.moveaxis(attended, 0, 1).reshape(item_count, length, 1, head_cols)
    log_total = jnp.moveaxis(log_total, 0, 2).reshape(item_count, groups, length)
    return (heads_in, attended, log_total)


def attend_back(heads_in, attended, log_total, grad_heads):
    item_count, length, head_cols = (heads_in.shape[0], heads_in.shape[1], heads_in.shape[4])
    groups = head_cols // HEAD_DIM
    score_scale = HEAD_DIM ** (-0.5)
    key_heads = split_parts(heads_in, 1)
    value_heads = split_parts(heads_in, 2)
    block_total = block_count(length)
    block_rows = length // block_total
    lse_blocks = jnp.moveaxis(log_total.reshape(item_count, groups, block_total, block_rows), 2, 0)
    out_heads = attended.reshape(item_count, length, groups, HEAD_DIM)
    grad_mixed = grad_heads.reshape(item_count, length, groups, HEAD_DIM)

    def one_block(running, pieces):
        key_grad, value_grad = running
        query_block, out_block, grad_block, lse_block = pieces
        scores = (
            jnp.einsum(
                "nqgd,nkgd->ngqk", query_block, key_heads, preferred_element_type=jnp.float32
            )
            * score_scale
        )
        probs = jnp.exp(scores - lse_block[..., None])
        value_grad = value_grad + jnp.einsum(
            "ngqk,nqgd->nkgd",
            probs.astype(jnp.bfloat16),
            grad_block,
            preferred_element_type=jnp.float32,
        )
        prob_grad = jnp.einsum(
            "nqgd,nkgd->ngqk", grad_block, value_heads, preferred_element_type=jnp.float32
        )
        delta_rows = jnp.moveaxis(
            jnp.sum(grad_block.astype(jnp.float32) * out_block.astype(jnp.float32), axis=-1), 1, 2
        )
        score_grad = (probs * (prob_grad - delta_rows[..., None]) * score_scale).astype(
            jnp.bfloat16
        )
        query_grad = jnp.einsum(
            "ngqk,nkgd->nqgd", score_grad, key_heads, preferred_element_type=jnp.float32
        )
        key_grad = key_grad + jnp.einsum(
            "ngqk,nqgd->nkgd", score_grad, query_block, preferred_element_type=jnp.float32
        )
        return ((key_grad, value_grad), query_grad)

    zero_grads = jnp.zeros((item_count, length, groups, HEAD_DIM), jnp.float32)
    pieces = (
        to_blocks(split_parts(heads_in, 0), block_total),
        to_blocks(out_heads, block_total),
        to_blocks(grad_mixed, block_total),
        lse_blocks,
    )
    (key_grad, value_grad), query_grad = lax.scan(one_block, (zero_grads, zero_grads), pieces)
    query_grad = jnp.moveaxis(query_grad, 0, 1).reshape(item_count, length, head_cols)
    return (
        query_grad,
        key_grad.reshape(item_count, length, head_cols),
        value_grad.reshape(item_count, length, head_cols),
    )


def body(
    images,
    qkv_weight,
    qv_bias,
    proj_weight,
    proj_bias,
    ln1_gain,
    ln1_bias,
    ln2_gain,
    ln2_bias,
    fc1_weight,
    fc1_bias,
    fc2_weight,
    fc2_bias,
    cotangent,
):
    item_count, tokens, model_width = images.shape
    row_count = item_count * tokens
    seq_ways = lax.axis_size("seq")
    head_cols = model_width // seq_ways
    attn_full = (
        lax.all_gather(qkv_weight, "dp", axis=0, tiled=True),
        lax.all_gather(proj_weight, "dp", axis=0, tiled=True),
        lax.all_gather(ln1_gain, "dp", axis=0, tiled=True),
        lax.all_gather(ln1_bias, "dp", axis=0, tiled=True),
        lax.all_gather(qv_bias, "dp", axis=0, tiled=True),
        lax.all_gather(proj_bias, "dp", axis=0, tiled=True),
    )
    qkv_full, proj_full, gain_first_low, shift_first_low, qv_full, proj_bias_full = attn_full
    gain_first = gain_first_low.astype(jnp.float32)
    shift_first = shift_first_low.astype(jnp.float32)
    bias_row = jnp.concatenate(
        [
            qv_full[:model_width].astype(jnp.float32),
            jnp.zeros((model_width,), jnp.float32),
            qv_full[model_width:].astype(jnp.float32),
        ]
    )
    flat_rows = images.reshape(row_count, model_width).astype(jnp.float32)
    normed_first, inv_first, pre_first = norm_forward(flat_rows, gain_first, shift_first)
    hidden_first = pre_first.astype(jnp.bfloat16)
    projected = (
        jnp.dot(hidden_first, qkv_full, preferred_element_type=jnp.float32) + bias_row
    ).astype(jnp.bfloat16)
    projected = projected.reshape(item_count, tokens, 3, seq_ways, head_cols)
    heads_in, attended_heads, log_total = attend(
        lax.all_to_all(projected, "seq", split_axis=3, concat_axis=1, tiled=True)
    )
    attended_rows = lax.all_to_all(
        attended_heads, "seq", split_axis=1, concat_axis=2, tiled=True
    ).reshape(row_count, model_width)
    residual_first = (
        flat_rows
        + jnp.dot(attended_rows, proj_full, preferred_element_type=jnp.float32)
        + proj_bias_full.astype(jnp.float32)
    )
    mlp_full = (
        lax.all_gather(fc1_weight, "dp", axis=0, tiled=True),
        lax.all_gather(fc2_weight, "dp", axis=0, tiled=True),
        lax.all_gather(ln2_gain, "dp", axis=0, tiled=True),
        lax.all_gather(ln2_bias, "dp", axis=0, tiled=True),
        lax.all_gather(fc1_bias, "dp", axis=0, tiled=True),
        lax.all_gather(fc2_bias, "dp", axis=0, tiled=True),
    )
    fc_one, fc_two, gain_second_low, shift_second_low, bias_one, bias_two = mlp_full
    gain_second = gain_second_low.astype(jnp.float32)
    normed_second, inv_second, pre_second = norm_forward(
        residual_first, gain_second, shift_second_low.astype(jnp.float32)
    )
    hidden_second = pre_second.astype(jnp.bfloat16)
    pre_act = jnp.dot(hidden_second, fc_one, preferred_element_type=jnp.float32) + bias_one.astype(
        jnp.float32
    )
    acts = (pre_act * gelu_cdf(pre_act)).astype(jnp.bfloat16)
    output = (
        residual_first
        + jnp.dot(acts, fc_two, preferred_element_type=jnp.float32)
        + bias_two.astype(jnp.float32)
    )
    mlp_back = (
        lax.all_gather(fc1_weight, "dp", axis=0, tiled=True),
        lax.all_gather(fc2_weight, "dp", axis=0, tiled=True),
        lax.all_gather(ln2_gain, "dp", axis=0, tiled=True),
    )
    back_one, back_two, back_gain_second = mlp_back
    gain_second_back = back_gain_second.astype(jnp.float32)
    grad_low = cotangent.reshape(row_count, model_width)
    grad_out = grad_low.astype(jnp.float32)
    grad_fc_two = jnp.dot(acts.T, grad_low, preferred_element_type=jnp.float32)
    grad_bias_two = jnp.sum(grad_out, axis=0)
    pre_grad = jnp.dot(grad_low, back_two.T, preferred_element_type=jnp.float32) * gelu_slope(
        pre_act
    )
    pre_grad_low = pre_grad.astype(jnp.bfloat16)
    grad_fc_one = jnp.dot(hidden_second.T, pre_grad_low, preferred_element_type=jnp.float32)
    grad_bias_one = jnp.sum(pre_grad, axis=0)
    hidden_second_grad = jnp.dot(pre_grad_low, back_one.T, preferred_element_type=jnp.float32)
    grad_gain_second = jnp.sum(hidden_second_grad * normed_second, axis=0)
    grad_shift_second = jnp.sum(hidden_second_grad, axis=0)
    residual_grad = grad_out + norm_backward(
        hidden_second_grad, normed_second, inv_second, gain_second_back
    )
    residual_grad_low = residual_grad.astype(jnp.bfloat16)
    grad_proj = jnp.dot(attended_rows.T, residual_grad_low, preferred_element_type=jnp.float32)
    grad_proj_bias = jnp.sum(residual_grad, axis=0)
    attn_back = (
        lax.all_gather(qkv_weight, "dp", axis=0, tiled=True),
        lax.all_gather(proj_weight, "dp", axis=0, tiled=True),
        lax.all_gather(ln1_gain, "dp", axis=0, tiled=True),
    )
    back_qkv, back_proj, back_gain_first = attn_back
    attended_grad = jnp.dot(
        residual_grad_low, back_proj.T, preferred_element_type=jnp.float32
    ).astype(jnp.bfloat16)
    attended_grad = attended_grad.reshape(item_count, tokens, seq_ways, head_cols)
    grad_heads = lax.all_to_all(attended_grad, "seq", split_axis=2, concat_axis=1, tiled=True)
    query_grad, key_grad, value_grad = attend_back(heads_in, attended_heads, log_total, grad_heads)
    seq_index = lax.axis_index("seq")
    grad_qv = jnp.zeros((2 * model_width,), jnp.float32)
    grad_qv = lax.dynamic_update_slice(
        grad_qv, jnp.sum(query_grad, axis=(0, 1)), (seq_index * head_cols,)
    )
    grad_qv = lax.dynamic_update_slice(
        grad_qv, jnp.sum(value_grad, axis=(0, 1)), (model_width + seq_index * head_cols,)
    )
    stacked_grad = jnp.stack(
        [
            query_grad.astype(jnp.bfloat16),
            key_grad.astype(jnp.bfloat16),
            value_grad.astype(jnp.bfloat16),
        ],
        axis=2,
    )[:, :, :, None, :]
    qkv_grad = lax.all_to_all(stacked_grad, "seq", split_axis=1, concat_axis=3, tiled=True).reshape(
        row_count, 3 * model_width
    )
    grad_qkv = jnp.dot(hidden_first.T, qkv_grad, preferred_element_type=jnp.float32)
    hidden_first_grad = jnp.dot(qkv_grad, back_qkv.T, preferred_element_type=jnp.float32)
    grad_gain_first = jnp.sum(hidden_first_grad * normed_first, axis=0)
    grad_shift_first = jnp.sum(hidden_first_grad, axis=0)
    image_grad = residual_grad + norm_backward(
        hidden_first_grad, normed_first, inv_first, back_gain_first.astype(jnp.float32)
    )
    shares = (
        lax.psum_scatter(
            grad_qkv.astype(jnp.bfloat16), "dp", scatter_dimension=0, tiled=True
        ).astype(jnp.float32),
        lax.psum_scatter(
            grad_qv.astype(jnp.bfloat16), "dp", scatter_dimension=0, tiled=True
        ).astype(jnp.float32),
        lax.psum_scatter(
            grad_proj.astype(jnp.bfloat16), "dp", scatter_dimension=0, tiled=True
        ).astype(jnp.float32),
        lax.psum_scatter(
            grad_proj_bias.astype(jnp.bfloat16), "dp", scatter_dimension=0, tiled=True
        ).astype(jnp.float32),
        lax.psum_scatter(
            grad_gain_first.astype(jnp.bfloat16), "dp", scatter_dimension=0, tiled=True
        ).astype(jnp.float32),
        lax.psum_scatter(
            grad_shift_first.astype(jnp.bfloat16), "dp", scatter_dimension=0, tiled=True
        ).astype(jnp.float32),
        lax.psum_scatter(
            grad_gain_second.astype(jnp.bfloat16), "dp", scatter_dimension=0, tiled=True
        ).astype(jnp.float32),
        lax.psum_scatter(
            grad_shift_second.astype(jnp.bfloat16), "dp", scatter_dimension=0, tiled=True
        ).astype(jnp.float32),
        lax.psum_scatter(
            grad_fc_one.astype(jnp.bfloat16), "dp", scatter_dimension=0, tiled=True
        ).astype(jnp.float32),
        lax.psum_scatter(
            grad_bias_one.astype(jnp.bfloat16), "dp", scatter_dimension=0, tiled=True
        ).astype(jnp.float32),
        lax.psum_scatter(
            grad_fc_two.astype(jnp.bfloat16), "dp", scatter_dimension=0, tiled=True
        ).astype(jnp.float32),
        lax.psum_scatter(
            grad_bias_two.astype(jnp.bfloat16), "dp", scatter_dimension=0, tiled=True
        ).astype(jnp.float32),
    )
    shares = (
        lax.psum(shares[0].astype(jnp.bfloat16), "seq").astype(jnp.float32),
        lax.psum(shares[1].astype(jnp.bfloat16), "seq").astype(jnp.float32),
        lax.psum(shares[2].astype(jnp.bfloat16), "seq").astype(jnp.float32),
        lax.psum(shares[3].astype(jnp.bfloat16), "seq").astype(jnp.float32),
        lax.psum(shares[4].astype(jnp.bfloat16), "seq").astype(jnp.float32),
        lax.psum(shares[5].astype(jnp.bfloat16), "seq").astype(jnp.float32),
        lax.psum(shares[6].astype(jnp.bfloat16), "seq").astype(jnp.float32),
        lax.psum(shares[7].astype(jnp.bfloat16), "seq").astype(jnp.float32),
        lax.psum(shares[8].astype(jnp.bfloat16), "seq").astype(jnp.float32),
        lax.psum(shares[9].astype(jnp.bfloat16), "seq").astype(jnp.float32),
        lax.psum(shares[10].astype(jnp.bfloat16), "seq").astype(jnp.float32),
        lax.psum(shares[11].astype(jnp.bfloat16), "seq").astype(jnp.float32),
    )
    return (
        output.reshape(item_count, tokens, model_width),
        image_grad.reshape(item_count, tokens, model_width),
        shares[0],
        shares[1],
        shares[2],
        shares[3],
        shares[4],
        shares[5],
        shares[6],
        shares[7],
        shares[8],
        shares[9],
        shares[10],
        shares[11],
    )


def solution(mesh):
    in_specs = (
        P("dp", "seq", None),
        P("dp", None),
        P("dp"),
        P("dp", None),
        P("dp"),
        P("dp"),
        P("dp"),
        P("dp"),
        P("dp"),
        P("dp", None),
        P("dp"),
        P("dp", None),
        P("dp"),
        P("dp", "seq", None),
    )
    out_specs = (
        P("dp", "seq", None),
        P("dp", "seq", None),
        P("dp", None),
        P("dp"),
        P("dp", None),
        P("dp"),
        P("dp"),
        P("dp"),
        P("dp"),
        P("dp"),
        P("dp", None),
        P("dp"),
        P("dp", None),
        P("dp"),
    )
    return jax.shard_map(body, mesh=mesh, in_specs=in_specs, out_specs=out_specs, check_vma=False)
```

profile of v0, /device:TPU:0, one launch (start us, length us, event | category | flops | bytes accessed | tf_op | source)
XLA Modules:
  0.0 803.4 jit_solution(16673565859064357602)
XLA Ops:
  11.0 10.3 %all-gather = bf16[8,1,128]{2,1,0:T(2,128)(2,1)S(1)} all-gather(bf16[1,1,128]{2,1,0:T(2,128)(2,1)S(1)} %bitcast.225), channel_id=1, replica_groups=mesh['dp'=8,'seq'=4] {'dp'}, dimensions={0}, use_global_device_ids=true | all-gather | bytes 2304 | tf_op jit(solution)/shard_map/all_gather | solution.py:170
  21.3 9.0 %all-gather.1 = bf16[8,1,128]{2,1,0:T(2,128)(2,1)S(1)} all-gather(bf16[1,1,128]{2,1,0:T(2,128)(2,1)S(1)} %bitcast.226), channel_id=1, replica_groups=mesh['dp'=8,'seq'=4] {'dp'}, dimensions={0}, use_global_device_ids=true | all-gather | bytes 2304 | tf_op jit(solution)/shard_map/all_gather | solution.py:171
  30.3 8.0 all-gather.2
  39.3 18.8 %all-gather.13.cloned.1.call-done = bf16[1024,3072]{1,0:T(8,128)(2,1)} async-done(((bf16[128,3072]{1,0:T(8,128)(2,1)}), bf16[1024,3072]{1,0:T(8,128)(2,1)}) %all-gather.13.cloned.1.call-update) | async-done | bytes 6291472 | tf_op jit(solution)/shard_map/all_gather | solution.py:168
  58.1 8.0 add_convert_fusion
  66.1 6.3 reshape.211
  72.4 2.4 copy.58
  74.8 4.6 all-to-all-start
  80.0 78.9 %all-to-all-done = bf16[2,288,3,4,256]{4,1,2,0,3:T(8,128)(2,1)S(1)} async-done(((bf16[2,288,3,4,256]{4,1,2,0,3:T(8,128)(2,1)}), bf16[2,288,3,4,256]{4,1,2,0,3:T(8,128)(2,1)S(1)}, u32[]{:S(2)}, u32[]{:S(2)}) %all-to-all-start) | async-done | bytes 3538976 | tf_op jit(solution)/shard_map/all_to_all | solution.py:193
  165.6 55.7 %while.27 = (s32[]{:T(128)}, bf16[2,2,576,4,64]{2,4,3,1,0:T(8,128)(2,1)}, f32[2,2,4,576]{3,2,1,0:T(4,128)}, bf16[2,2,576,4,64]{2,4,3,1,0:T(8,128)(2,1)}, bf16[2,...) while((s32[]{:T(128)}, bf16[2,2,576,4,64]{2,4,3,1,0:T(8,128)(2,1)}, ...), condition=%wide.region_5.6_spmd, body=%wide.region_2.5_spmd.sunk | while | flops 1407020544 | bytes 152455312 | solution.py:80
  165.6 4.5 multiply_reduce_fusion.9
  170.2 8.4 %copy-done = f32[2,4,576,1152]{3,2,1,0:T(8,128)} copy-done((f32[2,4,576,1152]{3,2,1,0:T(8,128)}, f32[2,4,576,1152]{3,2,1,0:T(8,128)S(1)}, u32[]{:S(2)}) %copy-start) | copy-done | bytes 21233688 | tf_op jit(solution)/shard_map/while
  178.6 4.5 fusion.110
  183.1 10.5 %fusion.111 = bf16[2,2,576,4,64]{2,4,3,1,0:T(8,128)(2,1)} fusion(bf16[2,2,576,4,64]{2,4,3,1,0:T(8,128)(2,1)} %get-tuple-element.380, s32[]{:T(128)S(6)} %copy.85, bf16[2,1152,4,64]{1,3,2,0:T(8,128)(2,1)} %get-tuple-element.391, f32[2,4,576,1152]{3,2,1,0:T(8,128)} %copy-done, f32[2,4,576]{2,1,0:T(4,128)S(1)} %fusion.110, ...), kind=kOutput, calls=%fused_computation.7.clone.1 | convolution fusion | flops 701005824 | bytes 23105540 | tf_op jit(solution)/shard_map/while/body/eval_jaxpr/ngqk,nkgd->nqgd/dot_general | solution.py:75
  194.3 4.5 multiply_reduce_fusion.9
  198.8 7.1 copy-done
  205.9 4.5 fusion.110
  210.4 10.3 %fusion.111 = bf16[2,2,576,4,64]{2,4,3,1,0:T(8,128)(2,1)} fusion(bf16[2,2,576,4,64]{2,4,3,1,0:T(8,128)(2,1)} %get-tuple-element.380, s32[]{:T(128)S(6)} %copy.85, bf16[2,1152,4,64]{1,3,2,0:T(8,128)(2,1)} %get-tuple-element.391, f32[2,4,576,1152]{3,2,1,0:T(8,128)} %copy-done, f32[2,4,576]{2,1,0:T(4,128)S(1)} %fusion.110, ...), kind=kOutput, calls=%fused_computation.7.clone.1 | convolution fusion | flops 701005824 | bytes 23105540 | tf_op jit(solution)/shard_map/while/body/eval_jaxpr/ngqk,nkgd->nqgd/dot_general | solution.py:75
  221.4 3.4 copy.76
  224.8 2.5 reshape.249
  227.3 3.5 all-to-all-start.1
  230.9 8.7 %all-gather.3 = bf16[8,1,128]{2,1,0:T(2,128)(2,1)S(1)} all-gather(bf16[1,1,128]{2,1,0:T(2,128)(2,1)S(1)} %bitcast.227), channel_id=1, replica_groups=mesh['dp'=8,'seq'=4] {'dp'}, dimensions={0}, use_global_device_ids=true | all-gather | bytes 2304 | tf_op jit(solution)/shard_map/all_gather | solution.py:173
  239.7 7.9 all-gather.4
  247.5 8.7 %all-gather.5 = bf16[8,1,128]{2,1,0:T(2,128)(2,1)S(1)} all-gather(bf16[1,1,128]{2,1,0:T(2,128)(2,1)S(1)} %bitcast.229), channel_id=1, replica_groups=mesh['dp'=8,'seq'=4] {'dp'}, dimensions={0}, use_global_device_ids=true | all-gather | bytes 2304 | tf_op jit(solution)/shard_map/all_gather | solution.py:207
  256.9 8.1 %all-gather.6 = bf16[8,1,512]{2,1,0:T(2,128)(2,1)S(1)} all-gather(bf16[1,1,512]{2,1,0:T(2,128)(2,1)S(1)} %reshape.233), channel_id=1, replica_groups=mesh['dp'=8,'seq'=4] {'dp'}, dimensions={0}, use_global_device_ids=true | all-gather | bytes 9216 | tf_op jit(solution)/shard_map/all_gather | solution.py:208
  268.0 3.3 bitcast_add_fusion
  272.1 11.4 %multiply_convert_fusion.1 = (bf16[576,4096]{1,0:T(8,128)(2,1)}, f32[576,4096]{1,0:T(8,128)}) fusion(f32[4096]{0:T(1024)} %bitcast.218, bf16[1024,4096]{1,0:T(8,128)(2,1)} %all-gather.17.cloned.1.call-done, f32[1024]{0:T(1024)} %bitcast.222, f32[1024]{0:T(1024)S(1)} %bitcast.214, f32[576]{0:T(1024)S(1)} %add_rsqrt_fusion, ...), kind=kOutput, calls=%fused_computation.49 | convolution fusion | flops 4849532928 | bytes 24936960 | tf_op jit(solution)/shard_map/dot_general | solution.py:217
  283.6 12.8 %fusion.62 = (bf16[4096]{0:T(1024)(128)(2,1)}, bf16[576,4096]{1,0:T(8,128)(2,1)S(1)}) fusion(f32[576,4096]{1,0:T(8,128)} %get-tuple-element.261, f32[4096]{0:T(1024)} %bitcast.219, bf16[576,1024]{1,0:T(8,128)(2,1)S(1)} %bitcast.193, bf16[4096,1024]{1,0:T(8,128)(2,1)} %all-gather.19.cloned.1.call-done), kind=kOutput, calls=%fused_computation.108 | convolution fusion | flops 4860145664 | bytes 23748608 | tf_op jit(solution)/shard_map/dot_general | solution.py:237
  296.3 6.1 multiply_reduce_fusion.1
  305.5 3.2 convolution_convert_fusion.3
  308.7 12.1 %convolution_convert_fusion = bf16[1024,4096]{1,0:T(8,128)(2,1)} fusion(bf16[576,4096]{1,0:T(8,128)(2,1)} %copy-done.46, f32[1024]{0:T(1024)S(1)} %bitcast.223, f32[1024]{0:T(1024)S(1)} %bitcast.217, f32[576,1024]{1,0:T(8,128)S(1)} %bitcast_add_fusion, f32[576]{0:T(1024)S(1)} %add_rsqrt_fusion, f32[576]{0:T(1024)S(1)} %broadcast_multiply_fusion.4, ...), kind=kOutput, calls=%fused_computation.51 | convolution fusion | flops 4839571456 | bytes 15483392 | tf_op jit(solution)/shard_map/dot_general | solution.py:241
  322.5 3.0 convolution_convert_fusion.4
  327.7 5.0 all-to-all-start.2
  332.7 11.3 %convolution_convert_fusion.1 = bf16[4096,1024]{1,0:T(8,128)(2,1)} fusion(bf16[576,4096]{1,0:T(8,128)(2,1)} %get-tuple-element.260, bf16[576,1024]{1,0:T(8,128)(2,1)S(1)} %bitcast.194), kind=kOutput, calls=%fused_computation.52 | convolution fusion | flops 4836032512 | bytes 14286848 | tf_op jit(solution)/shard_map/dot_general | solution.py:235
  344.0 17.7 %all-to-all-done.2 = bf16[2,288,4,256]{3,1,0,2:T(8,128)(2,1)S(1)} async-done(((bf16[2,288,4,256]{3,1,0,2:T(8,128)(2,1)}), bf16[2,288,4,256]{3,1,0,2:T(8,128)(2,1)S(1)}, u32[]{:S(2)}, u32[]{:S(2)}) %all-to-all-start.2) | async-done | bytes 1179680 | tf_op jit(solution)/shard_map/all_to_all | solution.py:262
  366.2 113.2 %while.28 = (s32[]{:T(128)}, f32[2,1152,4,64]{1,3,2,0:T(8,128)}, f32[2,1152,4,64]{1,3,2,0:T(8,128)}, f32[2,2,576,4,64]{2,4,3,1,0:T(8,128)}, bf16[2,2,576,4,64]{2...) while((s32[]{:T(128)}, f32[2,1152,4,64]{1,3,2,0:T(8,128)}, ...), condition=%wide.region_12.13_spmd.clone, body=%wide.region_10.12_spmd.clone.sunk | while | flops 3448696320 | bytes 156217520 | solution.py:138
  368.1 12.3 %fusion.122 = f32[2,4,576,1152]{3,2,1,0:T(8,128)} fusion(bf16[2,1152,4,64]{1,3,2,0:T(8,128)(2,1)} %get-tuple-element.422, bf16[2,2,576,4,64]{2,4,3,1,0:T(8,128)(2,1)} %get-tuple-element.421, s32[]{:T(128)S(6)} %copy.95), kind=kOutput, calls=%fused_computation.31.clone.1 | convolution fusion | flops 679477248 | bytes 23068676 | tf_op jit(solution)/shard_map/while/body/eval_jaxpr/nqgd,nkgd->ngqk/dot_general | solution.py:102
  380.5 12.8 %fusion.125 = f32[2,1152,4,64]{1,3,2,0:T(8,128)} fusion(f32[2,4,576,1152]{3,2,1,0:T(8,128)} %fusion.122, f32[2,4,576]{2,1,0:T(4,128)S(1)} %dynamic-slice_bitcast_fusion.2, f32[2,1152,4,64]{1,3,2,0:T(8,128)} %get-tuple-element.407, pred[]{:T(512)S(6)} %compare.3, bf16[2,2,576,4,64]{2,4,3,1,0:T(8,128)(2,1)} %get-tuple-element.424, s32[]{:T(128)S(6)} %copy.95), kind=kOutput, calls=%fused_computation.21.clone.1 | convolution fusion | flops 696582144 | bytes 26626052 | tf_op jit(solution)/shard_map/while/body/eval_jaxpr/ngqk,nqgd->nkgd/dot_general | solution.py:108
  393.3 13.5 %multiply_convert_fusion.3 = bf16[2,4,576,1152]{3,2,1,0:T(8,128)(2,1)} fusion(f32[2,4,576,1152]{3,2,1,0:T(8,128)} %fusion.122, bf16[2,1152,4,64]{1,3,2,0:T(8,128)(2,1)} %get-tuple-element.425, f32[2,4,576]{2,1,0:T(4,128)S(1)} %bitcast.200, f32[2,4,576]{2,1,0:T(4,128)S(1)} %dynamic-slice_bitcast_fusion.2, ...), kind=kOutput, calls=%fused_computation.14.clone.1 | convolution fusion | flops 711327744 | bytes 33722372 | tf_op jit(solution)/shard_map/while/body/eval_jaxpr/nqgd,nkgd->ngqk/dot_general | solution.py:114
  406.8 8.4 %fusion.124 = f32[2,1152,4,64]{1,3,2,0:T(8,128)} fusion(bf16[2,4,576,1152]{3,2,1,0:T(8,128)(2,1)} %multiply_convert_fusion.3, f32[2,1152,4,64]{1,3,2,0:T(8,128)} %get-tuple-element.406, pred[]{:T(512)S(6)} %compare.3, bf16[2,2,576,4,64]{2,4,3,1,0:T(8,128)(2,1)} %get-tuple-element.421, s32[]{:T(128)S(6)} %copy.95), kind=kOutput, calls=%fused_computation.23.clone.1 | convolution fusion | flops 680656896 | bytes 15990789 | tf_op jit(solution)/shard_map/while/body/eval_jaxpr/ngqk,nqgd->nkgd/dot_general | solution.py:126
  415.2 5.6 fusion.126
  422.3 12.1 %fusion.122 = f32[2,4,576,1152]{3,2,1,0:T(8,128)} fusion(bf16[2,1152,4,64]{1,3,2,0:T(8,128)(2,1)} %get-tuple-element.422, bf16[2,2,576,4,64]{2,4,3,1,0:T(8,128)(2,1)} %get-tuple-element.421, s32[]{:T(128)S(6)} %copy.95), kind=kOutput, calls=%fused_computation.31.clone.1 | convolution fusion | flops 679477248 | bytes 23068676 | tf_op jit(solution)/shard_map/while/body/eval_jaxpr/nqgd,nkgd->ngqk/dot_general | solution.py:102
  434.4 16.6 %fusion.125 = f32[2,1152,4,64]{1,3,2,0:T(8,128)} fusion(f32[2,4,576,1152]{3,2,1,0:T(8,128)} %fusion.122, f32[2,4,576]{2,1,0:T(4,128)S(1)} %dynamic-slice_bitcast_fusion.2, f32[2,1152,4,64]{1,3,2,0:T(8,128)} %get-tuple-element.407, pred[]{:T(512)S(6)} %compare.3, bf16[2,2,576,4,64]{2,4,3,1,0:T(8,128)(2,1)} %get-tuple-element.424, s32[]{:T(128)S(6)} %copy.95), kind=kOutput, calls=%fused_computation.21.clone.1 | convolution fusion | flops 696582144 | bytes 26626052 | tf_op jit(solution)/shard_map/while/body/eval_jaxpr/ngqk,nqgd->nkgd/dot_general | solution.py:108
  450.9 13.8 %multiply_convert_fusion.3 = bf16[2,4,576,1152]{3,2,1,0:T(8,128)(2,1)} fusion(f32[2,4,576,1152]{3,2,1,0:T(8,128)} %fusion.122, bf16[2,1152,4,64]{1,3,2,0:T(8,128)(2,1)} %get-tuple-element.425, f32[2,4,576]{2,1,0:T(4,128)S(1)} %bitcast.200, f32[2,4,576]{2,1,0:T(4,128)S(1)} %dynamic-slice_bitcast_fusion.2, ...), kind=kOutput, calls=%fused_computation.14.clone.1 | convolution fusion | flops 711327744 | bytes 33722372 | tf_op jit(solution)/shard_map/while/body/eval_jaxpr/nqgd,nkgd->ngqk/dot_general | solution.py:114
  464.7 8.9 %fusion.124 = f32[2,1152,4,64]{1,3,2,0:T(8,128)} fusion(bf16[2,4,576,1152]{3,2,1,0:T(8,128)(2,1)} %multiply_convert_fusion.3, f32[2,1152,4,64]{1,3,2,0:T(8,128)} %get-tuple-element.406, pred[]{:T(512)S(6)} %compare.3, bf16[2,2,576,4,64]{2,4,3,1,0:T(8,128)(2,1)} %get-tuple-element.421, s32[]{:T(128)S(6)} %copy.95), kind=kOutput, calls=%fused_computation.23.clone.1 | convolution fusion | flops 680656896 | bytes 15990789 | tf_op jit(solution)/shard_map/while/body/eval_jaxpr/ngqk,nqgd->nkgd/dot_general | solution.py:126
  473.7 5.5 fusion.126
  479.4 3.0 convert_element_type.248
  485.7 3.4 fusion.61
  489.6 7.3 copy.73
  496.9 4.9 all-to-all-start.3
  502.3 78.9 %all-to-all-done.3 = bf16[2,1152,3,1,256]{4,0,2,3,1:T(2,128)(2,1)} async-done(((bf16[2,1152,3,1,256]{4,0,2,3,1:T(2,128)(2,1)}), bf16[2,1152,3,1,256]{4,0,2,3,1:T(2,128)(2,1)}, u32[]{:S(2)}, u32[]{:S(2)}) %all-to-all-start.3) | async-done | bytes 3538976 | tf_op jit(solution)/shard_map/all_to_all | solution.py:280
  581.3 2.5 copy.74
  583.7 4.5 copy.75
  588.2 7.3 reshape.217
  595.5 9.0 %convolution_convert_fusion.2 = bf16[1024,3072]{1,0:T(8,128)(2,1)} fusion(bf16[576,1024]{1,0:T(8,128)(2,1)S(1)} %bitcast.199, bf16[576,3072]{1,0:T(8,128)(2,1)} %reshape.217), kind=kOutput, calls=%fused_computation.54 | convolution fusion | flops 3627024384 | bytes 11010048 | tf_op jit(solution)/shard_map/dot_general | solution.py:283
  610.0 9.0 %all-gather.7 = bf16[8,1,128]{2,1,0:T(2,128)(2,1)S(1)} all-gather(bf16[1,1,128]{2,1,0:T(2,128)(2,1)S(1)} %bitcast.230), channel_id=1, replica_groups=mesh['dp'=8,'seq'=4] {'dp'}, dimensions={0}, use_global_device_ids=true | all-gather | bytes 2304 | tf_op jit(solution)/shard_map/all_gather | solution.py:209
  619.1 45.7 %reduce-scatter.5.cloned.1.call-done = bf16[128,3072]{1,0:T(8,128)(2,1)} async-done(((bf16[1024,3072]{1,0:T(8,128)(2,1)}), bf16[128,3072]{1,0:T(8,128)(2,1)}) %reduce-scatter.5.cloned.1.call-update) | async-done | bytes 786448 | tf_op jit(solution)/shard_map/reduce_scatter | solution.py:291
  664.8 10.2 %add_add_fusion = f32[576,1024]{1,0:T(8,128)} fusion(f32[576,1024]{1,0:T(8,128)S(1)} %copy-done.6, bf16[576,4096]{1,0:T(8,128)(2,1)} %get-tuple-element.260, bf16[4096,1024]{1,0:T(8,128)(2,1)} %all-gather.19.cloned.1.call-done, f32[1024]{0:T(1024)S(1)} %bitcast.224, f32[1024]{0:T(1024)S(1)} %bitcast.207), kind=kOutput, calls=%fused_computation.78 | convolution fusion | flops 4833607680 | bytes 17833984 | tf_op jit(solution)/shard_map/dot_general | solution.py:223
  676.3 10.9 %fusion.58 = (bf16[1024]{0:T(1024)(128)(2,1)}, bf16[1024]{0:T(1024)(128)(2,1)}, f32[576]{0:T(1024)}, f32[576]{0:T(1024)}, f32[576,1024]{1,0:T(8,128)}) fusion(f32[576]{0:T(1024)S(1)} %copy-done.28, f32[576]{0:T(1024)S(1)} %copy-done.26, bf16[2,288,1024]{2,1,0:T(8,128)(2,1)S(1)} %copy-done.4, f32[576,1024]{1,0:T(8,128)} %copy-done.16, ...), kind=kOutput, calls=%fused_computation.104 | convolution fusion | flops 3629773824 | bytes 15746048 | tf_op jit(solution)/shard_map/dot_general | solution.py:284
  687.1 25.8 %all-reduce.8 = (bf16[2048]{0:T(1024)(128)(2,1)}, bf16[1024]{0:T(1024)(128)(2,1)}, bf16[1024]{0:T(1024)(128)(2,1)}, bf16[1024]{0:T(1024)(128)(2,1)}, bf16[1024]{...) all-reduce(bf16[2048]{0:T(1024)(128)(2,1)S(1)} %dynamic_update_slic, ...), channel_id=3, replica_groups=mesh['dp'=8,'seq'=4] {'dp'}, use_global_device_ids=true, to_apply=%region_19.20.clone | all-reduce | flops 12288 | bytes 49152
  722.4 12.5 %all-reduce.9 = (bf16[256]{0:T(256)(128)(2,1)}, bf16[128]{0:T(256)(128)(2,1)}, bf16[128]{0:T(256)(128)(2,1)}, bf16[128]{0:T(256)(128)(2,1)}, bf16[128]{0:T(256)(...) all-reduce(bf16[256]{0:T(256)(128)(2,1)} %dynamic-slice.1, ...), channel_id=1, replica_groups=mesh['dp'=8,'seq'=4] {'seq'}, use_global_device_ids=true, to_apply=%region_20.21 | all-reduce | flops 1536 | bytes 6144 | tf_op jit(solution)/shard_map/psum | solution.py:330
  745.7 3.8 multiply_add_fusion
  749.6 39.3 %all-reduce.13.cloned.1.call-done = (bf16[128,3072]{1,0:T(8,128)(2,1)}, bf16[128,1024]{1,0:T(8,128)(2,1)}, bf16[128,4096]{1,0:T(8,128)(2,1)}, bf16[512,1024]{1,0:T(8,128)(2,1)}) async-done(((bf16[128,3072]{1,0:T(8,128)(2,1)}, bf16[128,1024]{1,0:T(8,128)(2,1)}, bf16[128,4096]{1,0:T(8,128)(2,1)}, bf16[512,1024]{1,0:T(8,128)(2,1)}), (bf16[128,3072]{1,0:T(8,128)(2,1)}, bf16[128,1024]{1,0:T(8,128)(2,1)}, ...) | async-done | bytes 3145744 | tf_op jit(solution)/shard_map/psum | solution.py:329
  790.8 2.5 convert_element_type.255
  (206 shorter events, 66.4 us)
Async XLA Ops:
  7.2 2.9 copy-start.2
  7.2 3.8 copy-start.38
  7.2 14.1 %copy-start.39 = (bf16[128]{0:T(256)(128)(2,1)S(1)}, bf16[128]{0:T(256)(128)(2,1)}, u32[]{:S(2)}) copy-start(bf16[128]{0:T(256)(128)(2,1)} %param.24) | copy-start | bytes 772
  7.2 50.9 %all-gather.13.cloned.1.call-start = ((), (), s32[]{:S(2)}) async-start(), calls=%async_computation.8 | async-start | bytes 7077888 | tf_op jit(solution)/shard_map/all_gather | solution.py:168
  7.9 260.1 %all-gather.15.cloned.1.call-start = ((), (), s32[]{:S(2)}) async-start(), calls=%async_computation.9 | async-start | bytes 2359296 | tf_op jit(solution)/shard_map/all_gather | solution.py:169
  8.7 263.4 %all-gather.17.cloned.1.call-start = ((), (), s32[]{:S(2)}) async-start(), calls=%async_computation.10 | async-start | bytes 9437184 | tf_op jit(solution)/shard_map/all_gather | solution.py:204
  10.3 28.0 %copy-start.23 = (f32[2,288]{1,0:T(2,128)}, f32[2,288]{1,0:T(2,128)S(1)}, u32[]{:S(2)}) copy-start(f32[2,288]{1,0:T(2,128)S(1)} %broadcast_multiply_fusion.5) | copy-start | bytes 6916
  10.4 28.8 %copy-start.25 = (f32[576]{0:T(1024)}, f32[576]{0:T(1024)S(1)}, u32[]{:S(2)}) copy-start(f32[576]{0:T(1024)S(1)} %div.35) | copy-start | bytes 6916
  10.9 19.4 %copy-start.31 = (f32[2,288]{1,0:T(2,128)}, f32[2,288]{1,0:T(2,128)S(1)}, u32[]{:S(2)}) copy-start(f32[2,288]{1,0:T(2,128)S(1)} %add_rsqrt_fusion.1) | copy-start | bytes 6916
  11.0 55.1 %copy-start.27 = (f32[576]{0:T(1024)}, f32[576]{0:T(1024)S(1)}, u32[]{:S(2)}) copy-start(f32[576]{0:T(1024)S(1)} %rsqrt.21) | copy-start | bytes 6916
  21.3 44.8 %copy-start.29 = (f32[8,1,128]{2,1,0:T(1,128)}, f32[8,1,128]{2,1,0:T(1,128)S(1)}, u32[]{:S(2)}) copy-start(f32[8,1,128]{2,1,0:T(1,128)S(1)} %convert_element_type.279) | copy-start | bytes 12292
  30.3 35.8 %copy-start.33 = (f32[8,1,128]{2,1,0:T(1,128)}, f32[8,1,128]{2,1,0:T(1,128)S(1)}, u32[]{:S(2)}) copy-start(f32[8,1,128]{2,1,0:T(1,128)S(1)} %convert_element_type.280) | copy-start | bytes 12292
  39.2 18.8 %copy-start.16 = (f32[576,1024]{1,0:T(8,128)}, f32[576,1024]{1,0:T(8,128)S(1)}, u32[]{:S(2)}) copy-start(f32[576,1024]{1,0:T(8,128)S(1)} %fusion.49) | copy-start | bytes 7077892
  74.8 84.1 %all-to-all-start = ((bf16[2,288,3,4,256]{4,1,2,0,3:T(8,128)(2,1)}), bf16[2,288,3,4,256]{4,1,2,0,3:T(8,128)(2,1)S(1)}, u32[]{:S(2)}, u32[]{:S(2)}) async-start(bf16[2,288,3,4,256]{4,1,2,0,3:T(8,128)(2,1)} %copy.58), calls=%async_computation | async-start | bytes 7077888 | tf_op jit(solution)/shard_map/all_to_all | solution.py:193
  79.4 204.1 %all-gather.19.cloned.1.call-start = ((), (), s32[]{:S(2)}) async-start(), calls=%async_computation.11 | async-start | bytes 9437184 | tf_op jit(solution)/shard_map/all_gather | solution.py:205
  170.2 8.4 %copy-start = (f32[2,4,576,1152]{3,2,1,0:T(8,128)}, f32[2,4,576,1152]{3,2,1,0:T(8,128)S(1)}, u32[]{:S(2)}) copy-start(f32[2,4,576,1152]{3,2,1,0:T(8,128)S(1)} %get-tuple-element.360) | copy-start | bytes 63700996 | tf_op jit(solution)/shard_map/while
  198.8 7.1 copy-start
  224.8 6.1 copy-start.36
  224.8 6.1 copy-start.40
  224.8 14.9 %copy-start.41 = (bf16[128]{0:T(256)(128)(2,1)S(1)}, bf16[128]{0:T(256)(128)(2,1)}, u32[]{:S(2)}) copy-start(bf16[128]{0:T(256)(128)(2,1)} %param.25) | copy-start | bytes 772
  224.8 22.7 %copy-start.42 = (bf16[128]{0:T(256)(128)(2,1)S(1)}, bf16[128]{0:T(256)(128)(2,1)}, u32[]{:S(2)}) copy-start(bf16[128]{0:T(256)(128)(2,1)} %param.26) | copy-start | bytes 772
  227.3 38.3 %all-to-all-start.1 = ((bf16[2,1152,1,256]{3,0,2,1:T(2,128)(2,1)}), bf16[2,1152,1,256]{3,0,2,1:T(2,128)(2,1)S(1)}, u32[]{:S(2)}, u32[]{:S(2)}) async-start(bf16[2,1152,1,256]{3,0,2,1:T(2,128)(2,1)} %reshape.249), calls=%async_computation.1 | async-start | bytes 2359296 | tf_op jit(solution)/shard_map/all_to_all | solution.py:195
  230.8 388.2 %reduce-scatter.7.cloned.1.call-start = ((), (), s32[]{:S(2)}) async-start(), calls=%async_computation.13 | async-start | bytes 2359296 | tf_op jit(solution)/shard_map/reduce_scatter | solution.py:297
  239.7 69.0 %copy-start.21 = (f32[8,1,128]{2,1,0:T(1,128)}, f32[8,1,128]{2,1,0:T(1,128)S(1)}, u32[]{:S(2)}) copy-start(f32[8,1,128]{2,1,0:T(1,128)S(1)} %convert_element_type.281) | copy-start | bytes 12292
  265.8 2.2 copy-start.3
  271.4 37.3 %copy-start.5 = (f32[576,1024]{1,0:T(8,128)}, f32[576,1024]{1,0:T(8,128)S(1)}, u32[]{:S(2)}) copy-start(f32[576,1024]{1,0:T(8,128)S(1)} %bitcast_add_fusion) | copy-start | bytes 7077892
  272.1 11.4 %copy-start.14 = (bf16[2,288,1024]{2,1,0:T(8,128)(2,1)S(1)}, bf16[2,288,1024]{2,1,0:T(8,128)(2,1)}, u32[]{:S(2)}) copy-start(bf16[2,288,1024]{2,1,0:T(8,128)(2,1)} %param.31) | copy-start | bytes 3538948
  283.5 12.8 %copy-start.44 = (bf16[1024,4096]{1,0:T(8,128)(2,1)S(1)}, bf16[1024,4096]{1,0:T(8,128)(2,1)}, u32[]{:S(2)}) copy-start(bf16[1024,4096]{1,0:T(8,128)(2,1)} %all-gather.17.cloned.1.call-done) | copy-start | bytes 25165828
  296.3 6.1 copy-start.46
  302.5 3.0 copy-start.17
  304.0 1.4 copy-start.9
  305.4 3.3 copy-start.35
  308.6 310.4 %reduce-scatter.9.cloned.1.call-start = ((), (), s32[]{:S(2)}) async-start(), calls=%async_computation.14 | async-start | bytes 9437184 | tf_op jit(solution)/shard_map/reduce_scatter | solution.py:315
  320.8 1.7 copy-start.10
  326.4 6.2 copy-start.15
  327.7 34.0 %all-to-all-start.2 = ((bf16[2,288,4,256]{3,1,0,2:T(8,128)(2,1)}), bf16[2,288,4,256]{3,1,0,2:T(8,128)(2,1)S(1)}, u32[]{:S(2)}, u32[]{:S(2)}) async-start(bf16[2,288,4,256]{3,1,0,2:T(8,128)(2,1)} %copy.68), calls=%async_computation.2 | async-start | bytes 2359296 | tf_op jit(solution)/shard_map/all_to_all | solution.py:262
  332.6 286.4 %reduce-scatter.11.cloned.1.call-start = ((), (), s32[]{:S(2)}) async-start(), calls=%async_computation.15 | async-start | bytes 9437184 | tf_op jit(solution)/shard_map/reduce_scatter | solution.py:321
  363.0 3.2 copy-start.20
  406.8 8.4 %copy-start.1 = (bf16[2,4,576,1152]{3,2,1,0:T(8,128)(2,1)S(1)}, bf16[2,4,576,1152]{3,2,1,0:T(8,128)(2,1)}, u32[]{:S(2)}) copy-start(bf16[2,4,576,1152]{3,2,1,0:T(8,128)(2,1)} %multiply_convert_fusion.3) | copy-start | bytes 31850500 | tf_op jit(solution)/shard_map/while
  464.7 8.9 %copy-start.1 = (bf16[2,4,576,1152]{3,2,1,0:T(8,128)(2,1)S(1)}, bf16[2,4,576,1152]{3,2,1,0:T(8,128)(2,1)}, u32[]{:S(2)}) copy-start(bf16[2,4,576,1152]{3,2,1,0:T(8,128)(2,1)} %multiply_convert_fusion.3) | copy-start | bytes 31850500 | tf_op jit(solution)/shard_map/while
  479.4 3.1 copy-start.7
  485.7 3.4 copy-start.12
  485.7 3.4 copy-start.13
  496.8 4.9 copy-start.4
  496.8 4.9 copy-start.24
  496.8 5.0 copy-start.30
  496.8 5.0 copy-start.32
  496.8 5.0 copy-start.34
  496.9 84.4 %all-to-all-start.3 = ((bf16[2,1152,3,1,256]{4,0,2,3,1:T(2,128)(2,1)}), bf16[2,1152,3,1,256]{4,0,2,3,1:T(2,128)(2,1)}, u32[]{:S(2)}, u32[]{:S(2)}) async-start(bf16[2,1152,3,1,256]{4,0,2,3,1:T(2,128)(2,1)} %copy.73), calls=%async_computation.3 | async-start | bytes 7077888 | tf_op jit(solution)/shard_map/all_to_all | solution.py:280
  501.7 163.1 %reduce-scatter.5.cloned.1.call-start = ((), (), s32[]{:S(2)}) async-start(), calls=%async_computation.12 | async-start | bytes 7077888 | tf_op jit(solution)/shard_map/reduce_scatter | solution.py:291
  604.6 0.7 copy-start.45
  604.6 5.5 copy-start.43
  604.6 60.2 %copy-start.6 = (f32[576,1024]{1,0:T(8,128)S(1)}, f32[576,1024]{1,0:T(8,128)}, u32[]{:S(2)}) copy-start(f32[576,1024]{1,0:T(8,128)} %copy-done.5) | copy-start | bytes 7077892
  604.6 60.2 %copy-start.22 = (f32[8,1,128]{2,1,0:T(1,128)S(1)}, f32[8,1,128]{2,1,0:T(1,128)}, u32[]{:S(2)}) copy-start(f32[8,1,128]{2,1,0:T(1,128)} %copy-done.21) | copy-start | bytes 12292
  604.6 184.3 %all-reduce.13.cloned.1.call-start = ((), (), s32[]{:S(2)}) async-start(), calls=%async_computation.16 | async-start | bytes 6291456 | tf_op jit(solution)/shard_map/psum | solution.py:329
  664.8 10.3 %copy-start.8 = (f32[2,2,576,4,64]{2,4,3,1,0:T(8,128)S(1)}, f32[2,2,576,4,64]{2,4,3,1,0:T(8,128)}, u32[]{:S(2)}) copy-start(f32[2,2,576,4,64]{2,4,3,1,0:T(8,128)} %get-tuple-element.103) | copy-start | bytes 7077892
  675.1 0.7 copy-start.37
  675.1 1.1 copy-start.26
  675.1 1.1 copy-start.28
  676.2 69.5 %copy-start.11 = (f32[576,1024]{1,0:T(8,128)S(1)}, f32[576,1024]{1,0:T(8,128)}, u32[]{:S(2)}) copy-start(f32[576,1024]{1,0:T(8,128)} %copy-done.9) | copy-start | bytes 7077892
  788.9 4.4 copy-start.19
  790.8 4.1 copy-start.18
Sparse Core Ops, SparseCore 0:
  9.9 48.1 all-gather.12
  59.9 27.7 all-gather.14
  89.7 54.2 all-gather.16
  145.7 54.2 all-gather.18
  308.8 41.5 reduce-scatter.6
  353.6 71.5 reduce-scatter.8
  428.6 71.5 reduce-scatter.10
  604.7 60.0 reduce-scatter.4
  667.4 121.4 all-reduce.12
where the time goes:
time: 810 us; the launch traced here: 803 us
  waiting for transfers between devices  282 us (35%)
  matrix products  241 us (30%)
  blocking collectives  108 us (13%)
  local copies, waits for them, and re-layouts  85.9 us (11%)
  other arithmetic  50.8 us (6%)
  starting transfers between devices  18.8 us (2%)
  between operations  16.9 us (2%)
    all_to_all x1, waiting for transfers between devices, body(): lax.all_to_all(projected, 'seq', split_axis=3, concat_axis=1, tiled=True)  78.9 us
    all_to_all x1, waiting for transfers between devices, body(): lax.all_to_all(stacked_grad, 'seq', split_axis=1, concat_axis=3, tiled=True)  78.9 us
    reduce_scatter x1, waiting for transfers between devices, body(): lax.psum_scatter(grad_qkv.astype(jnp.bfloat16), 'dp', scatter_dimension=0...  45.7 us
    psum x1, waiting for transfers between devices, body(): lax.psum(shares[0].astype(jnp.bfloat16), 'seq').astype(jnp.float32)  39.3 us
    dot_general x4, matrix products, one_block(): jnp.einsum('nqgd,nkgd->ngqk', query_block, key_heads, preferred_element_t...  33.5 us
    dot_general x2, matrix products, one_block(): jnp.einsum('ngqk,nqgd->nkgd', probs.astype(jnp.bfloat16), grad_block, pre...  29.4 us
    dot_general x2, matrix products, one_block(): jnp.einsum('nqgd,nkgd->ngqk', grad_block, value_heads, preferred_element_...  27.3 us
    unnamed x1, blocking collectives  25.8 us
  transfers between devices with their start and end apart: 13, of which 6 were waited for; matrix products, arithmetic and copies ran while one was open for 41% of the time, Pallas kernels for 0%

commit v1 on v0

v1 whole, which is shorter than its diff:
```python
import functools

import jax
import jax.numpy as jnp
from jax import lax
from jax.experimental import pallas as pl
from jax.experimental.pallas import tpu as pltpu
from jax.sharding import PartitionSpec as P

HEAD_DIM = 64
LANES = 128
f32 = jnp.float32
bf16 = jnp.bfloat16

epsilon = 1e-06


def norm_stats(matrix):
    mean_val = jnp.mean(matrix, axis=-1, keepdims=True)
    centred = matrix - mean_val
    inv_std = lax.rsqrt(jnp.mean(centred * centred, axis=-1, keepdims=True) + epsilon)
    return (centred * inv_std, inv_std)


def norm_backward(grad_in, normed, inv_std, gain):
    scaled = grad_in * gain
    return inv_std * (
        scaled
        - jnp.mean(scaled, axis=-1, keepdims=True)
        - normed * jnp.mean(scaled * normed, axis=-1, keepdims=True)
    )


def gelu_cdf(pre_act):
    return 0.5 * (1.0 + lax.erf(pre_act * 0.7071067811865476))


def gelu_slope(pre_act):
    return gelu_cdf(pre_act) + pre_act * jnp.exp(-0.5 * pre_act * pre_act) * 0.3989422804014327


def dot(left, right, left_dim=1, right_dim=0):
    return lax.dot_general(
        left, right, (((left_dim,), (right_dim,)), ((), ())), preferred_element_type=f32
    )


def transpose_low(matrix):
    return matrix.astype(f32).T.astype(bf16)


def pair_masks():
    lane = lax.broadcasted_iota(jnp.int32, (1, LANES), 1)
    return (lane < HEAD_DIM, lane >= HEAD_DIM)


def attend_kernel(q_ref, k_ref, v_ref, out_ref, lse_ref, v_flip):
    @pl.when(pl.program_id(1) == 0)
    def _():
        v_flip[...] = transpose_low(v_ref[...])

    query = q_ref[...] * jnp.asarray(HEAD_DIM**-0.5, bf16)
    key = k_ref[...]
    pieces = []
    for head, mask in enumerate(pair_masks()):
        scores = dot(key, jnp.where(mask, query, jnp.zeros_like(query)), 1, 1)
        peak = jnp.max(scores, axis=0, keepdims=True)
        lifted = jnp.exp(scores - peak)
        total = jnp.sum(lifted, axis=0, keepdims=True)
        probs = (lifted * (1.0 / total)).astype(bf16)
        rows = slice(head * HEAD_DIM, (head + 1) * HEAD_DIM)
        pieces.append(dot(v_flip[rows, :], probs))
        lse_ref[0, head : head + 1, :] = peak + jnp.log(total)
    out_ref[...] = jnp.concatenate(pieces, axis=0).T.astype(bf16)


def attend_back_kernel(
    q_ref, k_ref, v_ref, out_ref, grad_ref, lse_ref, all_ref, sums_ref, k_flip, dk_sum, dv_sum
):
    pair, block = pl.program_id(0), pl.program_id(1)
    pairs, blocks = pl.num_programs(0), pl.num_programs(1)
    block_rows = q_ref.shape[0]

    @pl.when(block == 0)
    def _():
        k_flip[...] = transpose_low(k_ref[...])
        dk_sum[...] = jnp.zeros_like(dk_sum)
        dv_sum[...] = jnp.zeros_like(dv_sum)
        sums_ref[...] = jnp.zeros_like(sums_ref)

    query = q_ref[...] * jnp.asarray(HEAD_DIM**-0.5, bf16)
    key = k_ref[...]
    value = v_ref[...]
    grad = grad_ref[...]
    mixed = (grad.astype(f32) * out_ref[...].astype(f32)).T
    pieces = []
    for head, mask in enumerate(pair_masks()):
        rows = slice(head * HEAD_DIM, (head + 1) * HEAD_DIM)
        query_one = jnp.where(mask, query, jnp.zeros_like(query))
        grad_one = jnp.where(mask, grad, jnp.zeros_like(grad))
        probs = jnp.exp(dot(key, query_one, 1, 1) - lse_ref[0, head : head + 1, :])
        prob_grad = dot(value, grad_one, 1, 1)
        delta = jnp.sum(mixed[rows], axis=0, keepdims=True)
        score_grad = (probs * (prob_grad - delta) * HEAD_DIM**-0.5).astype(bf16)
        dv_sum[...] += dot(probs.astype(bf16), grad_one)
        dk_sum[...] += dot(score_grad, query_one)
        pieces.append(dot(k_flip[rows, :], score_grad))
    query_grad = jnp.concatenate(pieces, axis=0).T
    row_at = pl.multiple_of(block * block_rows, block_rows)
    lanes = pl.ds(pl.multiple_of(pair * LANES, LANES), LANES)
    all_ref[pl.ds(row_at, block_rows), lanes] = query_grad.astype(bf16)
    sums_ref[0, 0:1, :] += jnp.sum(query_grad, axis=0, keepdims=True)

    @pl.when(block == blocks - 1)
    def _():
        key_lanes = pl.ds(pl.multiple_of((pairs + pair) * LANES, LANES), LANES)
        value_lanes = pl.ds(pl.multiple_of((2 * pairs + pair) * LANES, LANES), LANES)
        all_ref[:, key_lanes] = (dk_sum[...] * HEAD_DIM**0.5).astype(bf16)
        all_ref[:, value_lanes] = dv_sum[...].astype(bf16)
        sums_ref[0, 1:2, :] = jnp.sum(dv_sum[...], axis=0, keepdims=True)


def block_size(length):
    return next(size for size in (384, 256, 128, length) if length % size == 0)


def attend(projected):
    length, head_cols = projected.shape[0], projected.shape[1] // 3
    pairs = head_cols // LANES
    rows = block_size(length)
    query_spec = pl.BlockSpec((rows, LANES), lambda h, b: (b, h))
    return pl.pallas_call(
        attend_kernel,
        grid=(pairs, length // rows),
        in_specs=[
            query_spec,
            pl.BlockSpec((length, LANES), lambda h, b: (0, pairs + h)),
            pl.BlockSpec((length, LANES), lambda h, b: (0, 2 * pairs + h)),
        ],
        out_specs=[query_spec, pl.BlockSpec((1, 2, rows), lambda h, b: (h, 0, b))],
        out_shape=[
            jax.ShapeDtypeStruct((length, head_cols), bf16),
            jax.ShapeDtypeStruct((pairs, 2, length), f32),
        ],
        scratch_shapes=[pltpu.VMEM((LANES, length), bf16)],
        compiler_params=pltpu.CompilerParams(vmem_limit_bytes=58 * 2**20),
        cost_estimate=pl.CostEstimate(
            flops=16 * pairs * length * length * LANES,
            bytes_accessed=8 * length * head_cols,
            transcendentals=2 * pairs * length * length,
        ),
        name="attend",
    )(projected, projected, projected)


def attend_back(projected, attended, log_total, grad):
    length, head_cols = attended.shape
    pairs = head_cols // LANES
    rows = block_size(length)
    query_spec = pl.BlockSpec((rows, LANES), lambda h, b: (b, h))
    return pl.pallas_call(
        attend_back_kernel,
        grid=(pairs, length // rows),
        in_specs=[
            query_spec,
            pl.BlockSpec((length, LANES), lambda h, b: (0, pairs + h)),
            pl.BlockSpec((length, LANES), lambda h, b: (0, 2 * pairs + h)),
            query_spec,
            query_spec,
            pl.BlockSpec((1, 2, rows), lambda h, b: (h, 0, b)),
        ],
        out_specs=[
            pl.BlockSpec((length, 3 * head_cols), lambda h, b: (0, 0)),
            pl.BlockSpec((1, 2, LANES), lambda h, b: (h, 0, 0)),
        ],
        out_shape=[
            jax.ShapeDtypeStruct((length, 3 * head_cols), bf16),
            jax.ShapeDtypeStruct((pairs, 2, LANES), f32),
        ],
        scratch_shapes=[
            pltpu.VMEM((LANES, length), bf16),
            pltpu.VMEM((length, LANES), f32),
            pltpu.VMEM((length, LANES), f32),
        ],
        compiler_params=pltpu.CompilerParams(vmem_limit_bytes=58 * 2**20),
        cost_estimate=pl.CostEstimate(
            flops=40 * pairs * length * length * LANES,
            bytes_accessed=16 * length * head_cols,
            transcendentals=2 * pairs * length * length,
        ),
        name="attend_back",
    )(projected, projected, projected, attended, grad, log_total)


def body(
    images,
    qkv_weight,
    qv_bias,
    proj_weight,
    proj_bias,
    ln1_gain,
    ln1_bias,
    ln2_gain,
    ln2_bias,
    fc1_weight,
    fc1_bias,
    fc2_weight,
    fc2_bias,
    cotangent,
):
    items, tokens, width = images.shape
    own_rows = items * tokens
    seq_ways, dp_ways = lax.axis_size("seq"), lax.axis_size("dp")
    chips = dp_ways // 2
    shard_rows = width // dp_ways
    column_items = 2 * items
    ranks = seq_ways // column_items
    groups = 2 * ranks
    head_cols = width // groups
    length = seq_ways * tokens
    half = tokens // 2
    dp_index, seq_index = lax.axis_index("dp"), lax.axis_index("seq")
    core, chip = dp_index % 2, dp_index // 2
    first_core = core == 0
    rank = seq_index % ranks
    group = rank * 2 + core
    same_core = [[2 * q + c for q in range(chips)] for c in range(2)]

    def swap(array):
        return lax.ppermute(array, "dp", [(i, i ^ 1) for i in range(dp_ways)])

    def by_core(own, other, axis):
        return jnp.where(
            first_core, jnp.stack([own, other], axis), jnp.stack([other, own], axis)
        )

    def pick(array, index, axis):
        return lax.dynamic_index_in_dim(array, index, axis, keepdims=False)

    def hop(array, bits):
        return lax.ppermute(array, "dp", [(i, i ^ (2 * bits)) for i in range(dp_ways)])

    def gather_chips(block):
        if chips != 4:
            return lax.all_gather(block, "dp", axis=0, axis_index_groups=same_core)
        gathered = jnp.zeros((4,) + block.shape, block.dtype)
        gathered = lax.dynamic_update_index_in_dim(gathered, block, chip, 0)
        for bits in (1, 2, 3):
            gathered = lax.dynamic_update_index_in_dim(gathered, hop(block, bits), chip ^ bits, 0)
        return gathered

    def scatter_chips(blocks):
        if chips != 4:
            return lax.psum_scatter(
                blocks, "dp", scatter_dimension=0, tiled=False, axis_index_groups=same_core
            )
        total = pick(blocks, chip, 0).astype(f32)
        for bits in (1, 2, 3):
            total = total + hop(pick(blocks, chip ^ bits, 0), bits).astype(f32)
        return total.astype(bf16)

    small_names = (qv_bias, proj_bias, ln1_gain, ln1_bias, ln2_gain, ln2_bias, fc1_bias, fc2_bias)
    small = lax.all_gather(jnp.concatenate(small_names), "dp", axis=0)
    smalls, at = [], 0
    for array in small_names:
        smalls.append(small[:, at : at + array.shape[0]].reshape(-1).astype(f32))
        at += array.shape[0]
    qv_full, bias_proj, gain_first, shift_first, gain_second, shift_second, bias_one, bias_two = (
        smalls
    )

    kept = lax.dynamic_slice_in_dim(images, core * half, half, 1)
    given = swap(lax.dynamic_slice_in_dim(images, (1 - core) * half, half, 1))
    column = by_core(kept, given, 0).reshape(column_items, half, width)
    arrived = lax.all_to_all(jnp.repeat(column, ranks, axis=0), "seq", 0, 0)
    image_rows = by_core(arrived, swap(arrived), 1).reshape(length, width).astype(f32)

    qkv_parts = qkv_weight.reshape(shard_rows, 3, groups, head_cols)
    qkv_block = by_core(pick(qkv_parts, group, 2), swap(pick(qkv_parts, group ^ 1, 2)), 0)
    qkv_block = qkv_block.reshape(2 * shard_rows, 3 * head_cols)
    qkv_full = gather_chips(qkv_block).reshape(width, 3 * head_cols)
    proj_full = lax.all_gather(proj_weight, "dp", axis=0, tiled=True)

    fc1_parts = fc1_weight.reshape(shard_rows, chips, 2, -1)
    fc1_block = by_core(pick(fc1_parts, core, 2), swap(pick(fc1_parts, 1 - core, 2)), 0)
    fc1_block = fc1_block.reshape(2 * shard_rows, -1)
    fc1_half = gather_chips(fc1_block).reshape(width, -1)
    fc2_half = gather_chips(fc2_weight).reshape(-1, width)
    bias_one_half = pick(bias_one.reshape(chips, 2, -1), core, 1).reshape(-1)
    cotangent_own = cotangent.reshape(own_rows, width)
    cotangent_all = by_core(cotangent_own, swap(cotangent_own), 0).reshape(2 * own_rows, width)

    bias_parts = qv_full.reshape(2, groups, head_cols)
    bias_group = pick(bias_parts, group, 1)
    bias_row = jnp.concatenate(
        [bias_group[0], jnp.zeros((head_cols,), f32), bias_group[1]]
    )
    normed_image, _ = norm_stats(image_rows)
    hidden_first = (normed_image * gain_first + shift_first).astype(bf16)
    projected = (dot(hidden_first, qkv_full) + bias_row).astype(bf16)
    attended, log_total = attend(projected)

    back = lax.all_to_all(attended.reshape(seq_ways, tokens, head_cols), "seq", 0, 0)
    back = back.reshape(2, items, ranks, tokens, head_cols)
    both = by_core(pick(back, core, 0), swap(pick(back, 1 - core, 0)), 3)
    attended_rows = jnp.moveaxis(both, 1, 2).reshape(own_rows, width)

    flat_rows = images.reshape(own_rows, width).astype(f32)
    residual_first = flat_rows + dot(attended_rows, proj_full) + bias_proj
    normed_second, inv_second = norm_stats(residual_first)
    hidden_own = (normed_second * gain_second + shift_second).astype(bf16)
    hidden_second = by_core(hidden_own, swap(hidden_own), 0).reshape(2 * own_rows, width)
    pre_act = dot(hidden_second, fc1_half) + bias_one_half
    acts = (pre_act * gelu_cdf(pre_act)).astype(bf16)

    def meet(partial):
        parts = partial.reshape(2, own_rows, width)
        return pick(parts, core, 0) + swap(pick(parts, 1 - core, 0).astype(bf16)).astype(f32)

    output = residual_first + meet(dot(acts, fc2_half)) + bias_two

    pre_grad = dot(cotangent_all, fc2_half, 1, 1) * gelu_slope(pre_act)
    pre_grad_low = pre_grad.astype(bf16)
    grad_bias_one = jnp.sum(pre_grad, axis=0)
    grad_out = cotangent_own.astype(f32)
    grad_bias_two = jnp.sum(grad_out, axis=0)
    hidden_second_grad = meet(dot(pre_grad_low, fc1_half, 1, 1))
    grad_gain_second = jnp.sum(hidden_second_grad * normed_second, axis=0)
    grad_shift_second = jnp.sum(hidden_second_grad, axis=0)
    residual_grad = grad_out + norm_backward(
        hidden_second_grad, normed_second, inv_second, gain_second
    )
    residual_grad_low = residual_grad.astype(bf16)
    grad_proj_bias = jnp.sum(residual_grad, axis=0)
    attended_grad = dot(residual_grad_low, proj_full, 1, 1).astype(bf16)
    attended_grad = attended_grad.reshape(items, tokens, ranks, 2, head_cols)
    mine = by_core(
        pick(attended_grad, core, 3), swap(pick(attended_grad, 1 - core, 3)), 0
    ).reshape(column_items, tokens, ranks, head_cols)
    mine = jnp.moveaxis(mine, 2, 1).reshape(seq_ways, tokens, head_cols)
    grad_heads = lax.all_to_all(mine, "seq", 0, 0).reshape(length, head_cols)

    grad_fc_two = dot(acts, cotangent_all, 0, 0).astype(bf16)
    grad_fc_one = dot(hidden_second, pre_grad_low, 0, 0).astype(bf16)
    grad_proj = dot(attended_rows, residual_grad_low, 0, 0).astype(bf16)

    def shares(vector):
        return vector.reshape(dp_ways, -1)

    one_parts = grad_bias_one.reshape(chips, 1, -1)
    one_all = jnp.where(
        jnp.arange(2)[None, :, None] == core, jnp.broadcast_to(one_parts, (chips, 2, one_parts.shape[2])), 0.0
    )
    extra = jnp.concatenate(
        [
            shares(grad_proj_bias),
            shares(grad_gain_second),
            shares(grad_shift_second),
            shares(grad_bias_two),
            shares(one_all),
        ],
        axis=1,
    ).astype(bf16)
    extra = jnp.pad(extra[:, None, :], ((0, 0), (0, 15), (0, width - extra.shape[1])))
    proj_blocks = jnp.concatenate([grad_proj.reshape(dp_ways, shard_rows, width), extra], axis=1)

    share_two = scatter_chips(grad_fc_two.reshape(chips, -1, width))
    share_one = scatter_chips(grad_fc_one.reshape(chips, 2 * shard_rows, -1))
    share_proj = lax.psum_scatter(proj_blocks, "dp", scatter_dimension=0, tiled=True)[0]
    share_two = lax.psum(share_two, "seq")
    share_one, share_two = lax.optimization_barrier((share_one, share_two))
    share_one = lax.psum(share_one, "seq")
    share_proj, share_one = lax.optimization_barrier((share_proj, share_one))
    share_proj = lax.psum(share_proj, "seq")

    qkv_grad, bias_sums = attend_back(projected, attended, log_total, grad_heads)
    hidden_partial = dot(qkv_grad, qkv_full, 1, 1)
    grad_gain_first = jnp.sum(hidden_partial * normed_image, axis=0)
    grad_shift_first = jnp.sum(hidden_partial, axis=0)
    partial_parts = hidden_partial.reshape(seq_ways, 2, half, width)
    chip_sum = pick(partial_parts, core, 1) + swap(
        pick(partial_parts, 1 - core, 1).astype(bf16)
    ).astype(f32)
    home = lax.all_to_all(chip_sum.astype(bf16), "seq", 0, 0)
    home = home.reshape(2, items, ranks, half, width)
    if ranks > 1:
        home = jnp.sum(home.astype(f32), axis=2, keepdims=True).astype(bf16)
    home = home[:, :, 0]
    hidden_first_grad = by_core(pick(home, core, 0), swap(pick(home, 1 - core, 0)), 1)
    hidden_first_grad = hidden_first_grad.reshape(own_rows, width).astype(f32)
    normed_first, inv_first = norm_stats(flat_rows)
    image_grad = residual_grad + norm_backward(
        hidden_first_grad, normed_first, inv_first, gain_first
    )

    grad_qkv = dot(hidden_first, qkv_grad, 0, 0).astype(bf16)
    grad_qkv = grad_qkv.reshape(chips, 2 * shard_rows, 3, 1, head_cols)
    qv_sums = jnp.moveaxis(bias_sums, 1, 0).reshape(2, 1, head_cols)
    qv_all = lax.dynamic_update_slice(jnp.zeros((2, groups, head_cols), f32), qv_sums, (0, group, 0))
    extra = jnp.concatenate(
        [
            grad_gain_first.reshape(chips, -1),
            grad_shift_first.reshape(chips, -1),
            qv_all.reshape(chips, -1),
        ],
        axis=1,
    ).astype(bf16)
    extra_cols = extra.shape[1]
    extra = jnp.pad(extra[:, None, :], ((0, 0), (0, 15), (0, 3 * head_cols - extra_cols)))
    blocks = jnp.concatenate(
        [grad_qkv.reshape(chips, 2 * shard_rows, 3 * head_cols), extra], axis=1
    )
    share_qkv = scatter_chips(blocks)
    extra = share_qkv[2 * shard_rows, :extra_cols]
    share_qkv = share_qkv[: 2 * shard_rows].reshape(2 * shard_rows, 3, 1, head_cols)
    if ranks > 1:
        share_qkv = lax.dynamic_update_slice(
            jnp.zeros((2 * shard_rows, 3, ranks, head_cols), bf16), share_qkv, (0, 0, rank, 0)
        )
    flat = jnp.concatenate(
        [
            share_qkv.reshape(2 * shard_rows, -1),
            jnp.pad(extra[None], ((0, 15), (0, ranks * 3 * head_cols - extra_cols))),
        ],
        axis=0,
    )
    flat, share_proj = lax.optimization_barrier((flat, share_proj))
    flat = lax.psum(flat, "seq")
    rows_parts = flat[: 2 * shard_rows].reshape(2, shard_rows, 3, ranks, head_cols)
    extra = flat[2 * shard_rows : 2 * shard_rows + 1]
    out_qkv = by_core(pick(rows_parts, core, 0), swap(pick(rows_parts, 1 - core, 0)), 3)
    out_qkv = out_qkv.reshape(shard_rows, 3 * width).astype(f32)
    extra = (extra.astype(f32) + swap(extra).astype(f32))[0]
    per_chip = width // chips
    out_gain_first = pick(extra[:per_chip].reshape(2, -1), core, 0)
    out_shift_first = pick(extra[per_chip : 2 * per_chip].reshape(2, -1), core, 0)
    out_qv = pick(extra[2 * per_chip : 4 * per_chip].reshape(2, -1), core, 0)

    one_rows = share_one.reshape(2, shard_rows, chips, -1)
    out_one = by_core(pick(one_rows, core, 0), swap(pick(one_rows, 1 - core, 0)), 2)
    out_one = out_one.reshape(shard_rows, -1).astype(f32)
    last = share_proj[shard_rows].astype(f32)
    out_smalls, at = [], 0
    for size in (shard_rows, shard_rows, shard_rows, shard_rows, 4 * shard_rows):
        out_smalls.append(last[at : at + size])
        at += size
    return (
        output.reshape(images.shape),
        image_grad.reshape(images.shape),
        out_qkv,
        out_qv,
        share_proj[:shard_rows].astype(f32),
        out_smalls[0],
        out_gain_first,
        out_shift_first,
        out_smalls[1],
        out_smalls[2],
        out_one,
        out_smalls[4],
        share_two.astype(f32),
        out_smalls[3],
    )


def solution(mesh):
    rows, cols, flat = P("dp", "seq", None), P("dp", None), P("dp")
    in_specs = (rows, cols, flat, cols, flat, flat, flat, flat, flat, cols, flat, cols, flat, rows)
    out_specs = (rows, rows, cols, flat, cols, flat, flat, flat, flat, flat, cols, flat, cols, flat)
    return jax.shard_map(body, mesh=mesh, in_specs=in_specs, out_specs=out_specs, check_vma=False)
```

time: 810 us -> 663 us (0.82)
  matrix products: 241 us -> 78.1 us
  blocking collectives: 108 us -> 33.3 us
  Pallas kernels: 0 us -> 60.3 us
  waiting for transfers between devices: 282 us -> 253 us
  starting transfers between devices: 18.8 us -> 46.2 us
  local copies, waits for them, and re-layouts: 85.9 us -> 111 us
  other arithmetic: 50.8 us -> 60.3 us
    all_to_all x4, waiting for transfers between devices: 176 us -> 6.18 us  [the longest x1 6.17 us: body(): lax.all_to_all(attended.reshape(seq_ways, tokens, head_cols), 'seq', 0, 0)]
    dot_general x26 -> x12, matrix products: 241 us -> 78.1 us  [dot(): lax.dot_general(left, right, (((left_dim,), (right_dim,)), ((), ())), pre...]
    ppermute x0 -> x33, waiting for transfers between devices: none -> 139 us  [the longest x18 137 us: hop(): lax.ppermute(array, 'dp', [(i, i ^ 2 * bits) for i in range(dp_ways)])]
    psum x1 -> x4, waiting for transfers between devices: 39.3 us -> 107 us  [the longest x1 42.1 us: body(): share_proj = lax.psum(share_proj, 'seq')]
    pallas_call x0 -> x2, Pallas kernels: none -> 60.3 us  [the longest x1 35.5 us: attend_back(): pl.pallas_call(attend_back_kernel, grid=(pairs, length // rows), in_specs...]
    reduce_scatter x4 -> x1, waiting for transfers between devices: 45.7 us -> 0.02 us  [body(): lax.psum_scatter(proj_blocks, 'dp', scatter_dimension=0, tiled=True)[0]]
    all_gather x8 -> x1, blocking collectives: 69.7 us -> 33.3 us  [body(): small = lax.all_gather(jnp.concatenate(small_names), 'dp', axis=0)]
    unnamed x1 -> x0, blocking collectives: 25.8 us -> none
  transfers between devices with their start and end apart: 13 -> 43, of which waited for: 6 -> 16; matrix products, arithmetic and copies ran while one was open for 41% -> 28% of each run, Pallas kernels for 0% -> 9%
where the time goes in v1:
time: 663 us; the launch traced here: 657 us
  waiting for transfers between devices  253 us (38%)
  local copies, waits for them, and re-layouts  111 us (17%)
  matrix products  78.1 us (12%)
  other arithmetic  60.3 us (9%)
  Pallas kernels  60.3 us (9%)
  starting transfers between devices  46.2 us (7%)
  blocking collectives  33.3 us (5%)
  between operations  15.5 us (2%)
    ppermute x18, waiting for transfers between devices, hop(): lax.ppermute(array, 'dp', [(i, i ^ 2 * bits) for i in range(dp_ways)])  137 us
    dot_general x12, matrix products, dot(): lax.dot_general(left, right, (((left_dim,), (right_dim,)), ((), ())), pre...  78.1 us
    psum x1, waiting for transfers between devices, body(): share_proj = lax.psum(share_proj, 'seq')  42.1 us
    psum x1, waiting for transfers between devices, body(): flat = lax.psum(flat, 'seq')  36.7 us
    pallas_call x1, Pallas kernels, attend_back(): pl.pallas_call(attend_back_kernel, grid=(pairs, length // rows), in_specs...  35.5 us
    all_gather x1, blocking collectives, body(): small = lax.all_gather(jnp.concatenate(small_names), 'dp', axis=0)  33.3 us
    psum x1, waiting for transfers between devices, body(): share_two = lax.psum(share_two, 'seq')  28.2 us
    unnamed x140, local copies, waits for them, and re-layouts  28 us
  transfers between devices with their start and end apart: 43, of which 16 were waited for; matrix products, arithmetic and copies ran while one was open for 28% of the time, Pallas kernels for 9%

profile of v1, /device:TPU:0, one launch (start us, length us, event | category | flops | bytes accessed | tf_op | source)
XLA Modules:
  0.0 657.4 jit_solution(8035207081908690634)
XLA Ops:
  12.0 6.2 all-to-all-start
  22.3 33.3 %all-gather.1 = bf16[8,1,1536]{2,1,0:T(2,128)(2,1)S(1)} all-gather(bf16[1,1,1536]{2,1,0:T(2,128)(2,1)S(1)} %reshape.792), channel_id=2, replica_groups=mesh['dp'=8,'seq'=4] {'dp'}, dimensions={0}, use_global_device_ids=true | all-gather | bytes 27648 | tf_op jit(solution)/shard_map/all_gather | solution.py:263
  61.8 2.1 copy.141
  68.5 2.0 copy.108
  73.5 2.6 reshape.797
  78.2 7.5 %collective-permute-done.5 = bf16[256,1536]{0,1:T(8,128)(2,1)} collective-permute-done((bf16[256,1536]{0,1:T(8,128)(2,1)}, bf16[256,1536]{0,1:T(8,128)(2,1)}, u32[]{:S(2)}, u32[]{:S(2)}) %collective-permute-start.5) | collective-permute-done | bytes 786464 | tf_op jit(solution)/shard_map/ppermute | solution.py:241
  87.1 2.3 copy.104
  89.4 13.0 %collective-permute-done.4 = bf16[256,1536]{0,1:T(8,128)(2,1)} collective-permute-done((bf16[256,1536]{0,1:T(8,128)(2,1)}, bf16[256,1536]{0,1:T(8,128)(2,1)}, u32[]{:S(2)}, u32[]{:S(2)}) %collective-permute-start.4) | collective-permute-done | bytes 786464 | tf_op jit(solution)/shard_map/ppermute | solution.py:241
  103.7 2.3 copy.103
  106.0 2.3 copy.102
  108.3 2.2 constant_dynamic-update-slice_fusion.3
  110.5 2.1 constant_dynamic-update-slice_fusion.2
  118.0 5.4 fusion.4.q_ref.k_ref.v_ref
  123.4 24.8 %attend.1 = (bf16[1152,512]{1,0:T(8,128)(2,1)}, f32[4,2,1152]{2,1,0:T(2,128)}) custom-call(bf16[1152,1536]{1,0:T(8,128)(2,1)} %fusion.4.q_ref.k_ref.v_ref, bf16[1152,1536]{1,0:T(8,128)(2,1)} %fusion.4.q_ref.k_ref.v_ref, bf16[1152,1536]{1,0:T(8,128)(2,1)} %fusion.4.q_ref.k_ref.v_ref), custom_call_target="tpu_custom_call" | custom-call | flops 10871635968 | bytes 4718592 | tf_op jit(solution)/shard_map/attend/pallas_call | solution.py:132
  148.2 5.7 all-to-all-start.1
  155.0 2.5 broadcast_in_dim.106
  157.5 2.3 bitcast_dynamic-update-slice_fusion.3
  168.0 3.1 bitcast_dynamic-update-slice_fusion.2
  171.9 2.3 bitcast_dynamic-update-slice_fusion.1
  174.2 2.3 bitcast_dynamic-update-slice_fusion
  176.5 6.2 all-to-all-done.1
  182.8 3.5 maximum_select_fusion.2
  186.3 26.6 %collective-permute-done.9 = bf16[256,2048]{1,0:T(8,128)(2,1)} collective-permute-done((bf16[256,2048]{1,0:T(8,128)(2,1)}, bf16[256,2048]{1,0:T(8,128)(2,1)}, u32[]{:S(2)}, u32[]{:S(2)}) %collective-permute-start.9) | collective-permute-done | bytes 1048608 | tf_op jit(solution)/shard_map/ppermute | solution.py:241
  212.9 2.3 bitcast_dynamic-update-slice_fusion.6
  217.0 3.4 bitcast_add_fusion.3
  226.7 8.7 %multiply_convert_fusion = (bf16[1152,2048]{1,0:T(8,128)(2,1)}, f32[1152,2048]{1,0:T(8,128)}) fusion(f32[2048]{0:T(1024)S(1)} %bitcast.332, bf16[1152,1024]{1,0:T(8,128)(2,1)S(1)} %bitcast.307, bf16[1024,2048]{1,0:T(8,128)(2,1)S(1)} %bitcast.288), kind=kOutput, calls=%fused_computation.6 | convolution fusion | flops 4845993984 | bytes 20717568 | tf_op jit(solution)/shard_map/dot_general | solution.py:43
  235.4 11.8 %fusion.53 = (bf16[2048]{0:T(1024)(128)(2,1)}, bf16[1152,2048]{1,0:T(8,128)(2,1)S(1)}) fusion(f32[1152,2048]{1,0:T(8,128)} %get-tuple-element.130, bf16[1152,1024]{1,0:T(8,128)(2,1)S(1)} %bitcast.305, bf16[2048,1024]{1,0:T(8,128)(2,1)} %bitcast.44), kind=kOutput, calls=%fused_computation.192 | convolution fusion | flops 4857788416 | bytes 20713472 | tf_op jit(solution)/shard_map/dot_general | solution.py:43
  247.1 6.0 convolution_convert_fusion.1
  253.2 5.1 fusion.56
  258.5 8.1 %fusion.55 = f32[2,576,1024]{2,1,0:T(8,128)S(1)} fusion(bf16[2,576,2048]{2,1,0:T(8,128)(2,1)S(1)} %bitcast.342, bf16[2048,1024,1]{1,0,2:T(8,128)(2,1)} %bitcast.45), kind=kOutput, calls=%fused_computation.194 | convolution fusion | flops 4831838208 | bytes 13631488 | tf_op jit(solution)/shard_map/dot_general | solution.py:43
  267.4 6.0 convolution_convert_fusion
  273.5 1.9 dynamic-slice_bitcast_fusion.2
  282.9 2.0 multiply_reduce_fusion.2
  286.5 3.5 fusion.52
  290.0 12.2 %collective-permute-done.27 = bf16[512,1024]{1,0:T(8,128)(2,1)S(1)} collective-permute-done((bf16[512,1024]{1,0:T(8,128)(2,1)S(1)}, bf16[512,1024]{1,0:T(8,128)(2,1)S(1)}, u32[]{:S(2)}, u32[]{:S(2)}) %collective-permute-start.27) | collective-permute-done | bytes 1048608 | tf_op jit(solution)/shard_map/ppermute | solution.py:241
  303.8 4.1 convolution_convert_fusion.4
  307.9 3.5 reshape.761
  311.4 3.4 constant_dynamic-slice_fusion.9
  315.8 10.0 %collective-permute-done.29 = bf16[512,1024]{1,0:T(8,128)(2,1)} collective-permute-done((bf16[512,1024]{1,0:T(8,128)(2,1)}, bf16[512,1024]{1,0:T(8,128)(2,1)}, u32[]{:S(2)}, u32[]{:S(2)}) %collective-permute-start.29) | collective-permute-done | bytes 1048608 | tf_op jit(solution)/shard_map/ppermute | solution.py:241
  328.7 4.2 fusion.26
  333.1 2.5 maximum_select_fusion.5
  335.5 4.8 all-to-all-start.2
  340.4 6.8 %collective-permute-done.24 = bf16[256,2048]{1,0:T(8,128)(2,1)} collective-permute-done((bf16[256,2048]{1,0:T(8,128)(2,1)}, bf16[256,2048]{1,0:T(8,128)(2,1)}, u32[]{:S(2)}, u32[]{:S(2)}) %collective-permute-start.24) | collective-permute-done | bytes 1048608 | tf_op jit(solution)/shard_map/ppermute | solution.py:241
  347.2 22.7 %collective-permute-done.26 = bf16[256,2048]{1,0:T(8,128)(2,1)} collective-permute-done((bf16[256,2048]{1,0:T(8,128)(2,1)}, bf16[256,2048]{1,0:T(8,128)(2,1)}, u32[]{:S(2)}, u32[]{:S(2)}) %collective-permute-start.26) | collective-permute-done | bytes 1048608 | tf_op jit(solution)/shard_map/ppermute | solution.py:241
  371.5 3.9 fusion.29
  377.3 28.2 %all-reduce.8.cloned.1.call-done = bf16[512,1024]{1,0:T(8,128)(2,1)} async-done(((bf16[512,1024]{1,0:T(8,128)(2,1)}), bf16[512,1024]{1,0:T(8,128)(2,1)}) %all-reduce.8.cloned.1.call-update) | async-done | bytes 1048592 | tf_op jit(solution)/shard_map/psum | solution.py:370
  409.4 3.5 convolution_convert_fusion.3
  415.7 35.5 %attend_back.1 = (bf16[1152,1536]{1,0:T(8,128)(2,1)}, f32[4,2,128]{2,1,0:T(2,128)}) custom-call(bf16[1152,1536]{1,0:T(8,128)(2,1)} %fusion.4.q_ref.k_ref.v_ref, bf16[1152,1536]{1,0:T(8,128)(2,1)} %fusion.4.q_ref.k_ref.v_ref, bf16[1152,1536]{1,0:T(8,128)(2,1)} %fusion.4.q_ref.k_ref.v_ref, bf16[1152,512]{1,0:T(8,128)(2,1)} %get-tuple-element.24.out_ref, ...), custom_call_target="tpu_custom_call" | custom-call | flops 27179089920 | bytes 9437184 | tf_op jit(solution)/shard_map/attend_back/pallas_call | solution.py:161
  451.3 9.1 %multiply_reduce_fusion = (bf16[1024]{0:T(1024)(128)(2,1)S(1)}, bf16[1024]{0:T(1024)(128)(2,1)S(1)}, bf16[1152,1024]{1,0:T(8,128)(2,1)}, f32[1152,1024]{1,0:T(8,128)}) fusion(f32[1152]{0:T(1024)S(1)} %copy-done.43, f32[1152]{0:T(1024)S(1)} %copy-done.42, bf16[4,1,144,1024]{3,2,1,0:T(8,128)(2,1)S(1)} %bitcast.276, ...), kind=kOutput, calls=%fused_computation.16 | convolution fusion | flops 3645110272 | bytes 16143361 | tf_op jit(solution)/shard_map/dot_general | solution.py:43
  460.5 7.0 %convolution_convert_fusion.2 = bf16[1024,1536]{1,0:T(8,128)(2,1)S(1)} fusion(bf16[1152,1024]{1,0:T(8,128)(2,1)} %get-tuple-element.96, bf16[1152,1536]{1,0:T(8,128)(2,1)} %get-tuple-element.26), kind=kOutput, calls=%fused_computation.24 | convolution fusion | flops 3625451520 | bytes 9043968 | tf_op jit(solution)/shard_map/dot_general | solution.py:43
  474.1 2.9 fusion.36
  478.2 2.8 convert_element_type.381
  481.0 17.4 %collective-permute-done.21 = bf16[272,1536]{1,0:T(8,128)(2,1)} collective-permute-done((bf16[272,1536]{1,0:T(8,128)(2,1)}, bf16[272,1536]{1,0:T(8,128)(2,1)}, u32[]{:S(2)}, u32[]{:S(2)}) %collective-permute-start.21) | collective-permute-done | bytes 835616 | tf_op jit(solution)/shard_map/ppermute | solution.py:241
  498.5 17.9 %collective-permute-done.23 = bf16[272,1536]{1,0:T(8,128)(2,1)} collective-permute-done((bf16[272,1536]{1,0:T(8,128)(2,1)}, bf16[272,1536]{1,0:T(8,128)(2,1)}, u32[]{:S(2)}, u32[]{:S(2)}) %collective-permute-start.23) | collective-permute-done | bytes 835616 | tf_op jit(solution)/shard_map/ppermute | solution.py:241
  517.7 2.3 fusion.32
  520.1 3.3 fusion.14
  523.4 4.3 all-to-all-start.3
  531.8 42.1 %all-reduce.12.cloned.1.call-done = bf16[144,1024]{1,0:T(8,128)(2,1)} async-done(((bf16[144,1024]{1,0:T(8,128)(2,1)}), bf16[144,1024]{1,0:T(8,128)(2,1)}) %all-reduce.12.cloned.1.call-update) | async-done | bytes 294928 | tf_op jit(solution)/shard_map/psum | solution.py:374
  580.0 1.8 copy.122
  581.8 2.9 copy.124
  584.7 36.7 %all-reduce.14.cloned.1.call-done = bf16[272,1536]{1,0:T(8,128)(2,1)} async-done(((bf16[272,1536]{1,0:T(8,128)(2,1)}), bf16[272,1536]{1,0:T(8,128)(2,1)}) %all-reduce.14.cloned.1.call-update) | async-done | bytes 835600 | tf_op jit(solution)/shard_map/psum | solution.py:428
  629.6 2.2 dynamic-slice_bitcast_fusion.10
  636.7 3.0 copy.123
  646.1 4.1 fusion.13
  (325 shorter events, 115.3 us)
Async XLA Ops:
  8.6 2.2 collective-permute-start
  10.8 7.6 %copy-start.25 = (bf16[128,3072]{1,0:T(8,128)(2,1)S(1)}, bf16[128,3072]{1,0:T(8,128)(2,1)}, u32[]{:S(2)}) copy-start(bf16[128,3072]{1,0:T(8,128)(2,1)} %param.15) | copy-start | bytes 2359300
  12.0 59.2 %all-to-all-start = ((bf16[4,144,1024]{2,1,0:T(8,128)(2,1)}), bf16[4,144,1024]{2,1,0:T(8,128)(2,1)S(1)}, u32[]{:S(2)}, u32[]{:S(2)}) async-start(bf16[4,144,1024]{2,1,0:T(8,128)(2,1)} %bitcast.3), calls=%async_computation | async-start | bytes 2359296 | tf_op jit(solution)/shard_map/all_to_all | solution.py:275
  18.3 198.7 %all-gather.4.cloned.1.call-start = ((), (), s32[]{:S(2)}) async-start(), calls=%async_computation.5 | async-start | bytes 2359296 | tf_op jit(solution)/shard_map/all_gather | solution.py:282
  19.0 39.1 %collective-permute-start.2 = (bf16[128,3,512]{2,0,1:T(8,128)(2,1)S(1)}, bf16[128,3,512]{2,0,1:T(8,128)(2,1)S(1)}, u32[]{:S(2)}, u32[]{:S(2)}) collective-permute-start(bf16[128,3,512]{2,0,1:T(8,128)(2,1)S(1)} %bitcast.325), channel_id=1, source_target_pairs={{0,4},{4,0},{8,12},{12,8},{16,20},{20,16},{24,28},{28,24},{1,5},{5... | collective-permute-start | bytes 1179656 | tf_op jit(solution)/shard_map/ppermute | solution.py:230
  19.1 148.4 %collective-permute-start.12 = (bf16[512,1024]{1,0:T(8,128)(2,1)}, bf16[512,1024]{1,0:T(8,128)(2,1)}, u32[]{:S(2)}, u32[]{:S(2)}) collective-permute-start(bf16[512,1024]{1,0:T(8,128)(2,1)} %param.25), channel_id=1, source_target_pairs={{0,8},{4,12},{8,0},{12,4},{16,24},{20,28},{24,16},{28,20},{1,9},{5... | collective-permute-start | bytes 3145736 | tf_op jit(solution)/shard_map/ppermute | solution.py:241
  61.8 9.3 %copy-start.33 = (bf16[8,1,1536]{2,0,1:T(8,128)(2,1)S(1)}, bf16[8,1,1536]{2,0,1:T(8,128)(2,1)}, u32[]{:S(2)}) copy-start(bf16[8,1,1536]{2,0,1:T(8,128)(2,1)} %copy-done.32) | copy-start | bytes 73732
  64.0 21.7 %collective-permute-start.5 = (bf16[256,1536]{0,1:T(8,128)(2,1)}, bf16[256,1536]{0,1:T(8,128)(2,1)}, u32[]{:S(2)}, u32[]{:S(2)}) collective-permute-start(bf16[256,1536]{0,1:T(8,128)(2,1)} %bitcast.267), channel_id=1, source_target_pairs={{0,24},{4,28},{8,16},{12,20},{16,8},{20,12},{24,0},{28,4},{1,25},{... | collective-permute-start | bytes 2359304 | tf_op jit(solution)/shard_map/ppermute | solution.py:241
  65.4 37.0 %collective-permute-start.4 = (bf16[256,1536]{0,1:T(8,128)(2,1)}, bf16[256,1536]{0,1:T(8,128)(2,1)}, u32[]{:S(2)}, u32[]{:S(2)}) collective-permute-start(bf16[256,1536]{0,1:T(8,128)(2,1)} %bitcast.267), channel_id=1, source_target_pairs={{0,16},{4,20},{8,24},{12,28},{16,0},{20,4},{24,8},{28,12},{1,17},{... | collective-permute-start | bytes 2359304 | tf_op jit(solution)/shard_map/ppermute | solution.py:241
  66.7 39.3 %collective-permute-start.3 = (bf16[256,1536]{0,1:T(8,128)(2,1)}, bf16[256,1536]{0,1:T(8,128)(2,1)}, u32[]{:S(2)}, u32[]{:S(2)}) collective-permute-start(bf16[256,1536]{0,1:T(8,128)(2,1)} %bitcast.267), channel_id=1, source_target_pairs={{0,8},{4,12},{8,0},{12,4},{16,24},{20,28},{24,16},{28,20},{1,9},{5... | collective-permute-start | bytes 2359304 | tf_op jit(solution)/shard_map/ppermute | solution.py:241
  71.2 45.0 %copy-start.1 = (bf16[4,144,1024]{2,1,0:T(8,128)(2,1)}, bf16[4,144,1024]{2,1,0:T(8,128)(2,1)S(1)}, u32[]{:S(2)}) copy-start(bf16[4,144,1024]{2,1,0:T(8,128)(2,1)S(1)} %all-to-all-done) | copy-start | bytes 3538948
  71.2 42.5 %collective-permute-start.1 = (bf16[4,144,1024]{2,1,0:T(8,128)(2,1)S(1)}, bf16[4,144,1024]{2,1,0:T(8,128)(2,1)S(1)}, u32[]{:S(2)}, u32[]{:S(2)}) collective-permute-start(bf16[4,144,1024]{2,1,0:T(8,128)(2,1)S(1)} %all-to-all-done), channel_id=1, source_target_pairs={{0,4},{4,0},{8,12},{12,8},{16,20},{20,16},{24,28},{28,24},{1,5},{5... | collective-permute-start | bytes 3538952 | tf_op jit(solution)/shard_map/ppermute | solution.py:230
  71.9 44.3 %copy-start.29 = (f32[1024]{0:T(1024)}, f32[1024]{0:T(1024)S(1)}, u32[]{:S(2)}) copy-start(f32[1024]{0:T(1024)S(1)} %get-tuple-element.119) | copy-start | bytes 12292
  85.6 88.6 %collective-permute-start.14 = (bf16[512,1024]{1,0:T(8,128)(2,1)}, bf16[512,1024]{1,0:T(8,128)(2,1)}, u32[]{:S(2)}, u32[]{:S(2)}) collective-permute-start(bf16[512,1024]{1,0:T(8,128)(2,1)} %param.25), channel_id=1, source_target_pairs={{0,24},{4,28},{8,16},{12,20},{16,8},{20,12},{24,0},{28,4},{1,25},{... | collective-permute-start | bytes 3145736 | tf_op jit(solution)/shard_map/ppermute | solution.py:241
  102.4 68.7 %collective-permute-start.13 = (bf16[512,1024]{1,0:T(8,128)(2,1)}, bf16[512,1024]{1,0:T(8,128)(2,1)}, u32[]{:S(2)}, u32[]{:S(2)}) collective-permute-start(bf16[512,1024]{1,0:T(8,128)(2,1)} %param.25), channel_id=1, source_target_pairs={{0,16},{4,20},{8,24},{12,28},{16,0},{20,4},{24,8},{28,12},{1,17},{... | collective-permute-start | bytes 3145736 | tf_op jit(solution)/shard_map/ppermute | solution.py:241
  106.0 54.4 %collective-permute-start.8 = (bf16[128,4,512]{2,0,1:T(8,128)(2,1)}, bf16[128,4,512]{2,0,1:T(8,128)(2,1)}, u32[]{:S(2)}, u32[]{:S(2)}) collective-permute-start(bf16[128,4,512]{2,0,1:T(8,128)(2,1)} %bitcast.32), channel_id=1, source_target_pairs={{0,4},{4,0},{8,12},{12,8},{16,20},{20,16},{24,28},{28,24},{1,5},{5... | collective-permute-start | bytes 1572872 | tf_op jit(solution)/shard_map/ppermute | solution.py:230
  113.7 69.1 %collective-permute-start.16 = (bf16[576,1024]{1,0:T(8,128)(2,1)S(1)}, bf16[576,1024]{1,0:T(8,128)(2,1)}, u32[]{:S(2)}, u32[]{:S(2)}) collective-permute-start(bf16[576,1024]{1,0:T(8,128)(2,1)S(1)} %bitcast.277), channel_id=1, source_target_pairs={{0,4},{4,0},{8,12},{12,8},{16,20},{20,16},{24,28},{28,24},{1,5},{5... | collective-permute-start | bytes 3538952 | tf_op jit(solution)/shard_map/ppermute | solution.py:230
  148.2 34.4 %all-to-all-start.1 = ((bf16[4,288,512]{2,1,0:T(8,128)(2,1)}), bf16[4,288,512]{2,1,0:T(8,128)(2,1)S(1)}, u32[]{:S(2)}, u32[]{:S(2)}) async-start(bf16[4,288,512]{2,1,0:T(8,128)(2,1)} %bitcast.316), calls=%async_computation.1 | async-start | bytes 2359296 | tf_op jit(solution)/shard_map/all_to_all | solution.py:303
  153.9 251.5 %all-reduce.8.cloned.1.call-start = ((), (), s32[]{:S(2)}) async-start(), calls=%async_computation.7 | async-start | bytes 2097152 | tf_op jit(solution)/shard_map/psum | solution.py:370
  165.5 58.7 %collective-permute-start.11 = (bf16[256,2048]{1,0:T(8,128)(2,1)}, bf16[256,2048]{1,0:T(8,128)(2,1)}, u32[]{:S(2)}, u32[]{:S(2)}) collective-permute-start(bf16[256,2048]{1,0:T(8,128)(2,1)} %bitcast.140), channel_id=1, source_target_pairs={{0,24},{4,28},{8,16},{12,20},{16,8},{20,12},{24,0},{28,4},{1,25},{... | collective-permute-start | bytes 3145736 | tf_op jit(solution)/shard_map/ppermute | solution.py:241
  167.4 6.8 %copy-start.10 = (bf16[4,256,2048]{2,1,0:T(8,128)(2,1)}, bf16[4,256,2048]{2,1,0:T(8,128)(2,1)S(1)}, u32[]{:S(2)}) copy-start(bf16[4,256,2048]{2,1,0:T(8,128)(2,1)S(1)} %constant_dynamic-update-slice_fusion) | copy-start | bytes 12582916
  167.5 45.5 %collective-permute-start.9 = (bf16[256,2048]{1,0:T(8,128)(2,1)}, bf16[256,2048]{1,0:T(8,128)(2,1)}, u32[]{:S(2)}, u32[]{:S(2)}) collective-permute-start(bf16[256,2048]{1,0:T(8,128)(2,1)} %bitcast.140), channel_id=1, source_target_pairs={{0,8},{4,12},{8,0},{12,4},{16,24},{20,28},{24,16},{28,20},{1,9},{5... | collective-permute-start | bytes 3145736 | tf_op jit(solution)/shard_map/ppermute | solution.py:241
  171.1 50.6 %collective-permute-start.10 = (bf16[256,2048]{1,0:T(8,128)(2,1)}, bf16[256,2048]{1,0:T(8,128)(2,1)}, u32[]{:S(2)}, u32[]{:S(2)}) collective-permute-start(bf16[256,2048]{1,0:T(8,128)(2,1)} %bitcast.140), channel_id=1, source_target_pairs={{0,16},{4,20},{8,24},{12,28},{16,0},{20,4},{24,8},{28,12},{1,17},{... | collective-permute-start | bytes 3145736 | tf_op jit(solution)/shard_map/ppermute | solution.py:241
  182.7 32.5 %collective-permute-start.6 = (bf16[2,1,288,512]{3,2,0,1:T(8,128)(2,1)S(1)}, bf16[2,1,288,512]{3,2,0,1:T(8,128)(2,1)S(1)}, u32[]{:S(2)}, u32[]{:S(2)}) collective-permute-start(bf16[2,1,288,512]{3,2,0,1:T(8,128)(2,1)S(1)} %get-tuple-element.103), channel_id=1, source_target_pairs={{0,4},{4,0},{8,12},{12,8},{16,20},{20,16},{24,28},{28,24},{1,5},{5... | collective-permute-start | bytes 1769480 | tf_op jit(solution)/shard_map/ppermute | solution.py:230
  221.6 4.4 collective-permute-start.7
  226.7 8.7 %copy-start.17 = (bf16[2,576,1024]{2,1,0:T(8,128)(2,1)S(1)}, bf16[2,576,1024]{2,1,0:T(8,128)(2,1)}, u32[]{:S(2)}) copy-start(bf16[2,576,1024]{2,1,0:T(8,128)(2,1)} %maximum_select_fusion.2) | copy-start | bytes 7077892
  247.1 11.4 %slice-start = ((s8[4718592]{0:T(1024)(128)(4,1)}), s8[524288]{0:T(1024)(128)(4,1)S(1)}, s32[]{:S(2)}) async-start(s8[4718592]{0:T(1024)(128)(4,1)} %bitcast.340), calls=%async_computation.11 | async-start | bytes 1048576
  253.2 26.4 %copy-start.12 = (bf16[1024,2048]{1,0:T(8,128)(2,1)}, bf16[1024,2048]{1,0:T(8,128)(2,1)S(1)}, u32[]{:S(2)}) copy-start(bf16[1024,2048]{1,0:T(8,128)(2,1)S(1)} %convolution_convert_fusion.1) | copy-start | bytes 12582916
  266.9 18.0 %collective-permute-start.15 = (bf16[576,1024]{1,0:T(8,128)(2,1)S(1)}, bf16[576,1024]{1,0:T(8,128)(2,1)S(1)}, u32[]{:S(2)}, u32[]{:S(2)}) collective-permute-start(bf16[576,1024]{1,0:T(8,128)(2,1)S(1)} %fusion.34), channel_id=1, source_target_pairs={{0,4},{4,0},{8,12},{12,8},{16,20},{20,16},{24,28},{28,24},{1,5},{5... | collective-permute-start | bytes 3538952 | tf_op jit(solution)/shard_map/ppermute | solution.py:230
  266.9 14.4 %collective-permute-start.17 = (bf16[576,1024]{1,0:T(8,128)(2,1)S(1)}, bf16[576,1024]{1,0:T(8,128)(2,1)S(1)}, u32[]{:S(2)}, u32[]{:S(2)}) collective-permute-start(bf16[576,1024]{1,0:T(8,128)(2,1)S(1)} %fusion.35), channel_id=1, source_target_pairs={{0,4},{4,0},{8,12},{12,8},{16,20},{20,16},{24,28},{28,24},{1,5},{5... | collective-permute-start | bytes 3538952 | tf_op jit(solution)/shard_map/ppermute | solution.py:230
  276.1 26.0 %collective-permute-start.27 = (bf16[512,1024]{1,0:T(8,128)(2,1)S(1)}, bf16[512,1024]{1,0:T(8,128)(2,1)S(1)}, u32[]{:S(2)}, u32[]{:S(2)}) collective-permute-start(bf16[512,1024]{1,0:T(8,128)(2,1)S(1)} %get-tuple-element.87), channel_id=1, source_target_pairs={{0,8},{4,12},{8,0},{12,4},{16,24},{20,28},{24,16},{28,20},{1,9},{5... | collective-permute-start | bytes 3145736 | tf_op jit(solution)/shard_map/ppermute | solution.py:241
  277.7 48.1 %collective-permute-start.29 = (bf16[512,1024]{1,0:T(8,128)(2,1)}, bf16[512,1024]{1,0:T(8,128)(2,1)}, u32[]{:S(2)}, u32[]{:S(2)}) collective-permute-start(bf16[512,1024]{1,0:T(8,128)(2,1)} %get-tuple-element.88), channel_id=1, source_target_pairs={{0,24},{4,28},{8,16},{12,20},{16,8},{20,12},{24,0},{28,4},{1,25},{... | collective-permute-start | bytes 3145736 | tf_op jit(solution)/shard_map/ppermute | solution.py:241
  279.2 49.5 %collective-permute-start.28 = (bf16[512,1024]{1,0:T(8,128)(2,1)}, bf16[512,1024]{1,0:T(8,128)(2,1)}, u32[]{:S(2)}, u32[]{:S(2)}) collective-permute-start(bf16[512,1024]{1,0:T(8,128)(2,1)} %get-tuple-element.89), channel_id=1, source_target_pairs={{0,16},{4,20},{8,24},{12,28},{16,0},{20,4},{24,8},{28,12},{1,17},{... | collective-permute-start | bytes 3145736 | tf_op jit(solution)/shard_map/ppermute | solution.py:241
  281.3 65.9 %collective-permute-start.24 = (bf16[256,2048]{1,0:T(8,128)(2,1)}, bf16[256,2048]{1,0:T(8,128)(2,1)}, u32[]{:S(2)}, u32[]{:S(2)}) collective-permute-start(bf16[256,2048]{1,0:T(8,128)(2,1)} %get-tuple-element.90), channel_id=1, source_target_pairs={{0,8},{4,12},{8,0},{12,4},{16,24},{20,28},{24,16},{28,20},{1,9},{5... | collective-permute-start | bytes 3145736 | tf_op jit(solution)/shard_map/ppermute | solution.py:241
  284.9 85.1 %collective-permute-start.26 = (bf16[256,2048]{1,0:T(8,128)(2,1)}, bf16[256,2048]{1,0:T(8,128)(2,1)}, u32[]{:S(2)}, u32[]{:S(2)}) collective-permute-start(bf16[256,2048]{1,0:T(8,128)(2,1)} %get-tuple-element.91), channel_id=1, source_target_pairs={{0,24},{4,28},{8,16},{12,20},{16,8},{20,12},{24,0},{28,4},{1,25},{... | collective-permute-start | bytes 3145736 | tf_op jit(solution)/shard_map/ppermute | solution.py:241
  286.5 17.3 %copy-start.55 = (bf16[1024,1024]{1,0:T(8,128)(2,1)S(1)}, bf16[1024,1024]{1,0:T(8,128)(2,1)}, u32[]{:S(2)}) copy-start(bf16[1024,1024]{1,0:T(8,128)(2,1)} %all-gather.4.cloned.1.call-done) | copy-start | bytes 6291460
  302.1 69.4 %collective-permute-start.25 = (bf16[256,2048]{1,0:T(8,128)(2,1)}, bf16[256,2048]{1,0:T(8,128)(2,1)}, u32[]{:S(2)}, u32[]{:S(2)}) collective-permute-start(bf16[256,2048]{1,0:T(8,128)(2,1)} %get-tuple-element.92), channel_id=1, source_target_pairs={{0,16},{4,20},{8,24},{12,28},{16,0},{20,4},{24,8},{28,12},{1,17},{... | collective-permute-start | bytes 3145736 | tf_op jit(solution)/shard_map/ppermute | solution.py:241
  314.8 13.1 %copy-start.35 = (f32[4,2,144]{2,1,0:T(2,128)S(1)}, f32[4,2,144]{2,1,0:T(2,128)}, u32[]{:S(2)}) copy-start(f32[4,2,144]{2,1,0:T(2,128)} %copy-done.34) | copy-start | bytes 13828
  314.8 13.8 %copy-start.45 = (bf16[2048]{0:T(1024)(128)(2,1)S(1)}, bf16[2048]{0:T(1024)(128)(2,1)}, u32[]{:S(2)}) copy-start(bf16[2048]{0:T(1024)(128)(2,1)} %get-tuple-element.85) | copy-start | bytes 12292
  325.8 7.2 %collective-permute-start.18 = (bf16[2,288,1,512]{3,1,0,2:T(8,128)(2,1)}, bf16[2,288,1,512]{3,1,0,2:T(8,128)(2,1)}, u32[]{:S(2)}, u32[]{:S(2)}) collective-permute-start(bf16[2,288,1,512]{3,1,0,2:T(8,128)(2,1)} %bitcast.268), channel_id=1, source_target_pairs={{0,4},{4,0},{8,12},{12,8},{16,20},{20,16},{24,28},{28,24},{1,5},{5... | collective-permute-start | bytes 1769480 | tf_op jit(solution)/shard_map/ppermute | solution.py:230
  335.5 79.1 %all-to-all-start.2 = ((bf16[4,288,512]{2,1,0:T(8,128)(2,1)}), bf16[4,288,512]{2,1,0:T(8,128)(2,1)S(1)}, u32[]{:S(2)}, u32[]{:S(2)}) async-start(bf16[4,288,512]{2,1,0:T(8,128)(2,1)} %bitcast.61), calls=%async_computation.2 | async-start | bytes 2359296 | tf_op jit(solution)/shard_map/all_to_all | solution.py:341
  340.3 36.4 %copy-start.40 = (bf16[1024]{0:T(1024)(128)(2,1)S(1)}, bf16[1024]{0:T(1024)(128)(2,1)}, u32[]{:S(2)}) copy-start(bf16[1024]{0:T(1024)(128)(2,1)} %get-tuple-element.76) | copy-start | bytes 6148
  340.3 69.1 %copy-start.21 = (bf16[72,8,2,512]{3,1,2,0:T(8,128)(2,1)S(1)}, bf16[72,8,2,512]{3,1,2,0:T(8,128)(2,1)}, u32[]{:S(2)}) copy-start(bf16[72,8,2,512]{3,1,2,0:T(8,128)(2,1)} %copy-done.20) | copy-start | bytes 3538948
  340.3 187.4 %all-reduce.10.cloned.1.call-start = ((), (), s32[]{:S(2)}) async-start(), calls=%async_computation.8 | async-start | bytes 2097152 | tf_op jit(solution)/shard_map/psum | solution.py:372
  405.5 122.3 %reduce-scatter.2.cloned.1.call-start = ((), (), s32[]{:S(2)}) async-start(), calls=%async_computation.6 | async-start | bytes 2654208 | tf_op jit(solution)/shard_map/reduce_scatter | solution.py:369
  415.7 35.5 %copy-start.2 = (bf16[4,144,1024]{2,1,0:T(8,128)(2,1)S(1)}, bf16[4,144,1024]{2,1,0:T(8,128)(2,1)}, u32[]{:S(2)}) copy-start(bf16[4,144,1024]{2,1,0:T(8,128)(2,1)} %copy-done.1) | copy-start | bytes 3538948
  415.7 35.5 %copy-start.6 = (bf16[4,144,1024]{2,1,0:T(8,128)(2,1)S(1)}, bf16[4,144,1024]{2,1,0:T(8,128)(2,1)}, u32[]{:S(2)}) copy-start(bf16[4,144,1024]{2,1,0:T(8,128)(2,1)} %copy-done.5) | copy-start | bytes 3538948
  415.7 35.6 %copy-start.30 = (f32[1024]{0:T(1024)S(1)}, f32[1024]{0:T(1024)}, u32[]{:S(2)}) copy-start(f32[1024]{0:T(1024)} %copy-done.29) | copy-start | bytes 12292
  415.7 35.6 %copy-start.38 = (f32[1024]{0:T(1024)S(1)}, f32[1024]{0:T(1024)}, u32[]{:S(2)}) copy-start(f32[1024]{0:T(1024)} %get-tuple-element.118) | copy-start | bytes 12292
  415.7 35.6 %copy-start.42 = (f32[1152]{0:T(1024)S(1)}, f32[1152]{0:T(1024)}, u32[]{:S(2)}) copy-start(f32[1152]{0:T(1024)} %div.62) | copy-start | bytes 13828
  415.7 35.6 %copy-start.43 = (f32[1152]{0:T(1024)S(1)}, f32[1152]{0:T(1024)}, u32[]{:S(2)}) copy-start(f32[1152]{0:T(1024)} %rsqrt.37) | copy-start | bytes 13828
  451.3 9.1 %copy-start.46 = (f32[4,2,128]{2,1,0:T(2,128)S(1)}, f32[4,2,128]{2,1,0:T(2,128)}, u32[]{:S(2)}) copy-start(f32[4,2,128]{2,1,0:T(2,128)} %get-tuple-element.27) | copy-start | bytes 12292
  470.4 28.1 %collective-permute-start.21 = (bf16[272,1536]{1,0:T(8,128)(2,1)}, bf16[272,1536]{1,0:T(8,128)(2,1)}, u32[]{:S(2)}, u32[]{:S(2)}) collective-permute-start(bf16[272,1536]{1,0:T(8,128)(2,1)} %get-tuple-element.93), channel_id=1, source_target_pairs={{0,8},{4,12},{8,0},{12,4},{16,24},{20,28},{24,16},{28,20},{1,9},{5... | collective-permute-start | bytes 2506760 | tf_op jit(solution)/shard_map/ppermute | solution.py:241
  471.8 44.5 %collective-permute-start.23 = (bf16[272,1536]{1,0:T(8,128)(2,1)}, bf16[272,1536]{1,0:T(8,128)(2,1)}, u32[]{:S(2)}, u32[]{:S(2)}) collective-permute-start(bf16[272,1536]{1,0:T(8,128)(2,1)} %get-tuple-element.94), channel_id=1, source_target_pairs={{0,24},{4,28},{8,16},{12,20},{16,8},{20,12},{24,0},{28,4},{1,25},{... | collective-permute-start | bytes 2506760 | tf_op jit(solution)/shard_map/ppermute | solution.py:241
  473.3 44.4 %collective-permute-start.22 = (bf16[272,1536]{1,0:T(8,128)(2,1)}, bf16[272,1536]{1,0:T(8,128)(2,1)}, u32[]{:S(2)}, u32[]{:S(2)}) collective-permute-start(bf16[272,1536]{1,0:T(8,128)(2,1)} %get-tuple-element.95), channel_id=1, source_target_pairs={{0,16},{4,20},{8,24},{12,28},{16,0},{20,4},{24,8},{28,12},{1,17},{... | collective-permute-start | bytes 2506760 | tf_op jit(solution)/shard_map/ppermute | solution.py:241
  477.0 43.1 %collective-permute-start.19 = (bf16[4,144,1024]{2,1,0:T(8,128)(2,1)}, bf16[4,144,1024]{2,1,0:T(8,128)(2,1)S(1)}, u32[]{:S(2)}, u32[]{:S(2)}) collective-permute-start(bf16[4,144,1024]{2,1,0:T(8,128)(2,1)} %fusion.36), channel_id=1, source_target_pairs={{0,4},{4,0},{8,12},{12,8},{16,20},{20,16},{24,28},{28,24},{1,5},{5... | collective-permute-start | bytes 3538952 | tf_op jit(solution)/shard_map/ppermute | solution.py:230
  523.4 106.2 %all-to-all-start.3 = ((bf16[4,144,1024]{2,1,0:T(8,128)(2,1)}), bf16[4,144,1024]{2,1,0:T(8,128)(2,1)}, u32[]{:S(2)}, u32[]{:S(2)}) async-start(bf16[4,144,1024]{2,1,0:T(8,128)(2,1)} %fusion.14), calls=%async_computation.3 | async-start | bytes 2359296 | tf_op jit(solution)/shard_map/all_to_all | solution.py:384
  527.7 46.2 %all-reduce.12.cloned.1.call-start = ((), (), s32[]{:S(2)}) async-start(), calls=%async_computation.9 | async-start | bytes 589824 | tf_op jit(solution)/shard_map/psum | solution.py:374
  528.3 93.2 %all-reduce.14.cloned.1.call-start = ((), (), s32[]{:S(2)}) async-start(), calls=%async_computation.10 | async-start | bytes 1671168 | tf_op jit(solution)/shard_map/psum | solution.py:428
  531.7 45.8 %collective-permute-start.32 = (bf16[128,4,512]{2,0,1:T(8,128)(2,1)S(1)}, bf16[128,4,512]{2,0,1:T(8,128)(2,1)S(1)}, u32[]{:S(2)}, u32[]{:S(2)}) collective-permute-start(bf16[128,4,512]{2,0,1:T(8,128)(2,1)S(1)} %bitcast.322), channel_id=1, source_target_pairs={{0,4},{4,0},{8,12},{12,8},{16,20},{20,16},{24,28},{28,24},{1,5},{5... | collective-permute-start | bytes 1572872 | tf_op jit(solution)/shard_map/ppermute | solution.py:230
  622.8 6.0 collective-permute-start.31
  628.2 4.8 collective-permute-start.30
  631.8 7.9 %copy-start.7 = (bf16[2,1,144,1024]{3,2,1,0:T(8,128)(2,1)}, bf16[2,1,144,1024]{3,2,1,0:T(8,128)(2,1)S(1)}, u32[]{:S(2)}) copy-start(bf16[2,1,144,1024]{3,2,1,0:T(8,128)(2,1)S(1)} %get-tuple-element.98) | copy-start | bytes 1769476
  631.8 7.8 %collective-permute-start.20 = (bf16[2,144,1024]{2,1,0:T(8,128)(2,1)}, bf16[2,144,1024]{2,1,0:T(8,128)(2,1)}, u32[]{:S(2)}, u32[]{:S(2)}) collective-permute-start(bf16[2,144,1024]{2,1,0:T(8,128)(2,1)} %get-tuple-element.99), channel_id=1, source_target_pairs={{0,4},{4,0},{8,12},{12,8},{16,20},{20,16},{24,28},{28,24},{1,5},{5... | collective-permute-start | bytes 1769480 | tf_op jit(solution)/shard_map/ppermute | solution.py:230
  (37 other events, 95.3 us)
Sparse Core Ops, SparseCore 0:
  21.0 33.9 all-gather.3
  333.0 72.3 all-reduce.7
  407.8 51.1 all-reduce.9
  462.2 65.4 reduce-scatter.1
  530.5 43.2 all-reduce.11
  576.1 45.3 all-reduce.13

commit v2 on v1

--- a/solution.py
+++ b/solution.py
@@ -190,6 +190,455 @@
         ),
         name="attend_back",
     )(projected, projected, projected, attended, grad, log_total)
+
+
+class Copies:
+    def __init__(self, send_sems, recv_sems, local_sems):
+        self.send_sems, self.recv_sems, self.local_sems = send_sems, recv_sems, local_sems
+        self.sent, self.locals, self.local_count = [], [], 0
+
+    def remote(self, src, dst, **device):
+        at = len(self.sent)
+        copy = pltpu.make_async_remote_copy(
+            src_ref=src,
+            dst_ref=dst,
+            send_sem=self.send_sems.at[at],
+            recv_sem=self.recv_sems.at[at],
+            device_id=device,
+            device_id_type=pl.DeviceIdType.MESH,
+        )
+        copy.start()
+        self.sent.append(copy)
+        return copy
+
+    def local(self, src, dst):
+        copy = pltpu.make_async_copy(src, dst, self.local_sems.at[self.local_count])
+        copy.start()
+        self.locals.append(copy)
+        self.local_count += 1
+        return copy
+
+    def wait_local(self, copy):
+        copy.wait()
+        self.locals = [kept for kept in self.locals if kept is not copy]
+
+    def finish(self):
+        for copy in self.sent:
+            copy.wait_send()
+        for copy in self.locals:
+            copy.wait()
+
+
+class Place:
+    def __init__(self, items):
+        self.dp_ways, self.seq_ways = lax.axis_size("dp"), lax.axis_size("seq")
+        self.chips = self.dp_ways // 2
+        self.ranks = self.seq_ways // (2 * items)
+        self.dp, self.seq = lax.axis_index("dp"), lax.axis_index("seq")
+        self.core, self.chip = lax.rem(self.dp, 2), lax.div(self.dp, 2)
+        self.rank = lax.rem(self.seq, self.ranks)
+        self.item = lax.div(self.seq, self.ranks)
+
+    def partner(self, offset):
+        if self.chips == 4:
+            x, y = lax.rem(self.chip, 2), lax.div(self.chip, 2)
+            x = 1 - x if offset % 2 else x
+            y = 1 - y if offset >= 2 else y
+            return y * 2 + x
+        return lax.rem(self.chip + offset, self.chips)
+
+    def source(self, offset):
+        if self.chips == 4:
+            return self.partner(offset)
+        return lax.rem(self.chip + self.chips - offset, self.chips)
+
+    def meet(self):
+        barrier = pltpu.get_barrier_semaphore()
+        for step in range(1, self.dp_ways):
+            pl.semaphore_signal(
+                barrier,
+                inc=1,
+                device_id={"dp": lax.rem(self.dp + step, self.dp_ways)},
+                device_id_type=pl.DeviceIdType.MESH,
+            )
+        for step in range(1, self.seq_ways):
+            for core in range(2):
+                pl.semaphore_signal(
+                    barrier,
+                    inc=1,
+                    device_id={
+                        "dp": self.chip * 2 + core,
+                        "seq": lax.rem(self.seq + step, self.seq_ways),
+                    },
+                    device_id_type=pl.DeviceIdType.MESH,
+                )
+        pl.semaphore_wait(barrier, self.dp_ways - 1 + 2 * (self.seq_ways - 1))
+
+
+def rows_at(start, size):
+    return pl.ds(pl.multiple_of(start, 16), size)
+
+
+def lanes_at(start, size):
+    return pl.ds(pl.multiple_of(start, LANES), size)
+
+
+def attend_rows(prj, out, lse, v_flip, pair, block, rows):
+    pairs = out.shape[1] // LANES
+    query = prj[rows_at(block * rows, rows), lanes_at(pair * LANES, LANES)]
+    query = query * jnp.asarray(HEAD_DIM**-0.5, bf16)
+    key = prj[:, lanes_at((pairs + pair) * LANES, LANES)]
+    pieces = []
+    for head, mask in enumerate(pair_masks()):
+        scores = dot(key, jnp.where(mask, query, jnp.zeros_like(query)), 1, 1)
+        peak = jnp.max(scores, axis=0, keepdims=True)
+        lifted = jnp.exp(scores - peak)
+        total = jnp.sum(lifted, axis=0, keepdims=True)
+        probs = (lifted * (1.0 / total)).astype(bf16)
+        pieces.append(dot(v_flip[head * HEAD_DIM : (head + 1) * HEAD_DIM, :], probs))
+        lse[pair, head : head + 1, lanes_at(block * rows, rows)] = peak + jnp.log(total)
+    out[rows_at(block * rows, rows), lanes_at(pair * LANES, LANES)] = (
+        jnp.concatenate(pieces, axis=0).T.astype(bf16)
+    )
+
+
+def forward_kernel(
+    items,
+    img,
+    wq,
+    wp,
+    w1,
+    w2,
+    cot,
+    small,
+    img_out,
+    wq_out,
+    wp_out,
+    w1_out,
+    w2_out,
+    cot_out,
+    small_out,
+    prj_out,
+    heads_out,
+    lse_out,
+    rows_out,
+    img_v,
+    wq_v,
+    prj_v,
+    heads_v,
+    small_v,
+    vec_v,
+    v_flip,
+    send_sems,
+    recv_sems,
+    local_sems,
+    swap_sems,
+    token_send,
+    token_recv,
+    back_send,
+    back_recv,
+):
+    at = Place(items)
+    chips, ranks, seq_ways, dp_ways = at.chips, at.ranks, at.seq_ways, at.dp_ways
+    tokens = img.shape[0] // items
+    half = tokens // 2
+    shard, width = wp.shape
+    head_cols = heads_v.shape[1]
+    unit_rows = w2.shape[0]
+    length = img_v.shape[0]
+    pairs = head_cols // LANES
+    relay = chips == 4
+    offsets = (1, 2) if relay else tuple(range(1, chips))
+    copies = Copies(send_sems, recv_sems, local_sems)
+    at.meet()
+    me = rows_at(at.dp * shard, shard)
+
+    token_jobs = []
+    for item in range(items):
+        for k in range(ranks):
+            for h in range(2):
+                to_seq = (at.core * items + item) * ranks + k
+                mine = (to_seq == at.seq) & (at.core == h)
+                src = img.at[pl.ds(item * tokens + h * half, half), :]
+                dst = img_v.at[rows_at(at.seq * tokens + h * half, half), :]
+                sem = token_send.at[len(token_jobs)]
+                far = pltpu.make_async_remote_copy(
+                    src_ref=src,
+                    dst_ref=dst,
+                    send_sem=sem,
+                    recv_sem=token_recv.at[at.seq],
+                    device_id={"dp": at.chip * 2 + h, "seq": to_seq},
+                    device_id_type=pl.DeviceIdType.MESH,
+                )
+                near = pltpu.make_async_copy(src, dst, token_recv.at[at.seq])
+                pl.when(mine)(near.start)
+                pl.when(jnp.logical_not(mine))(far.start)
+                token_jobs.append((mine, far))
+
+    other = at.chip * 2 + 1 - at.core
+    small_copies = []
+    small_rows = pl.ds(pl.multiple_of(at.dp * 8, 8), 8)
+    small_own = copies.local(small, small_v.at[small_rows, :])
+    for step in range(1, dp_ways):
+        small_copies.append(
+            copies.remote(small, small_v.at[small_rows, :], dp=lax.rem(at.dp + step, dp_ways))
+        )
+
+    def qkv_pieces(core):
+        group = at.rank * 2 + core
+        return [
+            (
+                wq.at[:, lanes_at(part * width + group * head_cols, head_cols)],
+                wq_v.at[me, pl.ds(part * head_cols, head_cols)],
+            )
+            for part in range(3)
+        ]
+
+    def fc1_pieces(core):
+        return [
+            (
+                w1.at[:, lanes_at((2 * q + core) * unit_rows, unit_rows)],
+                w1_out.at[me, pl.ds(q * unit_rows, unit_rows)],
+            )
+            for q in range(chips)
+        ]
+
+    def start_columns(pieces):
+        arrivals = {0: [], "local": [copies.local(src, dst) for src, dst in pieces(at.core)]}
+        for src, dst in pieces(1 - at.core):
+            arrivals[0].append(copies.remote(src, dst, dp=other))
+        for offset in offsets:
+            for core in (at.core, 1 - at.core):
+                for src, dst in pieces(core):
+                    copy = copies.remote(src, dst, dp=at.partner(offset) * 2 + core)
+                    arrivals.setdefault(offset, []).append(copy)
+        return arrivals
+
+    def pass_on(arrivals, block_of, first, second):
+        for copy in arrivals[1]:
+            copy.wait_recv()
+        last = []
+        if relay:
+            ref = block_of(at.partner(1), *first)
+            last.append(copies.remote(ref, ref, dp=at.partner(2) * 2 + at.core))
+        for copy in arrivals[2]:
+            copy.wait_recv()
+        if relay:
+            ref = block_of(at.partner(2), *second)
+            last.append(copies.remote(ref, ref, dp=at.partner(1) * 2 + at.core))
+        for offset in range(3, chips):
+            if not relay:
+                for copy in arrivals[offset]:
+                    copy.wait_recv()
+        return last
+
+    def settle(arrivals, last):
+        for copy in last:
+            copy.wait_recv()
+        for copy in arrivals[0]:
+            copy.wait_recv()
+
+    def shard_halves(ref):
+        return lambda chip, start, size: ref.at[rows_at(chip * 2 * shard + start, size), :]
+
+    qkv_arrivals = start_columns(qkv_pieces)
+
+    wp_near = [copies.remote(wp, wp_out.at[me, :], dp=other)]
+    copies.local(wp, wp_out.at[me, :])
+    wp_far = {
+        o: [copies.remote(wp, wp_out.at[me, :], dp=at.partner(o) * 2 + at.core)] for o in offsets
+    }
+    cot_rows = rows_at(at.core * cot.shape[0], cot.shape[0])
+    cot_near = copies.remote(cot, cot_out.at[cot_rows, :], dp=other)
+    copies.local(cot, cot_out.at[cot_rows, :])
+
+    for s in range(seq_ways):
+        pltpu.make_async_copy(
+            img.at[pl.ds(0, half), :], img_v.at[pl.ds(s * tokens, half), :], token_recv.at[s]
+        ).wait()
+    for mine, far in token_jobs:
+        pl.when(jnp.logical_not(mine))(far.wait_send)
+    token_near = []
+    for s in range(seq_ways):
+        ref = img_v.at[rows_at(s * tokens + at.core * half, half), :]
+        token_near.append(copies.remote(ref, ref, dp=other))
+    qkv_last = pass_on(qkv_arrivals, shard_halves(wq_v), (0, shard), (shard, shard))
+    fc1_arrivals = start_columns(fc1_pieces)
+    w2_to = lambda chip: w2_out.at[rows_at(chip * unit_rows, unit_rows), :]
+    copies.local(w2, w2_to(at.chip))
+    fc2_arrivals = {0: []}
+    for offset in offsets:
+        fc2_arrivals[offset] = [
+            copies.remote(w2, w2_to(at.chip), dp=at.partner(offset) * 2 + at.core)
+        ]
+
+    for copy in small_copies:
+        copy.wait_recv()
+    copies.wait_local(small_own)
+    names = {"query": (0, 2), "gain": (3, 1), "shift": (4, 1)}
+    for row, (start, size) in enumerate(names.values()):
+        for i in range(dp_ways):
+            vec_v[row : row + 1, i * size * shard : (i + 1) * size * shard] = small_v[
+                8 * i : 8 * i + 1, start * shard : (start + size) * shard
+            ]
+    for copy in token_near:
+        copy.wait_recv()
+    settle(qkv_arrivals, qkv_last)
+    for copy in qkv_arrivals["local"]:
+        copies.wait_local(copy)
+
+    group = at.rank * 2 + at.core
+    gain = vec_v[1:2, :width]
+    shift = vec_v[2:3, :width]
+
+    def project(step, carry):
+        rows = rows_at(step * tokens, tokens)
+        normed, _ = norm_stats(img_v[rows, :].astype(f32))
+        hidden = (normed * gain + shift).astype(bf16)
+        for part in range(3):
+            cols = slice(part * head_cols, (part + 1) * head_cols)
+            block = dot(hidden, wq_v[:, cols])
+            if part != 1:
+                lanes = lanes_at((part // 2) * width + group * head_cols, head_cols)
+                block = block + vec_v[0:1, lanes]
+            prj_v[rows, cols] = block.astype(bf16)
+        return carry
+
+    lax.fori_loop(0, seq_ways, project, 0)
+    copies.local(img_v, img_out)
+    copies.local(wq_v, wq_out)
+    copies.local(prj_v, prj_out)
+    copies.local(small_v, small_out)
+
+    rows = block_size(length)
+    home_core = lax.div(at.item, items)
+    home_item = lax.rem(at.item, items)
+
+    def back_copies(pair):
+        jobs = []
+        for s in range(seq_ways):
+            mine = (at.seq == s) & (at.core == home_core)
+            src = heads_v.at[pl.ds(s * tokens, tokens), lanes_at(pair * LANES, LANES)]
+            dst = rows_out.at[
+                rows_at(home_item * tokens, tokens),
+                lanes_at(group * head_cols + pair * LANES, LANES),
+            ]
+            far = pltpu.make_async_remote_copy(
+                src_ref=src,
+                dst_ref=dst,
+                send_sem=back_send.at[pair, s],
+                recv_sem=back_recv,
+                device_id={"dp": at.chip * 2 + home_core, "seq": s},
+                device_id_type=pl.DeviceIdType.MESH,
+            )
+            near = pltpu.make_async_copy(src, dst, back_recv)
+            jobs.append((mine, far, near))
+        return jobs
+
+    def one_pair(pair, carry):
+        v_flip[...] = transpose_low(prj_v[:, lanes_at((2 * pairs + pair) * LANES, LANES)])
+
+        def one_block(block, inner):
+            attend_rows(prj_v, heads_v, lse_out, v_flip, pair, block, rows)
+            return inner
+
+        lax.fori_loop(0, length // rows, one_block, 0)
+        for mine, far, near in back_copies(pair):
+            pl.when(mine)(near.start)
+            pl.when(jnp.logical_not(mine))(far.start)
+        return carry
+
+    lax.fori_loop(0, pairs, one_pair, 0)
+    copies.local(heads_v, heads_out)
+    wp_last = pass_on(
+        wp_far,
+        lambda chip, start, size: wp_out.at[
+            rows_at((chip * 2 + at.core) * shard + start, size), :
+        ],
+        (0, shard // 2),
+        (shard // 2, shard // 2),
+    )
+    fc1_last = pass_on(fc1_arrivals, shard_halves(w1_out), (0, shard), (shard, shard))
+    for copy in wp_last:
+        copy.wait_recv()
+    for offset in range(1, chips):
+        ref = wp_out.at[rows_at((at.source(offset) * 2 + at.core) * shard, shard), :]
+        wp_near.append(copies.remote(ref, ref, dp=other))
+    fc2_last = pass_on(
+        fc2_arrivals,
+        lambda chip, start, size: w2_out.at[rows_at(chip * unit_rows + start, size), :],
+        (0, unit_rows // 2),
+        (unit_rows // 2, unit_rows // 2),
+    )
+    settle(fc1_arrivals, fc1_last)
+    settle(fc2_arrivals, fc2_last)
+    for copy in wp_near:
+        copy.wait_recv()
+    cot_near.wait_recv()
+    pltpu.make_async_copy(rows_out, rows_out, back_recv).wait()
+
+    def drain(pair, carry):
+        for mine, far, _ in back_copies(pair):
+            pl.when(jnp.logical_not(mine))(far.wait_send)
+        return carry
+
+    lax.fori_loop(0, pairs, drain, 0)
+    copies.finish()
+
+
+def forward(items, img, wq, wp, w1, w2, cot, small):
+    dp_ways, seq_ways = lax.axis_size("dp"), lax.axis_size("seq")
+    ranks = seq_ways // (2 * items)
+    shard, width = wp.shape
+    head_cols = width // (2 * ranks)
+    tokens = img.shape[0] // items
+    length = seq_ways * tokens
+    half_units = w1.shape[1] // 2
+    pairs = head_cols // LANES
+    any_spec = pl.BlockSpec(memory_space=pl.ANY)
+    out_shape = [
+        jax.ShapeDtypeStruct((length, width), bf16),
+        jax.ShapeDtypeStruct((width, 3 * head_cols), bf16),
+        jax.ShapeDtypeStruct((width, width), bf16),
+        jax.ShapeDtypeStruct((width, half_units), bf16),
+        jax.ShapeDtypeStruct((half_units, width), bf16),
+        jax.ShapeDtypeStruct((2 * cot.shape[0], width), bf16),
+        jax.ShapeDtypeStruct((8 * dp_ways, small.shape[1]), f32),
+        jax.ShapeDtypeStruct((length, 3 * head_cols), bf16),
+        jax.ShapeDtypeStruct((length, head_cols), bf16),
+        jax.ShapeDtypeStruct((pairs, 2, length), f32),
+        jax.ShapeDtypeStruct(img.shape, bf16),
+    ]
+    out_specs = [any_spec] * len(out_shape)
+    out_specs[9] = pl.BlockSpec(memory_space=pltpu.VMEM)
+    remotes = 160
+    return pl.pallas_call(
+        functools.partial(forward_kernel, items),
+        in_specs=[any_spec] * 7,
+        out_specs=out_specs,
+        out_shape=out_shape,
+        scratch_shapes=[
+            pltpu.VMEM((length, width), bf16),
+            pltpu.VMEM((width, 3 * head_cols), bf16),
+            pltpu.VMEM((length, 3 * head_cols), bf16),
+            pltpu.VMEM((length, head_cols), bf16),
+            pltpu.VMEM((8 * dp_ways, small.shape[1]), f32),
+            pltpu.VMEM((8, 2 * width), f32),
+            pltpu.VMEM((LANES, length), bf16),
+            pltpu.SemaphoreType.DMA((remotes,)),
+            pltpu.SemaphoreType.DMA((remotes,)),
+            pltpu.SemaphoreType.DMA((32,)),
+            pltpu.SemaphoreType.DMA((2,)),
+            pltpu.SemaphoreType.DMA((2 * items * ranks,)),
+            pltpu.SemaphoreType.DMA((seq_ways,)),
+            pltpu.SemaphoreType.DMA((pairs, seq_ways)),
+            pltpu.SemaphoreType.DMA,
+        ],
+        compiler_params=pltpu.CompilerParams(
+            collective_id=0, has_side_effects=True, vmem_limit_bytes=62 * 2**20
+        ),
+        name="forward",
+    )(img, wq, wp, w1, w2, cot, small)
 
 
 def body(
@@ -260,50 +709,39 @@
         return total.astype(bf16)
 
     small_names = (qv_bias, proj_bias, ln1_gain, ln1_bias, ln2_gain, ln2_bias, fc1_bias, fc2_bias)
-    small = lax.all_gather(jnp.concatenate(small_names), "dp", axis=0)
+    small = jnp.concatenate(small_names).astype(f32)
+    cotangent_own = cotangent.reshape(own_rows, width)
+    (
+        image_low,
+        qkv_full,
+        proj_full,
+        fc1_half,
+        fc2_half,
+        cotangent_all,
+        small,
+        projected,
+        attended,
+        log_total,
+        attended_rows,
+    ) = forward(
+        items,
+        images.reshape(own_rows, width),
+        qkv_weight,
+        proj_weight,
+        fc1_weight,
+        fc2_weight,
+        cotangent_own,
+        jnp.broadcast_to(small, (8, small.shape[0])),
+    )
+    small = small.reshape(dp_ways, 8, -1)[:, 0]
     smalls, at = [], 0
     for array in small_names:
-        smalls.append(small[:, at : at + array.shape[0]].reshape(-1).astype(f32))
+        smalls.append(small[:, at : at + array.shape[0]].reshape(-1))
         at += array.shape[0]
-    qv_full, bias_proj, gain_first, shift_first, gain_second, shift_second, bias_one, bias_two = (
-        smalls
-    )
-
-    kept = lax.dynamic_slice_in_dim(images, core * half, half, 1)
-    given = swap(lax.dynamic_slice_in_dim(images, (1 - core) * half, half, 1))
-    column = by_core(kept, given, 0).reshape(column_items, half, width)
-    arrived = lax.all_to_all(jnp.repeat(column, ranks, axis=0), "seq", 0, 0)
-    image_rows = by_core(arrived, swap(arrived), 1).reshape(length, width).astype(f32)
-
-    qkv_parts = qkv_weight.reshape(shard_rows, 3, groups, head_cols)
-    qkv_block = by_core(pick(qkv_parts, group, 2), swap(pick(qkv_parts, group ^ 1, 2)), 0)
-    qkv_block = qkv_block.reshape(2 * shard_rows, 3 * head_cols)
-    qkv_full = gather_chips(qkv_block).reshape(width, 3 * head_cols)
-    proj_full = lax.all_gather(proj_weight, "dp", axis=0, tiled=True)
-
-    fc1_parts = fc1_weight.reshape(shard_rows, chips, 2, -1)
-    fc1_block = by_core(pick(fc1_parts, core, 2), swap(pick(fc1_parts, 1 - core, 2)), 0)
-    fc1_block = fc1_block.reshape(2 * shard_rows, -1)
-    fc1_half = gather_chips(fc1_block).reshape(width, -1)
-    fc2_half = gather_chips(fc2_weight).reshape(-1, width)
+    _, bias_proj, gain_first, shift_first, gain_second, shift_second, bias_one, bias_two = smalls
     bias_one_half = pick(bias_one.reshape(chips, 2, -1), core, 1).reshape(-1)
-    cotangent_own = cotangent.reshape(own_rows, width)
-    cotangent_all = by_core(cotangent_own, swap(cotangent_own), 0).reshape(2 * own_rows, width)
-
-    bias_parts = qv_full.reshape(2, groups, head_cols)
-    bias_group = pick(bias_parts, group, 1)
-    bias_row = jnp.concatenate(
-        [bias_group[0], jnp.zeros((head_cols,), f32), bias_group[1]]
-    )
-    normed_image, _ = norm_stats(image_rows)
+    normed_image, _ = norm_stats(image_low.astype(f32))
     hidden_first = (normed_image * gain_first + shift_first).astype(bf16)
-    projected = (dot(hidden_first, qkv_full) + bias_row).astype(bf16)
-    attended, log_total = attend(projected)
-
-    back = lax.all_to_all(attended.reshape(seq_ways, tokens, head_cols), "seq", 0, 0)
-    back = back.reshape(2, items, ranks, tokens, head_cols)
-    both = by_core(pick(back, core, 0), swap(pick(back, 1 - core, 0)), 3)
-    attended_rows = jnp.moveaxis(both, 1, 2).reshape(own_rows, width)
 
     flat_rows = images.reshape(own_rows, width).astype(f32)
     residual_first = flat_rows + dot(attended_rows, proj_full) + bias_proj

time: 663 us -> 634 us (0.956)
  Pallas kernels: 60.3 us -> 153 us
  local copies, waits for them, and re-layouts: 111 us -> 66.1 us
  blocking collectives: 33.3 us -> 0 us
  starting transfers between devices: 46.2 us -> 22.3 us
  waiting for transfers between devices: 253 us -> 239 us
  other arithmetic: 60.3 us -> 53.4 us
    pallas_call x1, Pallas kernels: 24.8 us -> 117 us  [forward(): pl.pallas_call(functools.partial(forward_kernel, items), in_specs=[any_sp...]
    ppermute x18 -> x9, waiting for transfers between devices: 137 us -> 101 us  [hop(): lax.ppermute(array, 'dp', [(i, i ^ 2 * bits) for i in range(dp_ways)])]
    all_gather x1 -> x0, blocking collectives: 33.3 us -> none  [body(): small = lax.all_gather(jnp.concatenate(small_names), 'dp', axis=0)]
    psum x1, waiting for transfers between devices: 28.2 us -> 55.9 us  [body(): share_two = lax.psum(share_two, 'seq')]
    dynamic_update_slice x12 -> x0, local copies, waits for them, and re-layouts: 20.3 us -> none  [the longest x9 17.9 us: gather_chips(): lax.dynamic_update_index_in_dim(gathered, hop(block, bits), chip ^ bits, 0)]
    all_to_all x2 -> x0, starting transfers between devices: 11.9 us -> none  [the longest x1 6.23 us: body(): arrived = lax.all_to_all(jnp.repeat(column, ranks, axis=0), 'seq', 0, 0)]
    ppermute x18 -> x9, starting transfers between devices: 22.3 us -> 11.5 us  [hop(): lax.ppermute(array, 'dp', [(i, i ^ 2 * bits) for i in range(dp_ways)])]
    select_n x6 -> x0, local copies, waits for them, and re-layouts: 9.72 us -> none  [by_core(): jnp.where(first_core, jnp.stack([own, other], axis), jnp.stack([other, ow...]
  transfers between devices with their start and end apart: 43 -> 25, of which waited for: 16 -> 8; matrix products, arithmetic and copies ran while one was open for 28% -> 21% of each run, Pallas kernels for 9% -> 6%
where the time goes in v2:
time: 634 us; the launch traced here: 625 us
  waiting for transfers between devices  239 us (38%)
  Pallas kernels  153 us (24%)
  matrix products  74.8 us (12%)
  local copies, waits for them, and re-layouts  66.1 us (10%)
  other arithmetic  53.4 us (8%)
  starting transfers between devices  22.3 us (4%)
  between operations  16.3 us (3%)
    pallas_call x1, Pallas kernels, forward(): pl.pallas_call(functools.partial(forward_kernel, items), in_specs=[any_sp...  117 us
    ppermute x9, waiting for transfers between devices, hop(): lax.ppermute(array, 'dp', [(i, i ^ 2 * bits) for i in range(dp_ways)])  101 us
    dot_general x11, matrix products, dot(): lax.dot_general(left, right, (((left_dim,), (right_dim,)), ((), ())), pre...  74.8 us
    psum x1, waiting for transfers between devices, body(): share_two = lax.psum(share_two, 'seq')  55.9 us
    psum x1, waiting for transfers between devices, body(): share_proj = lax.psum(share_proj, 'seq')  44.3 us
    psum x1, waiting for transfers between devices, body(): flat = lax.psum(flat, 'seq')  36.6 us
    pallas_call x1, Pallas kernels, attend_back(): pl.pallas_call(attend_back_kernel, grid=(pairs, length // rows), in_specs...  35.3 us
    unnamed x84, local copies, waits for them, and re-layouts  22.1 us
  transfers between devices with their start and end apart: 25, of which 8 were waited for; matrix products, arithmetic and copies ran while one was open for 21% of the time, Pallas kernels for 6%

profile of v2, /device:TPU:0, one launch (start us, length us, event | category | flops | bytes accessed | tf_op | source)
XLA Modules:
  0.0 624.5 jit_solution(1924094576080146325)
XLA Ops:
  15.4 117.5 %forward.1 = (bf16[1152,1024]{1,0:T(8,128)(2,1)}, bf16[1024,1536]{1,0:T(8,128)(2,1)}, bf16[1024,1024]{1,0:T(8,128)(2,1)}, bf16[1024,2048]{1,0:T(8,128)(2,1)}, bf...) custom-call(bf16[576,1024]{1,0:T(8,128)(2,1)} %bitcast.168, ...), custom_call_target="tpu_custom_call" | custom-call | tf_op jit(solution)/shard_map/forward/pallas_call | solution.py:615
  134.5 3.5 fusion.63
  138.4 1.5 add_convert_fusion
  140.5 1.3 reshape_reshape.6
  142.7 2.1 convert_reduce_fusion
  144.8 1.4 fusion.12
  146.6 2.1 maximum_select_fusion
  149.5 8.6 %multiply_convert_fusion = (bf16[1152,2048]{1,0:T(8,128)(2,1)}, f32[1152,2048]{1,0:T(8,128)}) fusion(f32[2048]{0:T(1024)S(1)} %bitcast.202, bf16[1152,1024]{1,0:T(8,128)(2,1)S(1)} %bitcast.188, bf16[1024,2048]{1,0:T(8,128)(2,1)S(1)} %copy-done.29), kind=kOutput, calls=%fused_computation.6 | convolution fusion | flops 4845993984 | bytes 20717568 | tf_op jit(solution)/shard_map/dot_general | solution.py:43
  158.1 12.4 %fusion.64 = (bf16[2048]{0:T(1024)(128)(2,1)}, bf16[1152,2048]{1,0:T(8,128)(2,1)}) fusion(f32[1152,2048]{1,0:T(8,128)} %get-tuple-element.122, bf16[1152,1024]{1,0:T(8,128)(2,1)S(1)} %copy-done.30, bf16[2048,1024]{1,0:T(8,128)(2,1)S(1)} %copy-done.28), kind=kOutput, calls=%fused_computation.163 | convolution fusion | flops 4857788416 | bytes 20713472 | tf_op jit(solution)/shard_map/dot_general | solution.py:43
  170.5 7.1 %fusion.37 = f32[1152,1024]{1,0:T(8,128)S(1)} fusion(bf16[1024,2048]{1,0:T(8,128)(2,1)S(1)} %copy-done.29, bf16[1152,2048]{1,0:T(8,128)(2,1)} %get-tuple-element.125), kind=kOutput, calls=%fused_computation.63 | convolution fusion | flops 4831838208 | bytes 13631488 | tf_op jit(solution)/shard_map/dot_general | solution.py:43
  177.7 5.9 convolution_convert_fusion.1
  184.4 7.6 %fusion.65 = f32[1152,1024]{1,0:T(8,128)S(1)} fusion(bf16[1152,2048]{1,0:T(8,128)(2,1)} %get-tuple-element.121, bf16[2048,1024]{1,0:T(8,128)(2,1)S(1)} %copy-done.28), kind=kOutput, calls=%fused_computation.164 | convolution fusion | flops 4831838208 | bytes 13631488 | tf_op jit(solution)/shard_map/dot_general | solution.py:43
  192.8 8.4 %convolution_convert_fusion = bf16[2048,1024]{1,0:T(8,128)(2,1)S(1)} fusion(bf16[1152,2048]{1,0:T(8,128)(2,1)} %get-tuple-element.121, bf16[1152,1024]{1,0:T(8,128)(2,1)S(1)} %copy-done.30), kind=kOutput, calls=%fused_computation.23 | convolution fusion | flops 4833935360 | bytes 11272192 | tf_op jit(solution)/shard_map/dot_general | solution.py:43
  201.2 1.8 dynamic-slice_bitcast_fusion.5
  203.0 1.4 collective-permute-start.11
  204.4 1.5 collective-permute-start.10
  206.0 1.8 dynamic-slice_bitcast_fusion.2
  207.7 1.4 collective-permute-start.14
  209.7 1.8 multiply_reduce_fusion
  211.6 1.5 collective-permute-start.12
  213.1 2.9 fusion.61
  216.1 36.6 %collective-permute-done.14 = bf16[512,1024]{1,0:T(8,128)(2,1)S(1)} collective-permute-done((bf16[512,1024]{1,0:T(8,128)(2,1)S(1)}, bf16[512,1024]{1,0:T(8,128)(2,1)S(1)}, u32[]{:S(2)}, u32[]{:S(2)}) %collective-permute-start.14) | collective-permute-done | bytes 1048608 | tf_op jit(solution)/shard_map/ppermute | solution.py:690
  252.7 1.5 collective-permute-start.9
  254.2 1.4 convolution_convert_fusion.4
  256.5 3.4 constant_dynamic-slice_fusion.8
  260.9 35.8 %collective-permute-done.13 = bf16[512,1024]{1,0:T(8,128)(2,1)} collective-permute-done((bf16[512,1024]{1,0:T(8,128)(2,1)}, bf16[512,1024]{1,0:T(8,128)(2,1)}, u32[]{:S(2)}, u32[]{:S(2)}) %collective-permute-start.13) | collective-permute-done | bytes 1048608 | tf_op jit(solution)/shard_map/ppermute | solution.py:690
  298.9 3.8 fusion.41
  302.9 2.4 maximum_select_fusion.1
  305.3 4.5 all-to-all-start
  309.9 4.1 fusion.44
  316.5 55.9 %all-reduce.8.cloned.1.call-done = bf16[512,1024]{1,0:T(8,128)(2,1)} async-done(((bf16[512,1024]{1,0:T(8,128)(2,1)}), bf16[512,1024]{1,0:T(8,128)(2,1)}) %all-reduce.8.cloned.1.call-update) | async-done | bytes 1048592 | tf_op jit(solution)/shard_map/psum | solution.py:808
  374.3 1.3 constant_dynamic-update-slice_fusion
  376.4 3.1 convolution_convert_fusion.3
  379.5 1.7 fusion.26
  381.3 35.3 %attend_back.1 = (bf16[1152,1536]{1,0:T(8,128)(2,1)}, f32[4,2,128]{2,1,0:T(2,128)}) custom-call(bf16[1152,1536]{1,0:T(8,128)(2,1)} %get-tuple-element.39.q_ref.k_ref.v_ref, bf16[1152,1536]{1,0:T(8,128)(2,1)} %get-tuple-element.39.q_ref.k_ref.v_ref, bf16[1152,1536]{1,0:T(8,128)(2,1)} %get-tuple-element.39.q_ref.k_ref.v_ref, ...), custom_call_target="tpu_custom_call" | custom-call | flops 27179089920 | bytes 9437184 | tf_op jit(solution)/shard_map/attend_back/pallas_call | solution.py:161
  417.9 1.3 dynamic_update_slice.3
  419.9 9.9 %fusion.11 = (bf16[1024]{0:T(1024)(128)(2,1)}, bf16[1024]{0:T(1024)(128)(2,1)}, f32[1152,1024]{1,0:T(8,128)}) fusion(bf16[1152,1024]{1,0:T(8,128)(2,1)S(1)} %copy-done.7, f32[1152]{0:T(1024)} %add_rsqrt_fusion, f32[1152]{0:T(1024)S(1)} %copy-done.23, bf16[1152,1536]{1,0:T(8,128)(2,1)} %get-tuple-element.42, bf16[1024,1536]{1,0:T(8,128)(2,1)} %get-tuple-element.43), kind=kOutput, calls=%fused_computation.19 | convolution fusion | flops 3630954496 | bytes 13775872 | tf_op jit(solution)/shard_map/dot_general | solution.py:43
  429.8 1.3 concatenate.60
  431.0 1.3 concatenate.59
  433.0 6.9 %convolution_convert_fusion.2 = bf16[1024,1536]{1,0:T(8,128)(2,1)S(1)} fusion(bf16[1152,1536]{1,0:T(8,128)(2,1)} %get-tuple-element.42, bf16[1152,1024]{1,0:T(8,128)(2,1)S(1)} %copy-done.7, f32[1024]{0:T(1024)} %get-tuple-element.107, f32[1024]{0:T(1024)S(1)} %get-tuple-element.108, f32[1152]{0:T(1024)} %add_rsqrt_fusion, f32[1152]{0:T(1024)S(1)} %copy-done.23), kind=kOutput, calls=%fused_computation.25 | convolution fusion | flops 3632529408 | bytes 9061376 | tf_op jit(solution)/shard_map/dot_general | solution.py:43
  440.2 1.6 dynamic-slice_bitcast_fusion.8
  442.7 2.4 collective-permute-start.8
  446.4 2.9 fusion.51
  450.5 2.8 convert_element_type.258
  453.3 12.1 %collective-permute-done.8 = bf16[272,1536]{1,0:T(8,128)(2,1)} collective-permute-done((bf16[272,1536]{1,0:T(8,128)(2,1)}, bf16[272,1536]{1,0:T(8,128)(2,1)}, u32[]{:S(2)}, u32[]{:S(2)}) %collective-permute-start.8) | collective-permute-done | bytes 835616 | tf_op jit(solution)/shard_map/ppermute | solution.py:690
  465.4 16.8 %collective-permute-done.7 = bf16[272,1536]{1,0:T(8,128)(2,1)} collective-permute-done((bf16[272,1536]{1,0:T(8,128)(2,1)}, bf16[272,1536]{1,0:T(8,128)(2,1)}, u32[]{:S(2)}, u32[]{:S(2)}) %collective-permute-start.7) | collective-permute-done | bytes 835616 | tf_op jit(solution)/shard_map/ppermute | solution.py:690
  482.3 2.3 fusion.47
  484.7 3.1 fusion.29
  487.8 4.3 all-to-all-start.1
  496.3 44.3 %all-reduce.12.cloned.1.call-done = bf16[144,1024]{1,0:T(8,128)(2,1)} async-done(((bf16[144,1024]{1,0:T(8,128)(2,1)}), bf16[144,1024]{1,0:T(8,128)(2,1)}) %all-reduce.12.cloned.1.call-update) | async-done | bytes 294928 | tf_op jit(solution)/shard_map/psum | solution.py:812
  542.5 1.8 slice_convert_fusion
  545.1 1.8 fusion.53
  546.9 1.8 copy.59
  548.7 2.9 copy.61
  551.6 36.6 %all-reduce.14.cloned.1.call-done = bf16[272,1536]{1,0:T(8,128)(2,1)} async-done(((bf16[272,1536]{1,0:T(8,128)(2,1)}), bf16[272,1536]{1,0:T(8,128)(2,1)}) %all-reduce.14.cloned.1.call-update) | async-done | bytes 835600 | tf_op jit(solution)/shard_map/psum | solution.py:866
  589.9 1.3 slice.122
  591.2 1.6 constant_dynamic-slice_fusion.6
  593.9 1.6 copy.54
  596.3 2.4 dynamic-slice_bitcast_fusion.10
  601.9 1.6 copy.56
  603.5 3.0 copy.60
  607.4 1.9 fusion.52
  611.1 1.3 broadcast_multiply_fusion.1
  613.1 3.8 fusion.25
  (184 shorter events, 47.0 us)
Async XLA Ops:
  8.0 364.4 %all-reduce.8.cloned.1.call-start = ((), (), s32[]{:S(2)}) async-start(), calls=%async_computation.4 | async-start | bytes 2097152 | tf_op jit(solution)/shard_map/psum | solution.py:808
  15.4 119.1 %copy-start = (bf16[2,288,1024]{2,1,0:T(8,128)(2,1)S(1)}, bf16[2,288,1024]{2,1,0:T(8,128)(2,1)}, u32[]{:S(2)}) copy-start(bf16[2,288,1024]{2,1,0:T(8,128)(2,1)} %param.14) | copy-start | bytes 3538948
  134.5 3.9 copy-start.20
  139.9 6.7 %collective-permute-start = (bf16[576,1024]{1,0:T(8,128)(2,1)}, bf16[576,1024]{1,0:T(8,128)(2,1)}, u32[]{:S(2)}, u32[]{:S(2)}) collective-permute-start(bf16[576,1024]{1,0:T(8,128)(2,1)} %add_convert_fusion), channel_id=1, source_target_pairs={{0,4},{4,0},{8,12},{12,8},{16,20},{20,16},{24,28},{28,24},{1,5},{5... | collective-permute-start | bytes 3538952 | tf_op jit(solution)/shard_map/ppermute | solution.py:679
  141.8 2.9 copy-start.6
  142.7 3.5 copy-start.21
  144.8 1.8 copy-start.22
  146.6 2.9 copy-start.29
  149.5 8.6 %copy-start.28 = (bf16[2048,1024]{1,0:T(8,128)(2,1)S(1)}, bf16[2048,1024]{1,0:T(8,128)(2,1)}, u32[]{:S(2)}) copy-start(bf16[2048,1024]{1,0:T(8,128)(2,1)} %get-tuple-element.37) | copy-start | bytes 12582916
  149.5 8.6 %copy-start.30 = (bf16[1152,1024]{1,0:T(8,128)(2,1)S(1)}, bf16[1152,1024]{1,0:T(8,128)(2,1)}, u32[]{:S(2)}) copy-start(bf16[1152,1024]{1,0:T(8,128)(2,1)} %get-tuple-element.38) | copy-start | bytes 7077892
  170.5 7.2 %copy-start.32 = (bf16[1152,2048]{1,0:T(8,128)(2,1)S(1)}, bf16[1152,2048]{1,0:T(8,128)(2,1)}, u32[]{:S(2)}) copy-start(bf16[1152,2048]{1,0:T(8,128)(2,1)} %get-tuple-element.125) | copy-start | bytes 14155780
  183.6 17.6 %copy-start.10 = (bf16[1024,2048]{1,0:T(8,128)(2,1)}, bf16[1024,2048]{1,0:T(8,128)(2,1)S(1)}, u32[]{:S(2)}) copy-start(bf16[1024,2048]{1,0:T(8,128)(2,1)S(1)} %convolution_convert_fusion.1) | copy-start | bytes 12582916
  183.8 25.4 %collective-permute-start.2 = (bf16[576,1024]{1,0:T(8,128)(2,1)S(1)}, bf16[576,1024]{1,0:T(8,128)(2,1)S(1)}, u32[]{:S(2)}, u32[]{:S(2)}) collective-permute-start(bf16[576,1024]{1,0:T(8,128)(2,1)S(1)} %fusion.50), channel_id=1, source_target_pairs={{0,4},{4,0},{8,12},{12,8},{16,20},{20,16},{24,28},{28,24},{1,5},{5... | collective-permute-start | bytes 3538952 | tf_op jit(solution)/shard_map/ppermute | solution.py:679
  192.2 19.4 %collective-permute-start.1 = (bf16[576,1024]{1,0:T(8,128)(2,1)S(1)}, bf16[576,1024]{1,0:T(8,128)(2,1)S(1)}, u32[]{:S(2)}, u32[]{:S(2)}) collective-permute-start(bf16[576,1024]{1,0:T(8,128)(2,1)S(1)} %fusion.49), channel_id=1, source_target_pairs={{0,4},{4,0},{8,12},{12,8},{16,20},{20,16},{24,28},{28,24},{1,5},{5... | collective-permute-start | bytes 3538952 | tf_op jit(solution)/shard_map/ppermute | solution.py:679
  201.2 4.8 copy-start.11
  203.0 106.9 %collective-permute-start.11 = (bf16[256,2048]{1,0:T(8,128)(2,1)}, bf16[256,2048]{1,0:T(8,128)(2,1)}, u32[]{:S(2)}, u32[]{:S(2)}) collective-permute-start(bf16[256,2048]{1,0:T(8,128)(2,1)} %get-tuple-element.93), channel_id=1, source_target_pairs={{0,24},{4,28},{8,16},{12,20},{16,8},{20,12},{24,0},{28,4},{1,25},{... | collective-permute-start | bytes 3145736 | tf_op jit(solution)/shard_map/ppermute | solution.py:690
  204.4 105.5 %collective-permute-start.10 = (bf16[256,2048]{1,0:T(8,128)(2,1)}, bf16[256,2048]{1,0:T(8,128)(2,1)}, u32[]{:S(2)}, u32[]{:S(2)}) collective-permute-start(bf16[256,2048]{1,0:T(8,128)(2,1)} %get-tuple-element.94), channel_id=1, source_target_pairs={{0,16},{4,20},{8,24},{12,28},{16,0},{20,4},{24,8},{28,12},{1,17},{... | collective-permute-start | bytes 3145736 | tf_op jit(solution)/shard_map/ppermute | solution.py:690
  207.7 44.9 %collective-permute-start.14 = (bf16[512,1024]{1,0:T(8,128)(2,1)S(1)}, bf16[512,1024]{1,0:T(8,128)(2,1)S(1)}, u32[]{:S(2)}, u32[]{:S(2)}) collective-permute-start(bf16[512,1024]{1,0:T(8,128)(2,1)S(1)} %get-tuple-element.90), channel_id=1, source_target_pairs={{0,24},{4,28},{8,16},{12,20},{16,8},{20,12},{24,0},{28,4},{1,25},{... | collective-permute-start | bytes 3145736 | tf_op jit(solution)/shard_map/ppermute | solution.py:690
  209.2 3.9 copy-start.2
  209.2 3.9 copy-start.25
  209.2 87.6 %collective-permute-start.13 = (bf16[512,1024]{1,0:T(8,128)(2,1)}, bf16[512,1024]{1,0:T(8,128)(2,1)}, u32[]{:S(2)}, u32[]{:S(2)}) collective-permute-start(bf16[512,1024]{1,0:T(8,128)(2,1)} %get-tuple-element.91), channel_id=1, source_target_pairs={{0,16},{4,20},{8,24},{12,28},{16,0},{20,4},{24,8},{28,12},{1,17},{... | collective-permute-start | bytes 3145736 | tf_op jit(solution)/shard_map/ppermute | solution.py:690
  211.6 87.3 %collective-permute-start.12 = (bf16[512,1024]{1,0:T(8,128)(2,1)}, bf16[512,1024]{1,0:T(8,128)(2,1)}, u32[]{:S(2)}, u32[]{:S(2)}) collective-permute-start(bf16[512,1024]{1,0:T(8,128)(2,1)} %get-tuple-element.89), channel_id=1, source_target_pairs={{0,8},{4,12},{8,0},{12,4},{16,24},{20,28},{24,16},{28,20},{1,9},{5... | collective-permute-start | bytes 3145736 | tf_op jit(solution)/shard_map/ppermute | solution.py:690
  213.1 41.0 %copy-start.31 = (bf16[1024,1024]{1,0:T(8,128)(2,1)S(1)}, bf16[1024,1024]{1,0:T(8,128)(2,1)}, u32[]{:S(2)}) copy-start(bf16[1024,1024]{1,0:T(8,128)(2,1)} %get-tuple-element.34) | copy-start | bytes 6291460
  216.1 38.1 %copy-start.4 = (f32[576,1024]{1,0:T(8,128)}, f32[576,1024]{1,0:T(8,128)S(1)}, u32[]{:S(2)}) copy-start(f32[576,1024]{1,0:T(8,128)S(1)} %get-tuple-element.87) | copy-start | bytes 7077892
  252.7 1.5 copy-start.16
  252.7 57.3 %collective-permute-start.9 = (bf16[256,2048]{1,0:T(8,128)(2,1)}, bf16[256,2048]{1,0:T(8,128)(2,1)}, u32[]{:S(2)}, u32[]{:S(2)}) collective-permute-start(bf16[256,2048]{1,0:T(8,128)(2,1)} %get-tuple-element.92), channel_id=1, source_target_pairs={{0,8},{4,12},{8,0},{12,4},{16,24},{20,28},{24,16},{28,20},{1,9},{5... | collective-permute-start | bytes 3145736 | tf_op jit(solution)/shard_map/ppermute | solution.py:690
  256.5 40.2 %copy-start.3 = (bf16[2,288,1024]{2,1,0:T(8,128)(2,1)S(1)}, bf16[2,288,1024]{2,1,0:T(8,128)(2,1)}, u32[]{:S(2)}) copy-start(bf16[2,288,1024]{2,1,0:T(8,128)(2,1)} %param.27) | copy-start | bytes 3538948
  260.0 38.2 %copy-start.24 = (f32[1152]{0:T(1024)S(1)}, f32[1152]{0:T(1024)}, u32[]{:S(2)}) copy-start(f32[1152]{0:T(1024)} %fusion.12) | copy-start | bytes 13828
  260.0 38.8 %copy-start.27 = (bf16[2048]{0:T(1024)(128)(2,1)S(1)}, bf16[2048]{0:T(1024)(128)(2,1)}, u32[]{:S(2)}) copy-start(bf16[2048]{0:T(1024)(128)(2,1)} %get-tuple-element.124) | copy-start | bytes 12292
  260.0 38.9 %copy-start.17 = (bf16[512,1024]{1,0:T(8,128)(2,1)S(1)}, bf16[512,1024]{1,0:T(8,128)(2,1)}, u32[]{:S(2)}) copy-start(bf16[512,1024]{1,0:T(8,128)(2,1)} %copy-done.16) | copy-start | bytes 3145732
  296.7 6.1 collective-permute-start.3
  298.8 3.9 copy-start.9
  305.3 75.9 %all-to-all-start = ((bf16[4,288,512]{2,1,0:T(8,128)(2,1)}), bf16[4,288,512]{2,1,0:T(8,128)(2,1)}, u32[]{:S(2)}, u32[]{:S(2)}) async-start(bf16[4,288,512]{2,1,0:T(8,128)(2,1)} %bitcast.21), calls=%async_computation | async-start | bytes 2359296 | tf_op jit(solution)/shard_map/all_to_all | solution.py:779
  309.8 62.7 %copy-start.26 = (bf16[1024]{0:T(1024)(128)(2,1)S(1)}, bf16[1024]{0:T(1024)(128)(2,1)}, u32[]{:S(2)}) copy-start(bf16[1024]{0:T(1024)(128)(2,1)} %get-tuple-element.85) | copy-start | bytes 6148
  309.8 66.6 %copy-start.5 = (f32[576,1024]{1,0:T(8,128)S(1)}, f32[576,1024]{1,0:T(8,128)}, u32[]{:S(2)}) copy-start(f32[576,1024]{1,0:T(8,128)} %copy-done.4) | copy-start | bytes 7077892
  309.9 182.3 %all-reduce.10.cloned.1.call-start = ((), (), s32[]{:S(2)}) async-start(), calls=%async_computation.5 | async-start | bytes 2097152 | tf_op jit(solution)/shard_map/psum | solution.py:810
  372.4 119.7 %reduce-scatter.2.cloned.1.call-start = ((), (), s32[]{:S(2)}) async-start(), calls=%async_computation.3 | async-start | bytes 2654208 | tf_op jit(solution)/shard_map/reduce_scatter | solution.py:807
  381.3 38.6 %copy-start.7 = (bf16[1152,1024]{1,0:T(8,128)(2,1)S(1)}, bf16[1152,1024]{1,0:T(8,128)(2,1)}, u32[]{:S(2)}) copy-start(bf16[1152,1024]{1,0:T(8,128)(2,1)} %get-tuple-element.44) | copy-start | bytes 7077892
  381.3 38.6 %copy-start.23 = (f32[1152]{0:T(1024)S(1)}, f32[1152]{0:T(1024)}, u32[]{:S(2)}) copy-start(f32[1152]{0:T(1024)} %copy-done.22) | copy-start | bytes 13828
  440.2 2.5 copy-start.1
  442.7 22.7 %collective-permute-start.8 = (bf16[272,1536]{1,0:T(8,128)(2,1)}, bf16[272,1536]{1,0:T(8,128)(2,1)}, u32[]{:S(2)}, u32[]{:S(2)}) collective-permute-start(bf16[272,1536]{1,0:T(8,128)(2,1)} %get-tuple-element.96), channel_id=1, source_target_pairs={{0,24},{4,28},{8,16},{12,20},{16,8},{20,12},{24,0},{28,4},{1,25},{... | collective-permute-start | bytes 2506760 | tf_op jit(solution)/shard_map/ppermute | solution.py:690
  445.1 37.1 %collective-permute-start.7 = (bf16[272,1536]{1,0:T(8,128)(2,1)}, bf16[272,1536]{1,0:T(8,128)(2,1)}, u32[]{:S(2)}, u32[]{:S(2)}) collective-permute-start(bf16[272,1536]{1,0:T(8,128)(2,1)} %get-tuple-element.97), channel_id=1, source_target_pairs={{0,16},{4,20},{8,24},{12,28},{16,0},{20,4},{24,8},{28,12},{1,17},{... | collective-permute-start | bytes 2506760 | tf_op jit(solution)/shard_map/ppermute | solution.py:690
  445.6 36.7 %collective-permute-start.6 = (bf16[272,1536]{1,0:T(8,128)(2,1)}, bf16[272,1536]{1,0:T(8,128)(2,1)}, u32[]{:S(2)}, u32[]{:S(2)}) collective-permute-start(bf16[272,1536]{1,0:T(8,128)(2,1)} %get-tuple-element.95), channel_id=1, source_target_pairs={{0,8},{4,12},{8,0},{12,4},{16,24},{20,28},{24,16},{28,20},{1,9},{5... | collective-permute-start | bytes 2506760 | tf_op jit(solution)/shard_map/ppermute | solution.py:690
  449.3 35.4 %collective-permute-start.4 = (bf16[4,144,1024]{2,1,0:T(8,128)(2,1)}, bf16[4,144,1024]{2,1,0:T(8,128)(2,1)S(1)}, u32[]{:S(2)}, u32[]{:S(2)}) collective-permute-start(bf16[4,144,1024]{2,1,0:T(8,128)(2,1)} %fusion.51), channel_id=1, source_target_pairs={{0,4},{4,0},{8,12},{12,8},{16,20},{20,16},{24,28},{28,24},{1,5},{5... | collective-permute-start | bytes 3538952 | tf_op jit(solution)/shard_map/ppermute | solution.py:679
  487.8 108.6 %all-to-all-start.1 = ((bf16[4,144,1024]{2,1,0:T(8,128)(2,1)}), bf16[4,144,1024]{2,1,0:T(8,128)(2,1)}, u32[]{:S(2)}, u32[]{:S(2)}) async-start(bf16[4,144,1024]{2,1,0:T(8,128)(2,1)} %fusion.29), calls=%async_computation.1 | async-start | bytes 2359296 | tf_op jit(solution)/shard_map/all_to_all | solution.py:822
  492.1 48.6 %all-reduce.12.cloned.1.call-start = ((), (), s32[]{:S(2)}) async-start(), calls=%async_computation.6 | async-start | bytes 589824 | tf_op jit(solution)/shard_map/psum | solution.py:812
  492.1 1.7 copy-start.15
  492.8 95.4 %all-reduce.14.cloned.1.call-start = ((), (), s32[]{:S(2)}) async-start(), calls=%async_computation.7 | async-start | bytes 1671168 | tf_op jit(solution)/shard_map/psum | solution.py:866
  495.3 49.0 %collective-permute-start.17 = (bf16[128,4,512]{2,0,1:T(8,128)(2,1)S(1)}, bf16[128,4,512]{2,0,1:T(8,128)(2,1)S(1)}, u32[]{:S(2)}, u32[]{:S(2)}) collective-permute-start(bf16[128,4,512]{2,0,1:T(8,128)(2,1)S(1)} %bitcast.195), channel_id=1, source_target_pairs={{0,4},{4,0},{8,12},{12,8},{16,20},{20,16},{24,28},{28,24},{1,5},{5... | collective-permute-start | bytes 1572872 | tf_op jit(solution)/shard_map/ppermute | solution.py:679
  544.3 0.8 copy-start.18
  591.2 4.3 collective-permute-start.16
  593.4 6.5 %collective-permute-start.15 = (bf16[128,3,1,512]{3,0,2,1:T(8,128)(2,1)S(1)}, bf16[128,3,1,512]{3,0,2,1:T(8,128)(2,1)S(1)}, u32[]{:S(2)}, u32[]{:S(2)}) collective-permute-start(bf16[128,3,1,512]{3,0,2,1:T(8,128)(2,1)S(1)} %bitcast.198), channel_id=1, source_target_pairs={{0,4},{4,0},{8,12},{12,8},{16,20},{20,16},{24,28},{28,24},{1,5},{5... | collective-permute-start | bytes 1179656 | tf_op jit(solution)/shard_map/ppermute | solution.py:679
  596.3 4.3 copy-start.14
  598.7 7.8 %collective-permute-start.5 = (bf16[2,144,1024]{2,1,0:T(8,128)(2,1)}, bf16[2,144,1024]{2,1,0:T(8,128)(2,1)S(1)}, u32[]{:S(2)}, u32[]{:S(2)}) collective-permute-start(bf16[2,144,1024]{2,1,0:T(8,128)(2,1)} %get-tuple-element.100), channel_id=1, source_target_pairs={{0,4},{4,0},{8,12},{12,8},{16,20},{20,16},{24,28},{28,24},{1,5},{5... | collective-permute-start | bytes 1769480 | tf_op jit(solution)/shard_map/ppermute | solution.py:679
  599.9 0.7 copy-start.19
  606.5 2.7 copy-start.8
  606.5 0.8 copy-start.12
  607.4 1.9 copy-start.13
Sparse Core Ops, SparseCore 0:
  302.8 69.5 all-reduce.7
  375.3 51.1 all-reduce.9
  495.2 45.3 all-reduce.11
  542.9 45.3 all-reduce.13
Sparse Core Ops, SparseCore 1:
  381.4 41.5 reduce-scatter.1

commit v3 on v2

--- a/solution.py
+++ b/solution.py
@@ -121,7 +121,11 @@
 
 
 def block_size(length):
-    return next(size for size in (384, 256, 128, length) if length % size == 0)
+    return next(
+        size
+        for size in (384, 256, 128, length)
+        if length % size == 0 and (size * length <= 384 * 1152 or size <= 128 or size == length)
+    )
 
 
 def attend(projected):
@@ -641,6 +645,502 @@
     )(img, wq, wp, w1, w2, cot, small)
 
 
+class Share:
+    def __init__(self, at, copies, slots, total, line, final):
+        self.at, self.copies = at, copies
+        self.slots, self.total, self.line, self.final = slots, total, line, final
+        self.part = total.shape[0] // at.seq_ways
+
+    def spread(self, block_of):
+        at = self.at
+        self.arrivals = [
+            self.copies.remote(
+                block_of(at.partner(offset)),
+                self.slots.at[offset - 1],
+                dp=at.partner(offset) * 2 + at.core,
+            )
+            for offset in range(1, at.chips)
+        ]
+
+    def add_chips(self):
+        for copy in self.arrivals:
+            copy.wait_recv()
+        step = 64 if self.total.shape[0] % 64 == 0 else 16
+
+        def add(i, carry):
+            rows = rows_at(i * step, step)
+            value = self.total[rows, :].astype(f32)
+            for slot in range(self.at.chips - 1):
+                value = value + self.slots[slot, rows, :].astype(f32)
+            self.total[rows, :] = value.astype(bf16)
+            return carry
+
+        lax.fori_loop(0, self.total.shape[0] // step, add, 0)
+        self.arrivals = []
+        for step in range(1, self.at.seq_ways):
+            to = lax.rem(self.at.seq + step, self.at.seq_ways)
+            self.arrivals.append(
+                self.copies.remote(
+                    self.total.at[rows_at(to * self.part, self.part), :],
+                    self.line.at[step - 1],
+                    seq=to,
+                )
+            )
+
+    def add_line(self):
+        for copy in self.arrivals:
+            copy.wait_recv()
+        rows = rows_at(self.at.seq * self.part, self.part)
+        value = self.total[rows, :].astype(f32)
+        for slot in range(self.at.seq_ways - 1):
+            value = value + self.line[slot].astype(f32)
+        self.final[rows, :] = value.astype(bf16)
+        self.arrivals = []
+        for step in range(1, self.at.seq_ways):
+            to = lax.rem(self.at.seq + step, self.at.seq_ways)
+            self.arrivals.append(
+                self.copies.remote(self.final.at[rows, :], self.final.at[rows, :], seq=to)
+            )
+
+    def arrive(self):
+        for copy in self.arrivals:
+            copy.wait_recv()
+
+
+def backward_kernel(
+    items,
+    rgl,
+    wp,
+    g2,
+    g1,
+    gp,
+    prj,
+    heads,
+    img,
+    wq,
+    small,
+    lse,
+    home_out,
+    o2_out,
+    op_out,
+    o1_out,
+    oq_out,
+    ox_out,
+    rgl_v,
+    wp_v,
+    prj_v,
+    heads_v,
+    img_v,
+    wq_v,
+    small_v,
+    da_v,
+    do_v,
+    hid_v,
+    dqkv_v,
+    keep_v,
+    near_v,
+    vec_v,
+    k_flip,
+    dk_sum,
+    dv_sum,
+    slots2,
+    total2,
+    line2,
+    final2,
+    slots1,
+    total1,
+    line1,
+    final1,
+    pair_own,
+    pair_far,
+    slotsp,
+    totalp,
+    linep,
+    finalp,
+    gq_v,
+    slotsq,
+    totalq,
+    lineq,
+    finalq,
+    swap1,
+    swapq,
+    swapx,
+    send_sems,
+    recv_sems,
+    local_sems,
+    token_send,
+    token_recv,
+    home_send,
+    home_recv,
+):
+    at = Place(items)
+    chips, ranks, seq_ways = at.chips, at.ranks, at.seq_ways
+    own_rows, width = rgl.shape
+    tokens = own_rows // items
+    half = tokens // 2
+    shard = width // at.dp_ways
+    head_cols = heads.shape[1]
+    length = heads.shape[0]
+    pairs = head_cols // LANES
+    unit_rows = total2.shape[0]
+    copies = Copies(send_sems, recv_sems, local_sems)
+    at.meet()
+    other = at.chip * 2 + 1 - at.core
+    group = at.rank * 2 + at.core
+
+    first_loads = [copies.local(rgl, rgl_v.at[pl.ds(0, own_rows), :]), copies.local(wp, wp_v)]
+    share2 = Share(at, copies, slots2, total2, line2, final2)
+    share1 = Share(at, copies, slots1, total1, line1, final1)
+    sharep = Share(at, copies, slotsp, totalp, linep, finalp)
+    shareq = Share(at, copies, slotsq, totalq, lineq, finalq)
+    pair_rows = pair_own.shape[0]
+    pair_copy = copies.remote(gp.at[rows_at((1 - at.core) * pair_rows, pair_rows), :], pair_far, dp=other)
+    pair_load = copies.local(gp.at[rows_at(at.core * pair_rows, pair_rows), :], pair_own)
+
+    def block2(chip):
+        return g2.at[rows_at(chip * unit_rows, unit_rows), :]
+
+    def block1(chip):
+        return g1.at[rows_at(chip * 2 * shard, 2 * shard), :]
+
+    share2.spread(block2)
+    share1.spread(block1)
+    load2 = copies.local(block2(at.chip), total2)
+    load1 = copies.local(block1(at.chip), total1)
+    hidden_loads = [copies.local(img, img_v), copies.local(small, small_v)]
+    loads = [copies.local(prj, prj_v), copies.local(heads, heads_v), copies.local(wq, wq_v)]
+
+    for copy in first_loads:
+        copies.wait_local(copy)
+    jobs = []
+    for item in range(items):
+        rows = pl.ds(item * tokens, tokens)
+        da_v[rows, :] = dot(rgl_v[rows, :], wp_v[...], 1, 1).astype(bf16)
+        for k in range(ranks):
+            for h in range(2):
+                to_seq = (at.core * items + item) * ranks + k
+                mine = (to_seq == at.seq) & (at.core == h)
+                src = da_v.at[rows, pl.ds((k * 2 + h) * head_cols, head_cols)]
+                dst = do_v.at[rows_at(at.seq * tokens, tokens), :]
+                far = pltpu.make_async_remote_copy(
+                    src_ref=src,
+                    dst_ref=dst,
+                    send_sem=token_send.at[len(jobs)],
+                    recv_sem=token_recv.at[at.seq],
+                    device_id={"dp": at.chip * 2 + h, "seq": to_seq},
+                    device_id_type=pl.DeviceIdType.MESH,
+                )
+                near = pltpu.make_async_copy(src, dst, token_recv.at[at.seq])
+                pl.when(mine)(near.start)
+                pl.when(jnp.logical_not(mine))(far.start)
+                jobs.append((mine, far))
+
+    pair_copy.wait_recv()
+    copies.wait_local(pair_load)
+    step = 64
+
+    def add_pair(i, carry):
+        rows = rows_at(i * step, step)
+        pair_own[rows, :] = (pair_own[rows, :].astype(f32) + pair_far[rows, :].astype(f32)).astype(bf16)
+        return carry
+
+    lax.fori_loop(0, pair_rows // step, add_pair, 0)
+    block_p = pair_rows // chips
+    sharep.spread(lambda chip: pair_own.at[rows_at(chip * block_p, block_p), :])
+
+    def own_p(i, carry):
+        totalp[rows_at(i * 16, 16), :] = pair_own[rows_at(at.chip * block_p + i * 16, 16), :]
+        return carry
+
+    lax.fori_loop(0, block_p // 16, own_p, 0)
+
+    for copy in hidden_loads:
+        copies.wait_local(copy)
+    for row, start in ((0, 3), (1, 4)):
+        for i in range(at.dp_ways):
+            vec_v[row : row + 1, i * shard : (i + 1) * shard] = small_v[
+                8 * i : 8 * i + 1, start * shard : (start + 1) * shard
+            ]
+    gain = vec_v[0:1, :width]
+    shift = vec_v[1:2, :width]
+
+    def hide(s, carry):
+        rows = rows_at(s * tokens, tokens)
+        normed, _ = norm_stats(img_v[rows, :].astype(f32))
+        hid_v[rows, :] = (normed * gain + shift).astype(bf16)
+        return carry
+
+    lax.fori_loop(0, seq_ways, hide, 0)
+    for copy in loads:
+        copies.wait_local(copy)
+    for s in range(seq_ways):
+        pltpu.make_async_copy(
+            do_v.at[pl.ds(s * tokens, tokens), :], do_v.at[pl.ds(s * tokens, tokens), :], token_recv.at[s]
+        ).wait()
+    for mine, far in jobs:
+        pl.when(jnp.logical_not(mine))(far.wait_send)
+
+    rows_q = block_size(length)
+    vec_v[2:4, :] = jnp.zeros((2, vec_v.shape[1]), f32)
+    vec_v[4:5, :] = jnp.zeros((1, vec_v.shape[1]), f32)
+
+    def one_pair(pair, carry):
+        q_lanes = lanes_at(pair * LANES, LANES)
+        k_lanes = lanes_at((pairs + pair) * LANES, LANES)
+        v_lanes = lanes_at((2 * pairs + pair) * LANES, LANES)
+        k_flip[...] = transpose_low(prj_v[:, k_lanes])
+        dk_sum[...] = jnp.zeros_like(dk_sum)
+        dv_sum[...] = jnp.zeros_like(dv_sum)
+
+        def one_block(block, sums):
+            rows = rows_at(block * rows_q, rows_q)
+            query = prj_v[rows, q_lanes] * jnp.asarray(HEAD_DIM**-0.5, bf16)
+            key = prj_v[:, k_lanes]
+            value = prj_v[:, v_lanes]
+            grad = do_v[rows, q_lanes]
+            mixed = (grad.astype(f32) * heads_v[rows, q_lanes].astype(f32)).T
+            pieces = []
+            for head, mask in enumerate(pair_masks()):
+                span = slice(head * HEAD_DIM, (head + 1) * HEAD_DIM)
+                query_one = jnp.where(mask, query, jnp.zeros_like(query))
+                grad_one = jnp.where(mask, grad, jnp.zeros_like(grad))
+                probs = jnp.exp(dot(key, query_one, 1, 1) - lse[pair, head : head + 1, rows])
+                prob_grad = dot(value, grad_one, 1, 1)
+                delta = jnp.sum(mixed[span], axis=0, keepdims=True)
+                score_grad = (probs * (prob_grad - delta) * HEAD_DIM**-0.5).astype(bf16)
+                dv_sum[...] += dot(probs.astype(bf16), grad_one)
+                dk_sum[...] += dot(score_grad, query_one)
+                pieces.append(dot(k_flip[span, :], score_grad))
+            query_grad = jnp.concatenate(pieces, axis=0).T
+            dqkv_v[rows, q_lanes] = query_grad.astype(bf16)
+            return sums + jnp.sum(query_grad, axis=0, keepdims=True)
+
+        sums = lax.fori_loop(0, length // rows_q, one_block, jnp.zeros((1, LANES), f32))
+        dqkv_v[:, k_lanes] = (dk_sum[...] * HEAD_DIM**0.5).astype(bf16)
+        dqkv_v[:, v_lanes] = dv_sum[...].astype(bf16)
+        vec_v[4:5, lanes_at(group * head_cols + pair * LANES, LANES)] = sums
+        vec_v[4:5, lanes_at(width + group * head_cols + pair * LANES, LANES)] = jnp.sum(
+            dv_sum[...], axis=0, keepdims=True
+        )
+        return carry
+
+    lax.fori_loop(0, pairs // 2, one_pair, 0)
+    copies.wait_local(load2)
+    share2.add_chips()
+    lax.fori_loop(pairs // 2, pairs, one_pair, 0)
+    share2.add_line()
+    sharep.add_chips()
+
+    def widen(s, carry):
+        rows = rows_at(s * tokens, tokens)
+        partial = dot(dqkv_v[rows, :], wq_v[...], 1, 1)
+        normed, _ = norm_stats(img_v[rows, :].astype(f32))
+        vec_v[2:3, :width] += jnp.sum(partial * normed, axis=0, keepdims=True)
+        vec_v[3:4, :width] += jnp.sum(partial, axis=0, keepdims=True)
+        near_rows = rows_at(s * half, half)
+
+        @pl.when(at.core == 0)
+        def _():
+            keep_v[near_rows, :] = partial[:half]
+            da_v[near_rows, :] = partial[half:].astype(bf16)
+
+        @pl.when(at.core == 1)
+        def _():
+            keep_v[near_rows, :] = partial[half:]
+            da_v[near_rows, :] = partial[:half].astype(bf16)
+
+        return carry
+
+    lax.fori_loop(0, seq_ways, widen, 0)
+    near_rows = pl.ds(0, seq_ways * half)
+    near_copy = copies.remote(da_v.at[near_rows, :], near_v, dp=other)
+
+    span = 3 * head_cols
+    gq_cols = ranks * span
+    per_chip = width // chips
+    for q in range(chips):
+        block = pl.ds(q * 2 * shard, 2 * shard)
+        lanes = slice(q * 2 * shard, (q + 1) * 2 * shard)
+        if ranks > 1:
+            gq_v[block, :] = jnp.zeros((2 * shard, gq_v.shape[1]), bf16)
+        gq_v[block, lanes_at(at.rank * span, span)] = dot(hid_v[:, lanes], dqkv_v[...], 0, 0).astype(bf16)
+        rows = [vec_v[2:3, q * per_chip + i : q * per_chip + i + LANES] for i in range(0, per_chip, LANES)]
+        rows += [vec_v[3:4, q * per_chip + i : q * per_chip + i + LANES] for i in range(0, per_chip, LANES)]
+        rows += [
+            vec_v[4:5, 2 * q * per_chip + i : 2 * q * per_chip + i + LANES]
+            for i in range(0, 2 * per_chip, LANES)
+        ]
+        which = lax.broadcasted_iota(jnp.int32, (16, LANES), 0)
+        extra = jnp.zeros((16, LANES), f32)
+        for i, row in enumerate(rows):
+            extra = jnp.where(which == i, row, extra)
+        gq_v[pl.ds(q * 2 * shard + 16, 2 * shard - 16), gq_cols : gq_cols + LANES] = jnp.zeros(
+            (2 * shard - 16, LANES), bf16
+        )
+        gq_v[pl.ds(q * 2 * shard, 16), gq_cols : gq_cols + LANES] = extra.astype(bf16)
+    shareq.spread(lambda chip: gq_v.at[rows_at(chip * 2 * shard, 2 * shard), :])
+
+    def own_q(i, carry):
+        totalq[rows_at(i * 16, 16), :] = gq_v[rows_at(at.chip * 2 * shard + i * 16, 16), :]
+        return carry
+
+    lax.fori_loop(0, 2 * shard // 16, own_q, 0)
+
+    near_copy.wait_recv()
+    home_core = lax.div(at.item, items)
+    home_item = lax.rem(at.item, items)
+    home_jobs = []
+    for s in range(seq_ways):
+        rows = pl.ds(s * half, half)
+        rgl_v[rows, :] = (keep_v[rows, :] + near_v[rows, :].astype(f32)).astype(bf16)
+        mine = (at.seq == s) & (at.core == home_core)
+        dst = home_out.at[
+            rows_at(at.rank * own_rows + home_item * tokens + at.core * half, half), :
+        ]
+        far = pltpu.make_async_remote_copy(
+            src_ref=rgl_v.at[rows, :],
+            dst_ref=dst,
+            send_sem=home_send.at[s],
+            recv_sem=home_recv,
+            device_id={"dp": at.chip * 2 + home_core, "seq": s},
+            device_id_type=pl.DeviceIdType.MESH,
+        )
+        near = pltpu.make_async_copy(rgl_v.at[rows, :], dst, home_recv)
+        pl.when(mine)(near.start)
+        pl.when(jnp.logical_not(mine))(far.start)
+        home_jobs.append((mine, far))
+
+    sharep.add_line()
+    copies.wait_local(load1)
+    share1.add_chips()
+    shareq.add_chips()
+    share1.add_line()
+    shareq.add_line()
+    share2.arrive()
+    copies.local(final2, o2_out)
+    sharep.arrive()
+    copies.local(finalp, op_out)
+    share1.arrive()
+    theirs = rows_at((1 - at.core) * shard, shard)
+    ours = rows_at(at.core * shard, shard)
+    swap1_copy = copies.remote(final1.at[theirs, :], swap1, dp=other)
+    units = final1.shape[1] // chips
+    for q in range(chips):
+        cols = slice(q * units, (q + 1) * units)
+        o1_out[:, lanes_at((2 * q + at.core) * units, units)] = final1[ours, cols]
+    swap1_copy.wait_recv()
+    for q in range(chips):
+        cols = slice(q * units, (q + 1) * units)
+        o1_out[:, lanes_at((2 * q + 1 - at.core) * units, units)] = swap1[:, cols]
+    shareq.arrive()
+    swapq_copy = copies.remote(final1_rows(finalq, theirs), swapq, dp=other)
+    swapx_copy = copies.remote(finalq.at[pl.ds(0, 16), pl.ds(gq_cols, LANES)], swapx, dp=other)
+
+    def place_q(ref, rows, core):
+        for j in range(ranks):
+            for part in range(3):
+                oq_out[:, lanes_at(part * width + (j * 2 + core) * head_cols, head_cols)] = ref[
+                    rows, pl.ds(j * span + part * head_cols, head_cols)
+                ]
+
+    place_q(finalq, ours, at.core)
+    swapq_copy.wait_recv()
+    place_q(swapq, pl.ds(0, shard), 1 - at.core)
+    swapx_copy.wait_recv()
+    ox_out[...] = finalq[0:16, gq_cols : gq_cols + LANES].astype(f32) + swapx[...].astype(f32)
+    pltpu.make_async_copy(home_out, home_out, home_recv).wait()
+    for mine, far in home_jobs:
+        pl.when(jnp.logical_not(mine))(far.wait_send)
+    copies.finish()
+
+
+def final1_rows(ref, rows):
+    return ref.at[rows, :]
+
+
+def backward(items, rgl, wp, g2, g1, gp, prj, heads, img, wq, small, lse):
+    dp_ways, seq_ways = lax.axis_size("dp"), lax.axis_size("seq")
+    chips = dp_ways // 2
+    ranks = seq_ways // (2 * items)
+    own_rows, width = rgl.shape
+    shard = width // dp_ways
+    length, head_cols = heads.shape
+    tokens = own_rows // items
+    half = tokens // 2
+    unit_rows = g2.shape[0] // chips
+    units_half = g1.shape[1]
+    gp_rows, gp_cols = gp.shape
+    block_p = gp_rows // dp_ways
+    gq_cols = ranks * 3 * head_cols + LANES
+    stage_rows = max(own_rows, seq_ways * half)
+    any_spec = pl.BlockSpec(memory_space=pl.ANY)
+    vmem_spec = pl.BlockSpec(memory_space=pltpu.VMEM)
+    low = lambda *shape: pltpu.VMEM(shape, bf16)
+
+    def share(rows, cols):
+        return [
+            low(chips - 1, rows, cols),
+            low(rows, cols),
+            low(seq_ways - 1, rows // seq_ways, cols),
+            low(rows, cols),
+        ]
+
+    remotes = 96
+    return pl.pallas_call(
+        functools.partial(backward_kernel, items),
+        in_specs=[any_spec] * 10 + [vmem_spec],
+        out_specs=[any_spec] * 3 + [vmem_spec] * 3,
+        out_shape=[
+            jax.ShapeDtypeStruct((ranks * own_rows, width), bf16),
+            jax.ShapeDtypeStruct((unit_rows, width), bf16),
+            jax.ShapeDtypeStruct((block_p, gp_cols), bf16),
+            jax.ShapeDtypeStruct((shard, 2 * units_half), bf16),
+            jax.ShapeDtypeStruct((shard, 3 * width), bf16),
+            jax.ShapeDtypeStruct((16, LANES), f32),
+        ],
+        scratch_shapes=[
+            low(stage_rows, width),
+            low(width, width),
+            low(length, 3 * head_cols),
+            low(length, head_cols),
+            low(length, width),
+            low(width, 3 * head_cols),
+            pltpu.VMEM(small.shape, f32),
+            low(stage_rows, width),
+            low(length, head_cols),
+            low(length, width),
+            low(length, 3 * head_cols),
+            pltpu.VMEM((seq_ways * half, width), f32),
+            low(seq_ways * half, width),
+            pltpu.VMEM((8, 2 * width), f32),
+            low(LANES, length),
+            pltpu.VMEM((length, LANES), f32),
+            pltpu.VMEM((length, LANES), f32),
+            *share(unit_rows, width),
+            *share(2 * shard, units_half),
+            low(gp_rows // 2, gp_cols),
+            low(gp_rows // 2, gp_cols),
+            *share(block_p, gp_cols),
+            low(width, gq_cols),
+            *share(2 * shard, gq_cols),
+            low(shard, units_half),
+            low(shard, gq_cols),
+            low(16, LANES),
+            pltpu.SemaphoreType.DMA((remotes,)),
+            pltpu.SemaphoreType.DMA((remotes,)),
+            pltpu.SemaphoreType.DMA((32,)),
+            pltpu.SemaphoreType.DMA((2 * items * ranks,)),
+            pltpu.SemaphoreType.DMA((seq_ways,)),
+            pltpu.SemaphoreType.DMA((seq_ways,)),
+            pltpu.SemaphoreType.DMA,
+        ],
+        compiler_params=pltpu.CompilerParams(
+            collective_id=1, has_side_effects=True, vmem_limit_bytes=67043328
+        ),
+        name="backward",
+    )(rgl, wp, g2, g1, gp, prj, heads, img, wq, small, lse)
+
+
 def body(
     images,
     qkv_weight,
@@ -733,6 +1233,7 @@
         cotangent_own,
         jnp.broadcast_to(small, (8, small.shape[0])),
     )
+    small_all = small
     small = small.reshape(dp_ways, 8, -1)[:, 0]
     smalls, at = [], 0
     for array in small_names:
@@ -740,9 +1241,6 @@
         at += array.shape[0]
     _, bias_proj, gain_first, shift_first, gain_second, shift_second, bias_one, bias_two = smalls
     bias_one_half = pick(bias_one.reshape(chips, 2, -1), core, 1).reshape(-1)
-    normed_image, _ = norm_stats(image_low.astype(f32))
-    hidden_first = (normed_image * gain_first + shift_first).astype(bf16)
-
     flat_rows = images.reshape(own_rows, width).astype(f32)
     residual_first = flat_rows + dot(attended_rows, proj_full) + bias_proj
     normed_second, inv_second = norm_stats(residual_first)
@@ -770,14 +1268,6 @@
     )
     residual_grad_low = residual_grad.astype(bf16)
     grad_proj_bias = jnp.sum(residual_grad, axis=0)
-    attended_grad = dot(residual_grad_low, proj_full, 1, 1).astype(bf16)
-    attended_grad = attended_grad.reshape(items, tokens, ranks, 2, head_cols)
-    mine = by_core(
-        pick(attended_grad, core, 3), swap(pick(attended_grad, 1 - core, 3)), 0
-    ).reshape(column_items, tokens, ranks, head_cols)
-    mine = jnp.moveaxis(mine, 2, 1).reshape(seq_ways, tokens, head_cols)
-    grad_heads = lax.all_to_all(mine, "seq", 0, 0).reshape(length, head_cols)
-
     grad_fc_two = dot(acts, cotangent_all, 0, 0).astype(bf16)
     grad_fc_one = dot(hidden_second, pre_grad_low, 0, 0).astype(bf16)
     grad_proj = dot(attended_rows, residual_grad_low, 0, 0).astype(bf16)
@@ -789,6 +1279,12 @@
     one_all = jnp.where(
         jnp.arange(2)[None, :, None] == core, jnp.broadcast_to(one_parts, (chips, 2, one_parts.shape[2])), 0.0
     )
+    block_rows = -(-shard_rows // (16 * seq_ways)) * 16 * seq_ways
+
+    def by_owner(array):
+        array = array.reshape((chips, 2) + array.shape[1:])
+        return jnp.moveaxis(array, 1, 0)
+
     extra = jnp.concatenate(
         [
             shares(grad_proj_bias),
@@ -798,86 +1294,40 @@
             shares(one_all),
         ],
         axis=1,
-    ).astype(bf16)
-    extra = jnp.pad(extra[:, None, :], ((0, 0), (0, 15), (0, width - extra.shape[1])))
-    proj_blocks = jnp.concatenate([grad_proj.reshape(dp_ways, shard_rows, width), extra], axis=1)
-
-    share_two = scatter_chips(grad_fc_two.reshape(chips, -1, width))
-    share_one = scatter_chips(grad_fc_one.reshape(chips, 2 * shard_rows, -1))
-    share_proj = lax.psum_scatter(proj_blocks, "dp", scatter_dimension=0, tiled=True)[0]
-    share_two = lax.psum(share_two, "seq")
-    share_one, share_two = lax.optimization_barrier((share_one, share_two))
-    share_one = lax.psum(share_one, "seq")
-    share_proj, share_one = lax.optimization_barrier((share_proj, share_one))
-    share_proj = lax.psum(share_proj, "seq")
-
-    qkv_grad, bias_sums = attend_back(projected, attended, log_total, grad_heads)
-    hidden_partial = dot(qkv_grad, qkv_full, 1, 1)
-    grad_gain_first = jnp.sum(hidden_partial * normed_image, axis=0)
-    grad_shift_first = jnp.sum(hidden_partial, axis=0)
-    partial_parts = hidden_partial.reshape(seq_ways, 2, half, width)
-    chip_sum = pick(partial_parts, core, 1) + swap(
-        pick(partial_parts, 1 - core, 1).astype(bf16)
-    ).astype(f32)
-    home = lax.all_to_all(chip_sum.astype(bf16), "seq", 0, 0)
-    home = home.reshape(2, items, ranks, half, width)
-    if ranks > 1:
-        home = jnp.sum(home.astype(f32), axis=2, keepdims=True).astype(bf16)
-    home = home[:, :, 0]
-    hidden_first_grad = by_core(pick(home, core, 0), swap(pick(home, 1 - core, 0)), 1)
-    hidden_first_grad = hidden_first_grad.reshape(own_rows, width).astype(f32)
+    )
+    extra = extra.reshape(dp_ways, -1, LANES).astype(bf16)
+    extra_rows = extra.shape[1]
+    extra = jnp.pad(extra, ((0, 0), (0, shard_rows - extra_rows), (0, 0)))
+    blocks = jnp.concatenate([grad_proj.reshape(dp_ways, shard_rows, width), extra], axis=2)
+    blocks = jnp.pad(blocks, ((0, 0), (0, block_rows - shard_rows), (0, 0)))
+    blocks = by_owner(blocks).reshape(dp_ways * block_rows, width + LANES)
+
+    home, share_two, share_proj, out_one, out_qkv, first_sums = backward(
+        items,
+        residual_grad_low,
+        proj_full,
+        grad_fc_two,
+        grad_fc_one,
+        blocks,
+        projected,
+        attended,
+        image_low,
+        qkv_full,
+        small_all,
+        log_total,
+    )
+    home = home.reshape(ranks, own_rows, width).astype(f32)
+    hidden_first_grad = jnp.sum(home, axis=0) if ranks > 1 else home[0]
     normed_first, inv_first = norm_stats(flat_rows)
     image_grad = residual_grad + norm_backward(
         hidden_first_grad, normed_first, inv_first, gain_first
     )
-
-    grad_qkv = dot(hidden_first, qkv_grad, 0, 0).astype(bf16)
-    grad_qkv = grad_qkv.reshape(chips, 2 * shard_rows, 3, 1, head_cols)
-    qv_sums = jnp.moveaxis(bias_sums, 1, 0).reshape(2, 1, head_cols)
-    qv_all = lax.dynamic_update_slice(jnp.zeros((2, groups, head_cols), f32), qv_sums, (0, group, 0))
-    extra = jnp.concatenate(
-        [
-            grad_gain_first.reshape(chips, -1),
-            grad_shift_first.reshape(chips, -1),
-            qv_all.reshape(chips, -1),
-        ],
-        axis=1,
-    ).astype(bf16)
-    extra_cols = extra.shape[1]
-    extra = jnp.pad(extra[:, None, :], ((0, 0), (0, 15), (0, 3 * head_cols - extra_cols)))
-    blocks = jnp.concatenate(
-        [grad_qkv.reshape(chips, 2 * shard_rows, 3 * head_cols), extra], axis=1
-    )
-    share_qkv = scatter_chips(blocks)
-    extra = share_qkv[2 * shard_rows, :extra_cols]
-    share_qkv = share_qkv[: 2 * shard_rows].reshape(2 * shard_rows, 3, 1, head_cols)
-    if ranks > 1:
-        share_qkv = lax.dynamic_update_slice(
-            jnp.zeros((2 * shard_rows, 3, ranks, head_cols), bf16), share_qkv, (0, 0, rank, 0)
-        )
-    flat = jnp.concatenate(
-        [
-            share_qkv.reshape(2 * shard_rows, -1),
-            jnp.pad(extra[None], ((0, 15), (0, ranks * 3 * head_cols - extra_cols))),
-        ],
-        axis=0,
-    )
-    flat, share_proj = lax.optimization_barrier((flat, share_proj))
-    flat = lax.psum(flat, "seq")
-    rows_parts = flat[: 2 * shard_rows].reshape(2, shard_rows, 3, ranks, head_cols)
-    extra = flat[2 * shard_rows : 2 * shard_rows + 1]
-    out_qkv = by_core(pick(rows_parts, core, 0), swap(pick(rows_parts, 1 - core, 0)), 3)
-    out_qkv = out_qkv.reshape(shard_rows, 3 * width).astype(f32)
-    extra = (extra.astype(f32) + swap(extra).astype(f32))[0]
-    per_chip = width // chips
-    out_gain_first = pick(extra[:per_chip].reshape(2, -1), core, 0)
-    out_shift_first = pick(extra[per_chip : 2 * per_chip].reshape(2, -1), core, 0)
-    out_qv = pick(extra[2 * per_chip : 4 * per_chip].reshape(2, -1), core, 0)
-
-    one_rows = share_one.reshape(2, shard_rows, chips, -1)
-    out_one = by_core(pick(one_rows, core, 0), swap(pick(one_rows, 1 - core, 0)), 2)
-    out_one = out_one.reshape(shard_rows, -1).astype(f32)
-    last = share_proj[shard_rows].astype(f32)
+    per_chip = 2 * shard_rows
+    first_sums = first_sums.reshape(-1)
+    out_gain_first = pick(first_sums[:per_chip].reshape(2, -1), core, 0)
+    out_shift_first = pick(first_sums[per_chip : 2 * per_chip].reshape(2, -1), core, 0)
+    out_qv = pick(first_sums[2 * per_chip : 4 * per_chip].reshape(2, -1), core, 0)
+    last = share_proj[:extra_rows, width:].reshape(-1).astype(f32)
     out_smalls, at = [], 0
     for size in (shard_rows, shard_rows, shard_rows, shard_rows, 4 * shard_rows):
         out_smalls.append(last[at : at + size])
@@ -885,15 +1335,15 @@
     return (
         output.reshape(images.shape),
         image_grad.reshape(images.shape),
-        out_qkv,
+        out_qkv.astype(f32),
         out_qv,
-        share_proj[:shard_rows].astype(f32),
+        share_proj[:shard_rows, :width].astype(f32),
         out_smalls[0],
         out_gain_first,
         out_shift_first,
         out_smalls[1],
         out_smalls[2],
-        out_one,
+        out_one.astype(f32),
         out_smalls[4],
         share_two.astype(f32),
         out_smalls[3],

time: 634 us -> 470 us (0.74)
  the two profiles are of different devices: /device:TPU:0 before, /device:TPU:11 now
where the time goes in v3:
time: 470 us; the launch traced here: 461 us
  Pallas kernels  353 us (75%)
  matrix products  49.7 us (11%)
  local copies, waits for them, and re-layouts  30.5 us (6%)
  other arithmetic  26.4 us (6%)
    pallas_call x1, Pallas kernels, backward(): pl.pallas_call(functools.partial(backward_kernel, items), in_specs=[any_s...  238 us
    pallas_call x1, Pallas kernels, forward(): pl.pallas_call(functools.partial(forward_kernel, items), in_specs=[any_sp...  115 us
    dot_general x8, matrix products, dot(): lax.dot_general(left, right, (((left_dim,), (right_dim,)), ((), ())), pre...  49.7 us
    unnamed x59, local copies, waits for them, and re-layouts  9.86 us
  transfers between devices with their start and end apart: 3, of which 0 were waited for; matrix products, arithmetic and copies ran while one was open for 6% of the time, Pallas kernels for 0%

profile of v3, /device:TPU:11, one launch (start us, length us, event | category | flops | bytes accessed | tf_op | source)
XLA Modules:
  0.0 461.2 jit_solution(2654228556200543795)
XLA Ops:
  0.7 0.9 dynamic-update-slice.5
  1.5 0.8 dynamic-update-slice.6
  2.3 0.8 dynamic-update-slice.7
  3.2 0.8 dynamic-update-slice.8
  4.0 0.8 dynamic-update-slice.9
  4.8 0.8 dynamic-update-slice.10
  5.7 0.9 dynamic-update-slice.11
  6.5 0.8 dynamic-update-slice.12
  7.4 0.6 broadcast_in_dim.37.small
  8.0 115.0 %forward.1 = (bf16[1152,1024]{1,0:T(8,128)(2,1)}, bf16[1024,1536]{1,0:T(8,128)(2,1)}, bf16[1024,1024]{1,0:T(8,128)(2,1)}, bf16[1024,2048]{1,0:T(8,128)(2,1)}, bf...) custom-call(bf16[576,1024]{1,0:T(8,128)(2,1)} %bitcast.89, ...), custom_call_target="tpu_custom_call" | custom-call | tf_op jit(solution)/shard_map/forward/pallas_call | solution.py:619
  123.0 1.0 slice.91
  124.0 0.6 slice_bitcast_fusion
  124.6 3.5 fusion.26
  128.1 0.4 multiply_reduce_fusion.2
  128.5 1.5 add_convert_fusion
  130.0 0.6 slice.95
  130.6 0.5 iota_compare_fusion
  131.1 1.3 reshape_reshape.3
  132.4 2.1 reduce.3
  134.5 1.2 broadcast_in_dim.38
  135.7 1.2 broadcast_in_dim.39
  137.1 0.6 broadcast_multiply_fusion.5
  137.7 1.3 div.33
  139.1 1.1 fusion.13
  140.2 0.7 rsqrt.21
  140.9 0.7 constant_dynamic-slice_fusion.3
  141.6 0.4 fusion.45
  142.1 2.1 maximum_select_fusion
  144.2 0.8 copy-done.19
  145.0 8.4 %multiply_convert_fusion = (bf16[1152,2048]{1,0:T(8,128)(2,1)S(1)}, f32[1152,2048]{1,0:T(8,128)}) fusion(f32[2048]{0:T(1024)S(1)} %bitcast.109, bf16[1152,1024]{1,0:T(8,128)(2,1)S(1)} %bitcast.100, bf16[1024,2048]{1,0:T(8,128)(2,1)S(1)} %copy-done.19), kind=kOutput, calls=%fused_computation.6 | convolution fusion | flops 4845993984 | bytes 20717568 | tf_op jit(solution)/shard_map/dot_general | solution.py:43
  153.4 5.1 %fusion.28 = f32[1152,1024]{1,0:T(8,128)S(1)} fusion(bf16[1152,2048]{1,0:T(8,128)(2,1)S(1)} %get-tuple-element.71, bf16[2048,1024]{1,0:T(8,128)(2,1)S(1)} %copy-done.20), kind=kOutput, calls=%fused_computation.87 | convolution fusion | flops 4831838208 | bytes 13631488 | tf_op jit(solution)/shard_map/dot_general | solution.py:43
  158.6 7.4 %convolution_convert_fusion.1.g2 = bf16[2048,1024]{1,0:T(8,128)(2,1)} fusion(bf16[1152,2048]{1,0:T(8,128)(2,1)S(1)} %get-tuple-element.71, bf16[1152,1024]{1,0:T(8,128)(2,1)S(1)} %copy-done.21), kind=kOutput, calls=%fused_computation.10 | convolution fusion | flops 4833935360 | bytes 11272192 | tf_op jit(solution)/shard_map/dot_general | solution.py:43
  165.9 10.5 %fusion.27 = (bf16[2048]{0:T(1024)(128)(2,1)}, bf16[1152,2048]{1,0:T(8,128)(2,1)S(1)}) fusion(f32[1152,2048]{1,0:T(8,128)} %get-tuple-element.72, bf16[1152,1024]{1,0:T(8,128)(2,1)S(1)} %copy-done.21, bf16[2048,1024]{1,0:T(8,128)(2,1)S(1)} %copy-done.20), kind=kOutput, calls=%fused_computation.86 | convolution fusion | flops 4857788416 | bytes 20713472 | tf_op jit(solution)/shard_map/dot_general | solution.py:43
  176.5 5.2 %fusion.18 = f32[1152,1024]{1,0:T(8,128)S(1)} fusion(bf16[1024,2048]{1,0:T(8,128)(2,1)S(1)} %copy-done.19, bf16[1152,2048]{1,0:T(8,128)(2,1)S(1)} %get-tuple-element.74), kind=kOutput, calls=%fused_computation.38 | convolution fusion | flops 4831838208 | bytes 13631488 | tf_op jit(solution)/shard_map/dot_general | solution.py:43
  181.6 1.3 fusion.21
  183.0 0.5 collective-permute-start.2
  183.5 1.2 fusion.20
  184.7 0.4 collective-permute-start.1
  185.0 7.8 %convolution_convert_fusion.g1 = bf16[1024,2048]{1,0:T(8,128)(2,1)} fusion(bf16[1152,1024]{1,0:T(8,128)(2,1)S(1)} %bitcast.101, bf16[1152,2048]{1,0:T(8,128)(2,1)S(1)} %get-tuple-element.74), kind=kOutput, calls=%fused_computation.9 | convolution fusion | flops 4833935360 | bytes 11272192 | tf_op jit(solution)/shard_map/dot_general | solution.py:43
  192.9 0.7 broadcast_in_dim.41
  193.6 0.6 broadcast_in_dim.42
  194.2 1.3 broadcast_in_dim.43
  195.5 3.3 multiply_reduce_fusion
  198.8 0.4 copy-done.8
  199.2 2.3 fusion.24
  201.8 0.4 copy-done.17
  202.5 1.4 copy-done.22
  203.9 1.8 convolution_convert_fusion.2
  206.0 1.6 copy.31
  207.6 237.6 %backward.1 = (bf16[576,1024]{1,0:T(8,128)(2,1)}, bf16[512,1024]{1,0:T(8,128)(2,1)}, bf16[128,1152]{1,0:T(8,128)(2,1)}, bf16[128,4096]{1,0:T(8,128)(2,1)}, bf16[128,3072]{1,0:T(8,128)(2,1)}, /*index=5*/f32[16,128]{1,0:T(8,128)}) custom-call(bf16[576,1024]{1,0:T(8,128)(2,1)} %copy-done.5, bf16[1024,1024]{1,0:T(8,128)(2,1)} %get-tuple-element.32.wp, ...), custom_call_target="tpu_custom_call" | custom-call | tf_op jit(solution)/shard_map/backward/pallas_call | solution.py:1089
  445.2 1.9 slice_convert_fusion
  447.1 0.7 slice_convert_fusion.1
  447.8 0.7 slice.76
  448.4 0.8 fusion.25
  449.2 0.5 slice_bitcast_fusion.6
  449.7 0.6 slice_bitcast_fusion.5
  450.3 2.5 convert_element_type.101
  452.8 0.6 constant_dynamic-slice_fusion.2
  453.4 1.5 convert_element_type.104
  455.0 1.6 convert_element_type.105
  456.5 0.8 copy-done.6
  457.3 0.9 fusion.16
  458.2 2.3 fusion.11
  460.5 0.5 fusion.22
  (64 shorter events, 1.0 us)
Async XLA Ops:
  8.0 116.6 %copy-start = (bf16[2,288,1024]{2,1,0:T(8,128)(2,1)S(1)}, bf16[2,288,1024]{2,1,0:T(8,128)(2,1)}, u32[]{:S(2)}) copy-start(bf16[2,288,1024]{2,1,0:T(8,128)(2,1)} %param.14) | copy-start | bytes 3538948
  130.0 12.1 %collective-permute-start = (bf16[576,1024]{1,0:T(8,128)(2,1)}, bf16[576,1024]{1,0:T(8,128)(2,1)}, u32[]{:S(2)}, u32[]{:S(2)}) collective-permute-start(bf16[576,1024]{1,0:T(8,128)(2,1)} %add_convert_fusion), channel_id=1, source_target_pairs={{0,4},{4,0},{8,12},{12,8},{16,20},{20,16},{24,28},{28,24},{1,5},{5... | collective-permute-start | bytes 3538952 | tf_op jit(solution)/shard_map/ppermute | solution.py:1179
  142.1 2.9 copy-start.19
  145.0 8.4 %copy-start.20 = (bf16[2048,1024]{1,0:T(8,128)(2,1)S(1)}, bf16[2048,1024]{1,0:T(8,128)(2,1)}, u32[]{:S(2)}) copy-start(bf16[2048,1024]{1,0:T(8,128)(2,1)} %get-tuple-element.35) | copy-start | bytes 12582916
  153.4 5.2 %copy-start.21 = (bf16[1152,1024]{1,0:T(8,128)(2,1)S(1)}, bf16[1152,1024]{1,0:T(8,128)(2,1)}, u32[]{:S(2)}) copy-start(bf16[1152,1024]{1,0:T(8,128)(2,1)} %get-tuple-element.36) | copy-start | bytes 7077892
  158.5 24.9 %copy-start.7 = (f32[1152,1024]{1,0:T(8,128)}, f32[1152,1024]{1,0:T(8,128)S(1)}, u32[]{:S(2)}) copy-start(f32[1152,1024]{1,0:T(8,128)S(1)} %fusion.28) | copy-start | bytes 14155780
  181.6 3.0 copy-start.9
  183.0 12.5 %collective-permute-start.2 = (bf16[576,1024]{1,0:T(8,128)(2,1)}, bf16[576,1024]{1,0:T(8,128)(2,1)}, u32[]{:S(2)}, u32[]{:S(2)}) collective-permute-start(bf16[576,1024]{1,0:T(8,128)(2,1)} %fusion.21), channel_id=1, source_target_pairs={{0,4},{4,0},{8,12},{12,8},{16,20},{20,16},{24,28},{28,24},{1,5},{5... | collective-permute-start | bytes 3538952 | tf_op jit(solution)/shard_map/ppermute | solution.py:1179
  184.7 14.1 %collective-permute-start.1 = (bf16[576,1024]{1,0:T(8,128)(2,1)}, bf16[576,1024]{1,0:T(8,128)(2,1)S(1)}, u32[]{:S(2)}, u32[]{:S(2)}) collective-permute-start(bf16[576,1024]{1,0:T(8,128)(2,1)} %fusion.20), channel_id=1, source_target_pairs={{0,4},{4,0},{8,12},{12,8},{16,20},{20,16},{24,28},{28,24},{1,5},{5... | collective-permute-start | bytes 3538952 | tf_op jit(solution)/shard_map/ppermute | solution.py:1179
  195.5 3.3 copy-start.4
  195.5 3.8 copy-start.8
  195.5 3.8 copy-start.16
  201.6 4.1 copy-start.2
  201.6 0.7 copy-start.17
  201.6 0.8 copy-start.15
  201.6 0.8 copy-start.18
  201.6 2.3 copy-start.22
  201.8 4.0 copy-start.5
  445.2 8.2 %copy-start.11 = (bf16[128,4096]{1,0:T(8,128)(2,1)S(1)}, bf16[128,4096]{1,0:T(8,128)(2,1)}, u32[]{:S(2)}) copy-start(bf16[128,4096]{1,0:T(8,128)(2,1)} %get-tuple-element.46) | copy-start | bytes 3145732
  450.3 4.7 %copy-start.10 = (bf16[512,1024]{1,0:T(8,128)(2,1)S(1)}, bf16[512,1024]{1,0:T(8,128)(2,1)}, u32[]{:S(2)}) copy-start(bf16[512,1024]{1,0:T(8,128)(2,1)} %get-tuple-element.47) | copy-start | bytes 3145732
  454.9 1.6 copy-start.1
  454.9 2.4 copy-start.6
  454.9 2.4 copy-start.12
  454.9 2.4 copy-start.13
  454.9 2.4 copy-start.14
  455.0 3.2 copy-start.3

commit v4 on v3

--- a/solution.py
+++ b/solution.py
@@ -202,6 +202,11 @@
         self.sent, self.locals, self.local_count = [], [], 0
 
     def remote(self, src, dst, **device):
+        copy = self.prepare(src, dst, **device)
+        copy.start()
+        return copy
+
+    def prepare(self, src, dst, **device):
         at = len(self.sent)
         copy = pltpu.make_async_remote_copy(
             src_ref=src,
@@ -211,14 +216,17 @@
             device_id=device,
             device_id_type=pl.DeviceIdType.MESH,
         )
-        copy.start()
         self.sent.append(copy)
         return copy
 
     def local(self, src, dst):
-        copy = pltpu.make_async_copy(src, dst, self.local_sems.at[self.local_count])
+        copy = self.prepare_local(src, dst)
         copy.start()
         self.locals.append(copy)
+        return copy
+
+    def prepare_local(self, src, dst):
+        copy = pltpu.make_async_copy(src, dst, self.local_sems.at[self.local_count])
         self.local_count += 1
         return copy
 
@@ -326,6 +334,10 @@
     heads_out,
     lse_out,
     rows_out,
+    res_out,
+    hid_out,
+    pre_out,
+    acts_out,
     img_v,
     wq_v,
     prj_v,
@@ -333,10 +345,17 @@
     small_v,
     vec_v,
     v_flip,
+    wp_v,
+    w1_v,
+    rows_v,
+    own_v,
+    res_v,
+    hid_v,
+    pre_v,
+    acts_v,
     send_sems,
     recv_sems,
     local_sems,
-    swap_sems,
     token_send,
     token_recv,
     back_send,
@@ -381,7 +400,7 @@
 
     other = at.chip * 2 + 1 - at.core
     small_copies = []
-    small_rows = pl.ds(pl.multiple_of(at.dp * 8, 8), 8)
+    small_rows = rows_at(at.dp * 16, 16)
     small_own = copies.local(small, small_v.at[small_rows, :])
     for step in range(1, dp_ways):
         small_copies.append(
@@ -402,7 +421,7 @@
         return [
             (
                 w1.at[:, lanes_at((2 * q + core) * unit_rows, unit_rows)],
-                w1_out.at[me, pl.ds(q * unit_rows, unit_rows)],
+                w1_v.at[me, pl.ds(q * unit_rows, unit_rows)],
             )
             for q in range(chips)
         ]
@@ -447,10 +466,11 @@
 
     qkv_arrivals = start_columns(qkv_pieces)
 
-    wp_near = [copies.remote(wp, wp_out.at[me, :], dp=other)]
-    copies.local(wp, wp_out.at[me, :])
+    wp_near = [copies.remote(wp, wp_v.at[me, :], dp=other)]
+    wp_own = copies.local(wp, wp_v.at[me, :])
+    own_copy = copies.local(img, own_v)
     wp_far = {
-        o: [copies.remote(wp, wp_out.at[me, :], dp=at.partner(o) * 2 + at.core)] for o in offsets
+        o: [copies.remote(wp, wp_v.at[me, :], dp=at.partner(o) * 2 + at.core)] for o in offsets
     }
     cot_rows = rows_at(at.core * cot.shape[0], cot.shape[0])
     cot_near = copies.remote(cot, cot_out.at[cot_rows, :], dp=other)
@@ -479,12 +499,17 @@
     for copy in small_copies:
         copy.wait_recv()
     copies.wait_local(small_own)
-    names = {"query": (0, 2), "gain": (3, 1), "shift": (4, 1)}
-    for row, (start, size) in enumerate(names.values()):
+    for row, start, size in ((0, 0, 2), (1, 3, 1), (2, 4, 1), (4, 2, 1), (5, 5, 1), (6, 6, 1)):
         for i in range(dp_ways):
-            vec_v[row : row + 1, i * size * shard : (i + 1) * size * shard] = small_v[
-                8 * i : 8 * i + 1, start * shard : (start + size) * shard
-            ]
+            for j in range(size):
+                lane = (i * size + j) * shard
+                line = 16 * i + start + j
+                vec_v[row : row + 1, lane : lane + shard] = small_v[line : line + 1, :shard]
+    for q in range(chips):
+        for j in range(4):
+            lane = (q * 4 + j) * shard
+            line = pl.ds((2 * q + at.core) * 16 + 7 + j, 1)
+            vec_v[3:4, lane : lane + shard] = small_v[line, :shard]
     for copy in token_near:
         copy.wait_recv()
     settle(qkv_arrivals, qkv_last)
@@ -523,7 +548,7 @@
         for s in range(seq_ways):
             mine = (at.seq == s) & (at.core == home_core)
             src = heads_v.at[pl.ds(s * tokens, tokens), lanes_at(pair * LANES, LANES)]
-            dst = rows_out.at[
+            dst = rows_v.at[
                 rows_at(home_item * tokens, tokens),
                 lanes_at(group * head_cols + pair * LANES, LANES),
             ]
@@ -556,17 +581,17 @@
     copies.local(heads_v, heads_out)
     wp_last = pass_on(
         wp_far,
-        lambda chip, start, size: wp_out.at[
+        lambda chip, start, size: wp_v.at[
             rows_at((chip * 2 + at.core) * shard + start, size), :
         ],
         (0, shard // 2),
         (shard // 2, shard // 2),
     )
-    fc1_last = pass_on(fc1_arrivals, shard_halves(w1_out), (0, shard), (shard, shard))
+    fc1_last = pass_on(fc1_arrivals, shard_halves(w1_v), (0, shard), (shard, shard))
     for copy in wp_last:
         copy.wait_recv()
     for offset in range(1, chips):
-        ref = wp_out.at[rows_at((at.source(offset) * 2 + at.core) * shard, shard), :]
+        ref = wp_v.at[rows_at((at.source(offset) * 2 + at.core) * shard, shard), :]
         wp_near.append(copies.remote(ref, ref, dp=other))
     fc2_last = pass_on(
         fc2_arrivals,
@@ -574,12 +599,47 @@
         (0, unit_rows // 2),
         (unit_rows // 2, unit_rows // 2),
     )
-    settle(fc1_arrivals, fc1_last)
-    settle(fc2_arrivals, fc2_last)
     for copy in wp_near:
         copy.wait_recv()
+    copies.wait_local(wp_own)
+    copies.local(wp_v, wp_out)
+    copies.wait_local(own_copy)
+    pltpu.make_async_copy(rows_v, rows_v, back_recv).wait()
+    copies.local(rows_v, rows_out)
+    own_rows = rows_v.shape[0]
+
+    def rejoin(item, carry):
+        rows = rows_at(item * tokens, tokens)
+        residual = own_v[rows, :].astype(f32) + dot(rows_v[rows, :], wp_v[...]) + vec_v[4:5, :width]
+        res_v[rows, :] = residual
+        normed, _ = norm_stats(residual)
+        hidden = normed * vec_v[5:6, :width] + vec_v[6:7, :width]
+        hid_v[rows_at(at.core * own_rows + item * tokens, tokens), :] = hidden.astype(bf16)
+        return carry
+
+    lax.fori_loop(0, items, rejoin, 0)
+    hid_own = hid_v.at[rows_at(at.core * own_rows, own_rows), :]
+    hid_near = copies.remote(hid_own, hid_own, dp=other)
+    copies.local(res_v, res_out)
+    settle(fc1_arrivals, fc1_last)
+    for copy in fc1_arrivals["local"]:
+        copies.wait_local(copy)
+    copies.local(w1_v, w1_out)
+    hid_near.wait_recv()
+    copies.local(hid_v, hid_out)
+
+    def widen(step, carry):
+        rows = rows_at(step * tokens, tokens)
+        pre_act = dot(hid_v[rows, :], w1_v[...]) + vec_v[3:4, : w1_v.shape[1]]
+        pre_v[rows, :] = pre_act
+        acts_v[rows, :] = (pre_act * gelu_cdf(pre_act)).astype(bf16)
+        return carry
+
+    lax.fori_loop(0, 2 * items, widen, 0)
+    copies.local(pre_v, pre_out)
+    copies.local(acts_v, acts_out)
+    settle(fc2_arrivals, fc2_last)
     cot_near.wait_recv()
-    pltpu.make_async_copy(rows_out, rows_out, back_recv).wait()
 
     def drain(pair, carry):
         for mine, far, _ in back_copies(pair):
@@ -607,11 +667,15 @@
         jax.ShapeDtypeStruct((width, half_units), bf16),
         jax.ShapeDtypeStruct((half_units, width), bf16),
         jax.ShapeDtypeStruct((2 * cot.shape[0], width), bf16),
-        jax.ShapeDtypeStruct((8 * dp_ways, small.shape[1]), f32),
+        jax.ShapeDtypeStruct((16 * dp_ways, small.shape[1]), f32),
         jax.ShapeDtypeStruct((length, 3 * head_cols), bf16),
         jax.ShapeDtypeStruct((length, head_cols), bf16),
         jax.ShapeDtypeStruct((pairs, 2, length), f32),
         jax.ShapeDtypeStruct(img.shape, bf16),
+        jax.ShapeDtypeStruct(img.shape, f32),
+        jax.ShapeDtypeStruct((2 * img.shape[0], width), bf16),
+        jax.ShapeDtypeStruct((2 * img.shape[0], half_units), f32),
+        jax.ShapeDtypeStruct((2 * img.shape[0], half_units), bf16),
     ]
     out_specs = [any_spec] * len(out_shape)
     out_specs[9] = pl.BlockSpec(memory_space=pltpu.VMEM)
@@ -626,85 +690,183 @@
             pltpu.VMEM((width, 3 * head_cols), bf16),
             pltpu.VMEM((length, 3 * head_cols), bf16),
             pltpu.VMEM((length, head_cols), bf16),
-            pltpu.VMEM((8 * dp_ways, small.shape[1]), f32),
+            pltpu.VMEM((16 * dp_ways, small.shape[1]), f32),
             pltpu.VMEM((8, 2 * width), f32),
             pltpu.VMEM((LANES, length), bf16),
+            pltpu.VMEM((width, width), bf16),
+            pltpu.VMEM((width, half_units), bf16),
+            pltpu.VMEM(img.shape, bf16),
+            pltpu.VMEM(img.shape, bf16),
+            pltpu.VMEM(img.shape, f32),
+            pltpu.VMEM((2 * img.shape[0], width), bf16),
+            pltpu.VMEM((2 * img.shape[0], half_units), f32),
+            pltpu.VMEM((2 * img.shape[0], half_units), bf16),
             pltpu.SemaphoreType.DMA((remotes,)),
             pltpu.SemaphoreType.DMA((remotes,)),
-            pltpu.SemaphoreType.DMA((32,)),
-            pltpu.SemaphoreType.DMA((2,)),
+            pltpu.SemaphoreType.DMA((40,)),
             pltpu.SemaphoreType.DMA((2 * items * ranks,)),
             pltpu.SemaphoreType.DMA((seq_ways,)),
             pltpu.SemaphoreType.DMA((pairs, seq_ways)),
             pltpu.SemaphoreType.DMA,
         ],
         compiler_params=pltpu.CompilerParams(
-            collective_id=0, has_side_effects=True, vmem_limit_bytes=62 * 2**20
+            collective_id=0, has_side_effects=True, vmem_limit_bytes=67043328
         ),
         name="forward",
     )(img, wq, wp, w1, w2, cot, small)
 
 
 class Share:
-    def __init__(self, at, copies, slots, total, line, final):
-        self.at, self.copies = at, copies
+    def __init__(self, at, copies, block_of, slots, total, line, final):
+        self.at = at
         self.slots, self.total, self.line, self.final = slots, total, line, final
-        self.part = total.shape[0] // at.seq_ways
-
-    def spread(self, block_of):
-        at = self.at
-        self.arrivals = [
-            self.copies.remote(
-                block_of(at.partner(offset)),
-                self.slots.at[offset - 1],
-                dp=at.partner(offset) * 2 + at.core,
+        rows = total.shape[0]
+        mid = rows // 2
+        self.mid = mid
+        self.relays = at.chips == 4
+        low, high = pl.ds(0, mid), pl.ds(mid, mid)
+
+        def to_chip(src, dst, offset):
+            return copies.prepare(src, dst, dp=at.partner(offset) * 2 + at.core)
+
+        if self.relays:
+            mine, x, y, far = (block_of(at.partner(offset)) for offset in (0, 1, 2, 3))
+            self.first = [
+                to_chip(x.at[low, :], slots.at[0, low, :], 1),
+                to_chip(far.at[low, :], slots.at[0, high, :], 1),
+                to_chip(y.at[high, :], slots.at[1, low, :], 2),
+                to_chip(far.at[high, :], slots.at[1, high, :], 2),
+            ]
+            self.loads = [
+                copies.prepare_local(mine, total),
+                copies.prepare_local(y.at[low, :], slots.at[2, low, :]),
+                copies.prepare_local(x.at[high, :], slots.at[2, high, :]),
+            ]
+            self.second = [
+                to_chip(slots.at[2, low, :], slots.at[3, low, :], 2),
+                to_chip(slots.at[2, high, :], slots.at[3, high, :], 1),
+            ]
+        else:
+            self.first = [
+                to_chip(block_of(at.partner(offset)), slots.at[offset - 1], offset)
+                for offset in range(1, at.chips)
+            ]
+            self.loads = [copies.prepare_local(block_of(at.chip), total)]
+            self.second = []
+
+        self.bits = at.seq_ways.bit_length() - 1
+        self.regions, self.halving = [], []
+        start, size, slot = 0, rows, 0
+        for bit in range(self.bits):
+            size //= 2
+            side = lax.rem(lax.div(at.seq, 2**bit), 2)
+            peer = at.seq + (1 - 2 * side) * 2**bit
+            there = rows_at(start + (1 - side) * size, size)
+            start = start + side * size
+            here = rows_at(start, size)
+            self.halving.append(
+                copies.prepare(total.at[there, :], line.at[pl.ds(slot, size), :], seq=peer)
             )
-            for offset in range(1, at.chips)
+            self.regions.append((start, size, slot, here, peer))
+            slot += size
+        self.doubling = [
+            copies.prepare(final.at[here, :], final.at[here, :], seq=peer)
+            for _, _, _, here, peer in reversed(self.regions)
         ]
+        self.done = 0
+
+    def spread(self):
+        for copy in self.first + self.loads:
+            copy.start()
+
+    def add_rows(self, size, value_of, put):
+        step = next(n for n in (64, 32, 16) if size % n == 0)
+
+        def add(i, carry):
+            put(i * step, step, value_of(i * step, step).astype(bf16))
+            return carry
+
+        lax.fori_loop(0, size // step, add, 0)
+
+    def relay(self):
+        if not self.relays:
+            return
+        for copy in self.first:
+            copy.wait_recv()
+        for copy in self.loads[1:]:
+            copy.wait()
+        slots, mid = self.slots, self.mid
+        for side in (0, 1):
+
+            def value(at, n):
+                kept = slots[2, rows_at(side * mid + at, n), :].astype(f32)
+                return kept + slots[side, rows_at(mid + at, n), :].astype(f32)
+
+            def put(at, n, result):
+                slots[2, rows_at(side * mid + at, n), :] = result
+
+            self.add_rows(mid, value, put)
+        for copy in self.second:
+            copy.start()
 
     def add_chips(self):
-        for copy in self.arrivals:
+        for copy in self.second if self.relays else self.first:
             copy.wait_recv()
-        step = 64 if self.total.shape[0] % 64 == 0 else 16
-
-        def add(i, carry):
-            rows = rows_at(i * step, step)
-            value = self.total[rows, :].astype(f32)
-            for slot in range(self.at.chips - 1):
-                value = value + self.slots[slot, rows, :].astype(f32)
-            self.total[rows, :] = value.astype(bf16)
-            return carry
-
-        lax.fori_loop(0, self.total.shape[0] // step, add, 0)
-        self.arrivals = []
-        for step in range(1, self.at.seq_ways):
-            to = lax.rem(self.at.seq + step, self.at.seq_ways)
-            self.arrivals.append(
-                self.copies.remote(
-                    self.total.at[rows_at(to * self.part, self.part), :],
-                    self.line.at[step - 1],
-                    seq=to,
-                )
-            )
-
-    def add_line(self):
-        for copy in self.arrivals:
-            copy.wait_recv()
-        rows = rows_at(self.at.seq * self.part, self.part)
-        value = self.total[rows, :].astype(f32)
-        for slot in range(self.at.seq_ways - 1):
-            value = value + self.line[slot].astype(f32)
-        self.final[rows, :] = value.astype(bf16)
-        self.arrivals = []
-        for step in range(1, self.at.seq_ways):
-            to = lax.rem(self.at.seq + step, self.at.seq_ways)
-            self.arrivals.append(
-                self.copies.remote(self.final.at[rows, :], self.final.at[rows, :], seq=to)
-            )
-
-    def arrive(self):
-        for copy in self.arrivals:
-            copy.wait_recv()
+        self.loads[0].wait()
+        slots, mid, total = self.slots, self.mid, self.total
+
+        def put(at, n, result):
+            total[rows_at(at, n), :] = result
+
+        if self.relays:
+            for side in (0, 1):
+
+                def value(at, n):
+                    rows = rows_at(side * mid + at, n)
+                    result = total[rows, :].astype(f32) + slots[side, rows_at(at, n), :].astype(f32)
+                    return result + slots[3, rows, :].astype(f32)
+
+                self.add_rows(mid, value, lambda at, n, result: put(side * mid + at, n, result))
+        else:
+
+            def value(at, n):
+                result = total[rows_at(at, n), :].astype(f32)
+                for slot in range(self.at.chips - 1):
+                    result = result + slots[slot, rows_at(at, n), :].astype(f32)
+                return result
+
+            self.add_rows(2 * mid, value, put)
+        self.halving[0].start()
+
+    def step(self):
+        if self.done == 2 * self.bits:
+            return
+        at = self.done
+        self.done += 1
+        if at < self.bits:
+            self.halving[at].wait_recv()
+            start, size, slot, _, _ = self.regions[at]
+            last = at == self.bits - 1
+            target = self.final if last else self.total
+
+            def value(row, n):
+                kept = self.total[rows_at(start + row, n), :].astype(f32)
+                return kept + self.line[rows_at(slot + row, n), :].astype(f32)
+
+            def put(row, n, result):
+                target[rows_at(start + row, n), :] = result
+
+            self.add_rows(size, value, put)
+            (self.doubling[0] if last else self.halving[at + 1]).start()
+            return
+        at -= self.bits
+        self.doubling[at].wait_recv()
+        if at + 1 < self.bits:
+            self.doubling[at + 1].start()
+
+    def finish(self):
+        while self.done < 2 * self.bits:
+            self.step()
 
 
 def backward_kernel(
@@ -757,13 +919,19 @@
     totalp,
     linep,
     finalp,
-    gq_v,
-    slotsq,
-    totalq,
-    lineq,
-    finalq,
+    ga_v,
+    slotsa,
+    totala,
+    linea,
+    finala,
+    gb_v,
+    slotsb,
+    totalb,
+    lineb,
+    finalb,
     swap1,
-    swapq,
+    swapa,
+    swapb,
     swapx,
     send_sems,
     recv_sems,
@@ -789,24 +957,57 @@
     group = at.rank * 2 + at.core
 
     first_loads = [copies.local(rgl, rgl_v.at[pl.ds(0, own_rows), :]), copies.local(wp, wp_v)]
-    share2 = Share(at, copies, slots2, total2, line2, final2)
-    share1 = Share(at, copies, slots1, total1, line1, final1)
-    sharep = Share(at, copies, slotsp, totalp, linep, finalp)
-    shareq = Share(at, copies, slotsq, totalq, lineq, finalq)
     pair_rows = pair_own.shape[0]
     pair_copy = copies.remote(gp.at[rows_at((1 - at.core) * pair_rows, pair_rows), :], pair_far, dp=other)
     pair_load = copies.local(gp.at[rows_at(at.core * pair_rows, pair_rows), :], pair_own)
 
-    def block2(chip):
-        return g2.at[rows_at(chip * unit_rows, unit_rows), :]
-
-    def block1(chip):
-        return g1.at[rows_at(chip * 2 * shard, 2 * shard), :]
-
-    share2.spread(block2)
-    share1.spread(block1)
-    load2 = copies.local(block2(at.chip), total2)
-    load1 = copies.local(block1(at.chip), total1)
+    block_p = pair_rows // chips
+    share2 = Share(
+        at,
+        copies,
+        lambda chip: g2.at[rows_at(chip * unit_rows, unit_rows), :],
+        slots2,
+        total2,
+        line2,
+        final2,
+    )
+    share2.spread()
+    share1 = Share(
+        at,
+        copies,
+        lambda chip: g1.at[rows_at(chip * 2 * shard, 2 * shard), :],
+        slots1,
+        total1,
+        line1,
+        final1,
+    )
+    sharep = Share(
+        at,
+        copies,
+        lambda chip: pair_own.at[rows_at(chip * block_p, block_p), :],
+        slotsp,
+        totalp,
+        linep,
+        finalp,
+    )
+    sharea = Share(
+        at,
+        copies,
+        lambda chip: ga_v.at[rows_at(chip * 2 * shard, 2 * shard), :],
+        slotsa,
+        totala,
+        linea,
+        finala,
+    )
+    shareb = Share(
+        at,
+        copies,
+        lambda chip: gb_v.at[rows_at(chip * 2 * shard, 2 * shard), :],
+        slotsb,
+        totalb,
+        lineb,
+        finalb,
+    )
     hidden_loads = [copies.local(img, img_v), copies.local(small, small_v)]
     loads = [copies.local(prj, prj_v), copies.local(heads, heads_v), copies.local(wq, wq_v)]
 
@@ -845,34 +1046,30 @@
         return carry
 
     lax.fori_loop(0, pair_rows // step, add_pair, 0)
-    block_p = pair_rows // chips
-    sharep.spread(lambda chip: pair_own.at[rows_at(chip * block_p, block_p), :])
-
-    def own_p(i, carry):
-        totalp[rows_at(i * 16, 16), :] = pair_own[rows_at(at.chip * block_p + i * 16, 16), :]
-        return carry
-
-    lax.fori_loop(0, block_p // 16, own_p, 0)
+    sharep.spread()
 
     for copy in hidden_loads:
         copies.wait_local(copy)
     for row, start in ((0, 3), (1, 4)):
         for i in range(at.dp_ways):
-            vec_v[row : row + 1, i * shard : (i + 1) * shard] = small_v[
-                8 * i : 8 * i + 1, start * shard : (start + 1) * shard
-            ]
+            line = 16 * i + start
+            vec_v[row : row + 1, i * shard : (i + 1) * shard] = small_v[line : line + 1, :shard]
     gain = vec_v[0:1, :width]
     shift = vec_v[1:2, :width]
 
+    wide = next(n for n in (384, 128, length) if length % n == 0)
+
     def hide(s, carry):
-        rows = rows_at(s * tokens, tokens)
-        normed, _ = norm_stats(img_v[rows, :].astype(f32))
-        hid_v[rows, :] = (normed * gain + shift).astype(bf16)
+        normed, _ = norm_stats(img_v[rows_at(s * wide, wide), :].astype(f32))
+        hid_v[:, lanes_at(s * wide, wide)] = (normed * gain + shift).T.astype(bf16)
         return carry
 
-    lax.fori_loop(0, seq_ways, hide, 0)
+    lax.fori_loop(0, length // wide, hide, 0)
     for copy in loads:
         copies.wait_local(copy)
+    share2.relay()
+    share1.spread()
+    sharep.relay()
     for s in range(seq_ways):
         pltpu.make_async_copy(
             do_v.at[pl.ds(s * tokens, tokens), :], do_v.at[pl.ds(s * tokens, tokens), :], token_recv.at[s]
@@ -922,14 +1119,41 @@
         vec_v[4:5, lanes_at(width + group * head_cols + pair * LANES, LANES)] = jnp.sum(
             dv_sum[...], axis=0, keepdims=True
         )
+        for turn, calls in enumerate(hooks[:pairs]):
+
+            @pl.when(pair == turn)
+            def _():
+                for call in calls:
+                    call()
+
         return carry
 
-    lax.fori_loop(0, pairs // 2, one_pair, 0)
-    copies.wait_local(load2)
-    share2.add_chips()
-    lax.fori_loop(pairs // 2, pairs, one_pair, 0)
-    share2.add_line()
-    sharep.add_chips()
+    split = max(1, pairs // 2)
+    width_a, width_b = split * LANES, (pairs - split) * LANES
+
+    def weigh(ref, start, cols):
+        for q in range(chips):
+            block = pl.ds(q * 2 * shard, 2 * shard)
+            if ranks > 1:
+                ref[block, :] = jnp.zeros((2 * shard, ref.shape[1]), bf16)
+            for part in range(3):
+                value = dot(
+                    hid_v[block, :],
+                    dqkv_v[:, part * head_cols + start : part * head_cols + start + cols],
+                )
+                ref[block, lanes_at((at.rank * 3 + part) * cols, cols)] = value.astype(bf16)
+
+    hooks = [
+        [share2.add_chips],
+        [share2.step, sharep.add_chips],
+        [share1.relay, share2.step, sharep.step],
+        [share1.add_chips, sharea.relay, share2.step, sharep.step],
+    ]
+    hooks[split - 1] += [lambda: weigh(ga_v, 0, width_a), sharea.spread]
+    lax.fori_loop(0, pairs, one_pair, 0)
+    for calls in hooks[pairs:]:
+        for call in calls:
+            call()
 
     def widen(s, carry):
         rows = rows_at(s * tokens, tokens)
@@ -954,16 +1178,15 @@
     lax.fori_loop(0, seq_ways, widen, 0)
     near_rows = pl.ds(0, seq_ways * half)
     near_copy = copies.remote(da_v.at[near_rows, :], near_v, dp=other)
-
-    span = 3 * head_cols
-    gq_cols = ranks * span
+    share1.step()
+    sharea.add_chips()
+    share2.finish()
+    sharep.step()
+
+    weigh(gb_v, width_a, width_b)
+    extra_at = ranks * 3 * width_b
     per_chip = width // chips
     for q in range(chips):
-        block = pl.ds(q * 2 * shard, 2 * shard)
-        lanes = slice(q * 2 * shard, (q + 1) * 2 * shard)
-        if ranks > 1:
-            gq_v[block, :] = jnp.zeros((2 * shard, gq_v.shape[1]), bf16)
-        gq_v[block, lanes_at(at.rank * span, span)] = dot(hid_v[:, lanes], dqkv_v[...], 0, 0).astype(bf16)
         rows = [vec_v[2:3, q * per_chip + i : q * per_chip + i + LANES] for i in range(0, per_chip, LANES)]
         rows += [vec_v[3:4, q * per_chip + i : q * per_chip + i + LANES] for i in range(0, per_chip, LANES)]
         rows += [
@@ -974,17 +1197,11 @@
         extra = jnp.zeros((16, LANES), f32)
         for i, row in enumerate(rows):
             extra = jnp.where(which == i, row, extra)
-        gq_v[pl.ds(q * 2 * shard + 16, 2 * shard - 16), gq_cols : gq_cols + LANES] = jnp.zeros(
+        gb_v[pl.ds(q * 2 * shard + 16, 2 * shard - 16), extra_at : extra_at + LANES] = jnp.zeros(
             (2 * shard - 16, LANES), bf16
         )
-        gq_v[pl.ds(q * 2 * shard, 16), gq_cols : gq_cols + LANES] = extra.astype(bf16)
-    shareq.spread(lambda chip: gq_v.at[rows_at(chip * 2 * shard, 2 * shard), :])
-
-    def own_q(i, carry):
-        totalq[rows_at(i * 16, 16), :] = gq_v[rows_at(at.chip * 2 * shard + i * 16, 16), :]
-        return carry
-
-    lax.fori_loop(0, 2 * shard // 16, own_q, 0)
+        gb_v[pl.ds(q * 2 * shard, 16), extra_at : extra_at + LANES] = extra.astype(bf16)
+    shareb.spread()
 
     near_copy.wait_recv()
     home_core = lax.div(at.item, items)
@@ -1010,52 +1227,55 @@
         pl.when(jnp.logical_not(mine))(far.start)
         home_jobs.append((mine, far))
 
-    sharep.add_line()
-    copies.wait_local(load1)
-    share1.add_chips()
-    shareq.add_chips()
-    share1.add_line()
-    shareq.add_line()
-    share2.arrive()
-    copies.local(final2, o2_out)
-    sharep.arrive()
-    copies.local(finalp, op_out)
-    share1.arrive()
     theirs = rows_at((1 - at.core) * shard, shard)
     ours = rows_at(at.core * shard, shard)
-    swap1_copy = copies.remote(final1.at[theirs, :], swap1, dp=other)
     units = final1.shape[1] // chips
-    for q in range(chips):
-        cols = slice(q * units, (q + 1) * units)
-        o1_out[:, lanes_at((2 * q + at.core) * units, units)] = final1[ours, cols]
-    swap1_copy.wait_recv()
-    for q in range(chips):
-        cols = slice(q * units, (q + 1) * units)
-        o1_out[:, lanes_at((2 * q + 1 - at.core) * units, units)] = swap1[:, cols]
-    shareq.arrive()
-    swapq_copy = copies.remote(final1_rows(finalq, theirs), swapq, dp=other)
-    swapx_copy = copies.remote(finalq.at[pl.ds(0, 16), pl.ds(gq_cols, LANES)], swapx, dp=other)
-
-    def place_q(ref, rows, core):
+
+    def place_one(ref, rows, core):
+        for q in range(chips):
+            cols = pl.ds(q * units, units)
+            o1_out[:, lanes_at((2 * q + core) * units, units)] = ref[rows, cols]
+
+    def place_q(ref, rows, core, start, cols):
         for j in range(ranks):
             for part in range(3):
-                oq_out[:, lanes_at(part * width + (j * 2 + core) * head_cols, head_cols)] = ref[
-                    rows, pl.ds(j * span + part * head_cols, head_cols)
-                ]
-
-    place_q(finalq, ours, at.core)
-    swapq_copy.wait_recv()
-    place_q(swapq, pl.ds(0, shard), 1 - at.core)
+                lane = part * width + (j * 2 + core) * head_cols + start
+                oq_out[:, lanes_at(lane, cols)] = ref[rows, pl.ds((j * 3 + part) * cols, cols)]
+
+    copies.local(final2, o2_out)
+    share1.step()
+    sharea.step()
+    sharep.finish()
+    copies.local(finalp, op_out)
+    share1.step()
+    sharea.step()
+    shareb.relay()
+    share1.finish()
+    swap1_copy = copies.remote(final1.at[theirs, :], swap1, dp=other)
+    sharea.step()
+    shareb.add_chips()
+    place_one(final1, ours, at.core)
+    sharea.finish()
+    swapa_copy = copies.remote(finala.at[theirs, :], swapa, dp=other)
+    place_q(finala, ours, at.core, 0, width_a)
+    shareb.step()
+    swap1_copy.wait_recv()
+    place_one(swap1, pl.ds(0, shard), 1 - at.core)
+    shareb.step()
+    swapa_copy.wait_recv()
+    place_q(swapa, pl.ds(0, shard), 1 - at.core, 0, width_a)
+    shareb.finish()
+    swapb_copy = copies.remote(finalb.at[theirs, :], swapb, dp=other)
+    swapx_copy = copies.remote(finalb.at[pl.ds(0, 16), pl.ds(extra_at, LANES)], swapx, dp=other)
+    place_q(finalb, ours, at.core, width_a, width_b)
+    swapb_copy.wait_recv()
+    place_q(swapb, pl.ds(0, shard), 1 - at.core, width_a, width_b)
     swapx_copy.wait_recv()
-    ox_out[...] = finalq[0:16, gq_cols : gq_cols + LANES].astype(f32) + swapx[...].astype(f32)
+    ox_out[...] = finalb[0:16, extra_at : extra_at + LANES].astype(f32) + swapx[...].astype(f32)
     pltpu.make_async_copy(home_out, home_out, home_recv).wait()
     for mine, far in home_jobs:
         pl.when(jnp.logical_not(mine))(far.wait_send)
     copies.finish()
-
-
-def final1_rows(ref, rows):
-    return ref.at[rows, :]
 
 
 def backward(items, rgl, wp, g2, g1, gp, prj, heads, img, wq, small, lse):
@@ -1071,7 +1291,8 @@
     units_half = g1.shape[1]
     gp_rows, gp_cols = gp.shape
     block_p = gp_rows // dp_ways
-    gq_cols = ranks * 3 * head_cols + LANES
+    split = max(1, head_cols // LANES // 2) * LANES
+    cols_a, cols_b = ranks * 3 * split, ranks * 3 * (head_cols - split) + LANES
     stage_rows = max(own_rows, seq_ways * half)
     any_spec = pl.BlockSpec(memory_space=pl.ANY)
     vmem_spec = pl.BlockSpec(memory_space=pltpu.VMEM)
@@ -1079,9 +1300,9 @@
 
     def share(rows, cols):
         return [
-            low(chips - 1, rows, cols),
+            low(4 if chips == 4 else chips - 1, rows, cols),
             low(rows, cols),
-            low(seq_ways - 1, rows // seq_ways, cols),
+            low(rows - rows // seq_ways, cols),
             low(rows, cols),
         ]
 
@@ -1108,7 +1329,7 @@
             pltpu.VMEM(small.shape, f32),
             low(stage_rows, width),
             low(length, head_cols),
-            low(length, width),
+            low(width, length),
             low(length, 3 * head_cols),
             pltpu.VMEM((seq_ways * half, width), f32),
             low(seq_ways * half, width),
@@ -1121,10 +1342,13 @@
             low(gp_rows // 2, gp_cols),
             low(gp_rows // 2, gp_cols),
             *share(block_p, gp_cols),
-            low(width, gq_cols),
-            *share(2 * shard, gq_cols),
+            low(width, cols_a),
+            *share(2 * shard, cols_a),
+            low(width, cols_b),
+            *share(2 * shard, cols_b),
             low(shard, units_half),
-            low(shard, gq_cols),
+            low(shard, cols_a),
+            low(shard, cols_b),
             low(16, LANES),
             pltpu.SemaphoreType.DMA((remotes,)),
             pltpu.SemaphoreType.DMA((remotes,)),
@@ -1209,7 +1433,8 @@
         return total.astype(bf16)
 
     small_names = (qv_bias, proj_bias, ln1_gain, ln1_bias, ln2_gain, ln2_bias, fc1_bias, fc2_bias)
-    small = jnp.concatenate(small_names).astype(f32)
+    small = jnp.concatenate([array.reshape(-1, shard_rows) for array in small_names]).astype(f32)
+    small = jnp.pad(small, ((0, 16 - small.shape[0]), (0, LANES - shard_rows)))
     cotangent_own = cotangent.reshape(own_rows, width)
     (
         image_low,
@@ -1223,6 +1448,10 @@
         attended,
         log_total,
         attended_rows,
+        residual_first,
+        hidden_second,
+        pre_act,
+        acts,
     ) = forward(
         items,
         images.reshape(own_rows, width),
@@ -1231,23 +1460,18 @@
         fc1_weight,
         fc2_weight,
         cotangent_own,
-        jnp.broadcast_to(small, (8, small.shape[0])),
+        small,
     )
     small_all = small
-    small = small.reshape(dp_ways, 8, -1)[:, 0]
+    small = small.reshape(dp_ways, 16, LANES)
     smalls, at = [], 0
     for array in small_names:
-        smalls.append(small[:, at : at + array.shape[0]].reshape(-1))
-        at += array.shape[0]
-    _, bias_proj, gain_first, shift_first, gain_second, shift_second, bias_one, bias_two = smalls
-    bias_one_half = pick(bias_one.reshape(chips, 2, -1), core, 1).reshape(-1)
+        count = array.shape[0] // shard_rows
+        smalls.append(small[:, at : at + count, :shard_rows].reshape(-1))
+        at += count
+    _, _, gain_first, _, gain_second, _, _, bias_two = smalls
     flat_rows = images.reshape(own_rows, width).astype(f32)
-    residual_first = flat_rows + dot(attended_rows, proj_full) + bias_proj
     normed_second, inv_second = norm_stats(residual_first)
-    hidden_own = (normed_second * gain_second + shift_second).astype(bf16)
-    hidden_second = by_core(hidden_own, swap(hidden_own), 0).reshape(2 * own_rows, width)
-    pre_act = dot(hidden_second, fc1_half) + bias_one_half
-    acts = (pre_act * gelu_cdf(pre_act)).astype(bf16)
 
     def meet(partial):
         parts = partial.reshape(2, own_rows, width)

time: 470 us -> 424 us (0.902)
  the two profiles are of different devices: /device:TPU:11 before, /device:TPU:0 now
where the time goes in v4:
time: 424 us; the launch traced here: 416 us
  Pallas kernels  329 us (78%)
  matrix products  43.6 us (10%)
  other arithmetic  21.3 us (5%)
  local copies, waits for them, and re-layouts  20.1 us (5%)
    pallas_call x1, Pallas kernels, backward(): pl.pallas_call(functools.partial(backward_kernel, items), in_specs=[any_s...  214 us
    pallas_call x1, Pallas kernels, forward(): pl.pallas_call(functools.partial(forward_kernel, items), in_specs=[any_sp...  115 us
    dot_general x6, matrix products, dot(): lax.dot_general(left, right, (((left_dim,), (right_dim,)), ((), ())), pre...  43.6 us
  transfers between devices with their start and end apart: 2, of which 0 were waited for; matrix products, arithmetic and copies ran while one was open for 9% of the time, Pallas kernels for 0%

profile of v4, /device:TPU:0, one launch (start us, length us, event | category | flops | bytes accessed | tf_op | source)
XLA Modules:
  0.0 415.6 jit_solution(8041369544888067226)
XLA Ops:
  0.7 2.2 concatenate.15
  2.9 0.6 pad_convert_fusion.small
  3.5 114.6 %forward.1 = (bf16[1152,1024]{1,0:T(8,128)(2,1)}, bf16[1024,1536]{1,0:T(8,128)(2,1)}, bf16[1024,1024]{1,0:T(8,128)(2,1)}, bf16[1024,2048]{1,0:T(8,128)(2,1)}, bf...) custom-call(bf16[576,1024]{1,0:T(8,128)(2,1)} %bitcast.78, ...), custom_call_target="tpu_custom_call" | custom-call | tf_op jit(solution)/shard_map/forward/pallas_call | solution.py:683
  118.1 0.0 copy-start.19
  118.1 12.0 %fusion.19 = (bf16[2048]{0:T(1024)(128)(2,1)S(1)}, bf16[1152,2048]{1,0:T(8,128)(2,1)S(1)}) fusion(f32[1152,2048]{1,0:T(8,128)} %get-tuple-element.40, bf16[1152,1024]{1,0:T(8,128)(2,1)} %get-tuple-element.39, bf16[2048,1024]{1,0:T(8,128)(2,1)} %get-tuple-element.37), kind=kOutput, calls=%fused_computation.68 | convolution fusion | flops 4857788416 | bytes 20713472 | tf_op jit(solution)/shard_map/dot_general | solution.py:43
  130.1 0.0 copy-start.21
  130.1 0.0 copy-done.19
  130.1 0.0 copy-start.17
  130.1 0.0 copy-start.18
  130.1 5.1 %fusion.10 = f32[1152,1024]{1,0:T(8,128)S(1)} fusion(bf16[1024,2048]{1,0:T(8,128)(2,1)S(1)} %copy-done.19, bf16[1152,2048]{1,0:T(8,128)(2,1)S(1)} %get-tuple-element.76), kind=kOutput, calls=%fused_computation.27 | convolution fusion | flops 4831838208 | bytes 13631488 | tf_op jit(solution)/shard_map/dot_general | solution.py:43
  135.3 0.0 copy-done.21
  135.3 0.0 copy-start.9
  135.3 1.4 fusion.13
  136.6 0.0 collective-permute-start.1
  136.6 1.1 copy-done.9
  137.7 0.0 copy-done.18
  137.7 5.1 %fusion.20 = f32[1152,1024]{1,0:T(8,128)S(1)} fusion(bf16[1152,2048]{1,0:T(8,128)(2,1)S(1)} %copy-done.17, bf16[2048,1024]{1,0:T(8,128)(2,1)S(1)} %copy-done.18), kind=kOutput, calls=%fused_computation.69 | convolution fusion | flops 4831838208 | bytes 13631488 | tf_op jit(solution)/shard_map/dot_general | solution.py:43
  142.8 0.0 copy-start.1
  142.9 2.1 copy-done.8
  145.0 1.2 fusion.12
  146.2 0.0 collective-permute-start
  146.2 0.2 convert_reduce_fusion
  146.4 0.5 fusion.5
  146.9 0.7 div.33
  147.5 9.9 %convolution_convert_fusion.1.g2 = bf16[2048,1024]{1,0:T(8,128)(2,1)} fusion(bf16[1152,2048]{1,0:T(8,128)(2,1)} %get-tuple-element.36, bf16[1152,1024]{1,0:T(8,128)(2,1)} %get-tuple-element.39), kind=kOutput, calls=%fused_computation.7 | convolution fusion | flops 4833935360 | bytes 11272192 | tf_op jit(solution)/shard_map/dot_general | solution.py:43
  157.5 0.6 broadcast_in_dim.35
  158.1 0.8 reduce.3
  158.9 0.7 rsqrt.21
  159.6 0.6 broadcast_in_dim.38
  160.2 0.7 broadcast_in_dim.39
  160.9 0.0 copy-done
  160.9 0.2 reduce_sum.117
  161.1 0.4 multiply_reduce_fusion.3
  161.5 9.7 %convolution_convert_fusion.g1 = bf16[1024,2048]{1,0:T(8,128)(2,1)} fusion(bf16[1152,1024]{1,0:T(8,128)(2,1)} %get-tuple-element.43, bf16[1152,2048]{1,0:T(8,128)(2,1)} %copy-done.21), kind=kOutput, calls=%fused_computation.6 | convolution fusion | flops 4833935360 | bytes 11272192 | tf_op jit(solution)/shard_map/dot_general | solution.py:43
  171.2 1.4 fusion.17
  172.6 0.0 collective-permute-done.1
  172.6 3.1 multiply_reduce_fusion.1
  175.8 0.0 collective-permute-done
  175.8 0.0 copy-start.15
  175.8 0.0 copy-start.16
  175.8 3.8 fusion.16
  179.6 0.1 constant_dynamic-update-slice_fusion
  179.8 0.2 convert_element_type.84.rgl
  179.9 0.0 copy-start.6
  180.0 1.7 copy-done.20
  181.7 1.8 convolution_convert_fusion.2
  183.6 0.3 pad_maximum_fusion
  183.8 1.6 copy.31
  185.4 214.5 %backward.1 = (bf16[576,1024]{1,0:T(8,128)(2,1)}, bf16[512,1024]{1,0:T(8,128)(2,1)}, bf16[128,1152]{1,0:T(8,128)(2,1)}, bf16[128,4096]{1,0:T(8,128)(2,1)}, bf16[128,3072]{1,0:T(8,128)(2,1)}, /*index=5*/f32[16,128]{1,0:T(8,128)}) custom-call(bf16[576,1024]{1,0:T(8,128)(2,1)} %copy-done.6, bf16[1024,1024]{1,0:T(8,128)(2,1)} %get-tuple-element.42.wp, ...), custom_call_target="tpu_custom_call" | custom-call | tf_op jit(solution)/shard_map/backward/pallas_call | solution.py:1310
  399.9 0.8 slice.60
  400.6 0.7 fusion.18
  401.4 0.7 slice_convert_fusion.1
  402.1 0.6 slice_bitcast_fusion
  402.6 0.5 slice_bitcast_fusion.1
  403.2 1.8 slice_convert_fusion
  405.0 0.6 constant_dynamic-slice_fusion.2
  405.5 2.5 convert_element_type.92
  408.1 1.5 convert_element_type.95
  409.6 0.0 copy-start.4
  409.6 1.6 convert_element_type.96
  411.2 0.5 fusion.14
  411.7 0.3 copy-done.7
  412.0 0.9 fusion.8
  412.9 2.3 multiply_add_fusion
  (43 shorter events, 0.2 us)
Async XLA Ops:
  118.1 12.0 %copy-start.19 = (bf16[1024,2048]{1,0:T(8,128)(2,1)S(1)}, bf16[1024,2048]{1,0:T(8,128)(2,1)}, u32[]{:S(2)}) copy-start(bf16[1024,2048]{1,0:T(8,128)(2,1)} %get-tuple-element.41) | copy-start | bytes 12582916
  130.1 5.2 %copy-start.21 = (bf16[1152,2048]{1,0:T(8,128)(2,1)}, bf16[1152,2048]{1,0:T(8,128)(2,1)S(1)}, u32[]{:S(2)}) copy-start(bf16[1152,2048]{1,0:T(8,128)(2,1)S(1)} %get-tuple-element.76) | copy-start | bytes 14155780
  130.1 7.6 %copy-start.17 = (bf16[1152,2048]{1,0:T(8,128)(2,1)S(1)}, bf16[1152,2048]{1,0:T(8,128)(2,1)}, u32[]{:S(2)}) copy-start(bf16[1152,2048]{1,0:T(8,128)(2,1)} %get-tuple-element.36) | copy-start | bytes 14155780
  130.1 7.6 %copy-start.18 = (bf16[2048,1024]{1,0:T(8,128)(2,1)S(1)}, bf16[2048,1024]{1,0:T(8,128)(2,1)}, u32[]{:S(2)}) copy-start(bf16[2048,1024]{1,0:T(8,128)(2,1)} %get-tuple-element.37) | copy-start | bytes 12582916
  135.3 2.5 copy-start.9
  136.6 36.0 %collective-permute-start.1 = (bf16[576,1024]{1,0:T(8,128)(2,1)}, bf16[576,1024]{1,0:T(8,128)(2,1)}, u32[]{:S(2)}, u32[]{:S(2)}) collective-permute-start(bf16[576,1024]{1,0:T(8,128)(2,1)} %fusion.13), channel_id=1, source_target_pairs={{0,4},{4,0},{8,12},{12,8},{16,20},{20,16},{24,28},{28,24},{1,5},{5... | collective-permute-start | bytes 3538952 | tf_op jit(solution)/shard_map/ppermute | solution.py:1403
  142.8 2.1 copy-start.8
  142.8 3.3 copy-start.1
  146.2 29.6 %collective-permute-start = (bf16[576,1024]{1,0:T(8,128)(2,1)}, bf16[576,1024]{1,0:T(8,128)(2,1)}, u32[]{:S(2)}, u32[]{:S(2)}) collective-permute-start(bf16[576,1024]{1,0:T(8,128)(2,1)} %fusion.12), channel_id=1, source_target_pairs={{0,4},{4,0},{8,12},{12,8},{16,20},{20,16},{24,28},{28,24},{1,5},{5... | collective-permute-start | bytes 3538952 | tf_op jit(solution)/shard_map/ppermute | solution.py:1403
  147.5 10.5 %copy-start.5 = (bf16[2,288,1024]{2,1,0:T(8,128)(2,1)S(1)}, bf16[2,288,1024]{2,1,0:T(8,128)(2,1)}, u32[]{:S(2)}) copy-start(bf16[2,288,1024]{2,1,0:T(8,128)(2,1)} %param.27) | copy-start | bytes 3538948
  147.5 13.3 %copy-start = (f32[576,1024]{1,0:T(8,128)S(1)}, f32[576,1024]{1,0:T(8,128)}, u32[]{:S(2)}) copy-start(f32[576,1024]{1,0:T(8,128)} %get-tuple-element.35) | copy-start | bytes 7077892
  175.8 3.8 copy-start.15
  175.8 3.8 copy-start.16
  179.6 4.0 copy-start.3
  179.6 2.1 copy-start.20
  179.9 3.6 copy-start.6
  399.9 8.2 %copy-start.11 = (bf16[128,4096]{1,0:T(8,128)(2,1)S(1)}, bf16[128,4096]{1,0:T(8,128)(2,1)}, u32[]{:S(2)}) copy-start(bf16[128,4096]{1,0:T(8,128)(2,1)} %get-tuple-element.54) | copy-start | bytes 3145732
  405.5 4.1 copy-start.10
  409.6 2.1 copy-start.2
  409.6 2.4 copy-start.7
  409.6 2.4 copy-start.12
  409.6 2.4 copy-start.13
  409.6 2.4 copy-start.14
  409.6 3.2 copy-start.4
